TPU v7x, 256 devices: a whole 4x4x8 slice. The times are simulated.
256 devices in a mesh: dp: 16 (over z_hi, x), blk: 16 (over y, z_lo, core).
Axes of the slice: x: 4, y: 4, z: 8 (z_hi: 4, z_lo: 2; z = z_hi * 2 + z_lo), core: 2. Of those that a mesh axis runs over, the one named last changes fastest.
Arguments:
- queries: bfloat16 [16, 2048, 2048], P('dp', 'blk'), may hold values from -6 to 6
- keys: bfloat16 [16, 2048, 512], P('dp', 'blk'), may hold values from -6 to 6
- values: bfloat16 [16, 2048, 512], P('dp', 'blk'), may hold values from -6 to 6
- out_grad: bfloat16 [16, 2048, 2048], P('dp', 'blk'), may hold values from -6 to 6
- layer_input: bfloat16 [16, 2048, 4096], P('dp', 'blk'), may hold values from -6 to 6
- lengths: int32 [16, 3], P('dp'), may hold values from 128 to 1792, as said below
Outputs:
- query_grad: bfloat16 [16, 2048, 2048], P('dp', 'blk')
- key_grad: bfloat16 [16, 2048, 512], P('dp', 'blk')
- value_grad: bfloat16 [16, 2048, 512], P('dp', 'blk')
- weight_grad: float32 [4096, 1024], P(('dp', 'blk'))
Inputs may be any that keep to these rules, and one draw needn't show every extreme that they name: `lengths`: each row sums to 2048; the chosen and rejected counts lie between 128 and 384.
All inputs are finite; a program needn't handle non-finite values.
Results may differ from a plain program's by a relative error of at most 0.023.
Values may be sent and summed in bfloat16 or wider, within the bound.
A program may use at most 128 MiB of HBM per device.

v0:
```python
import math

import jax
import jax.numpy as jnp
from jax import lax
from jax.sharding import PartitionSpec as P

HEAD = 128


rope_base = 500000.0
masked_fill = -1e30


def side_by_side(arrays, axis, dim, along):
    widths = [a.shape[along] for a in arrays]
    both = jnp.concatenate(arrays, axis=along)
    whole = lax.all_gather(both, axis, axis=dim, tiled=True)
    return tuple(jnp.split(whole, [sum(widths[:k]) for k in range(1, len(widths))], axis=along))


def in_one_piece(arrays, axis, dim, along):
    widths = [a.shape[along] for a in arrays]
    both = jnp.concatenate(arrays, axis=along)
    whole = lax.psum_scatter(both, axis, scatter_dimension=dim, tiled=True)
    return tuple(jnp.split(whole, [sum(widths[:k]) for k in range(1, len(widths))], axis=along))


def cut_along(array, dim, count):
    before, after = (array.shape[:dim], array.shape[dim + 1 :])
    return jnp.moveaxis(array.reshape(*before, count, -1, *after), dim, 0)


def sum_at_owner(array, axis, dim):
    pieces = cut_along(array, dim, lax.axis_size(axis))
    arrived = lax.all_to_all(pieces, axis, split_axis=0, concat_axis=0, tiled=True)
    return arrived.astype(jnp.float32).sum(axis=0)


def stored_positions(stored_rows, shard_rows, shard_count):
    half_rows = shard_rows // 2
    block_number = stored_rows // half_rows
    holder = block_number // 2
    upper_half = block_number % 2
    position_block = jnp.where(upper_half == 1, 2 * shard_count - 1 - holder, holder)
    return (position_block * half_rows + stored_rows % half_rows).astype(jnp.int32)


def allowed_pairs(query_pos, key_pos, prompt_len, chosen_len):
    causal = key_pos[None, :] <= query_pos[:, None]
    reject_start = prompt_len + chosen_len
    query_rejected = query_pos >= reject_start
    key_chosen = jnp.logical_and(key_pos >= prompt_len, key_pos < reject_start)
    return jnp.logical_and(
        causal, jnp.logical_not(jnp.logical_and(query_rejected[:, None], key_chosen[None, :]))
    )


def block_length(total_rows):
    chosen_size = 1
    for candidate in range(1, min(total_rows, 512) + 1):
        if total_rows % candidate == 0:
            chosen_size = candidate
    return chosen_size


def over_blocks(running, pieces, first_row, block_fn):
    total_rows = pieces[0].shape[0]
    block_rows = block_length(total_rows)

    def one_turn(turn_index, current):
        block_start = turn_index * block_rows
        block_parts = tuple(
            (lax.dynamic_slice_in_dim(member, block_start, block_rows, 0) for member in pieces)
        )
        return block_fn(current, block_parts, first_row + block_start)

    return lax.fori_loop(0, total_rows // block_rows, one_turn, running)


def keep_state(running):
    return running


def body(queries, keys, values, out_grad, layer_input, lengths):
    shard_count = lax.axis_size("blk")
    shard_index = lax.axis_index("blk")
    shard_rows = queries.shape[1]
    kv_heads = keys.shape[2] // HEAD
    group_heads = queries.shape[2] // keys.shape[2]
    seq_len = shard_rows * shard_count
    query_count = group_heads * shard_rows
    scale = 1.0 / math.sqrt(HEAD)
    prompt_len = lengths[0, 0]
    chosen_len = lengths[0, 1]
    own_rows = shard_index * shard_rows + jnp.arange(shard_rows, dtype=jnp.int32)
    own_pos = stored_positions(own_rows, shard_rows, shard_count)
    query_pos = jnp.tile(own_pos, group_heads)
    query_rows = (
        queries[0]
        .reshape(shard_rows, kv_heads, group_heads, HEAD)
        .transpose(1, 2, 0, 3)
        .reshape(kv_heads, query_count, HEAD)
    )
    grad_rows = (
        out_grad[0]
        .reshape(shard_rows, kv_heads, group_heads, HEAD)
        .transpose(1, 2, 0, 3)
        .reshape(kv_heads, query_count, HEAD)
    )

    def block_allowed(first_row, count_rows):
        key_pos = stored_positions(
            first_row + jnp.arange(count_rows, dtype=jnp.int32), shard_rows, shard_count
        )
        return allowed_pairs(query_pos, key_pos, prompt_len, chosen_len)

    def forward_block(running, block_parts, first_row):
        key_block, value_block = block_parts
        count_rows = key_block.shape[0]
        allowed = block_allowed(first_row, count_rows)

        def forward_compute(current):
            run_max, run_sum, run_acc = current
            key_heads = key_block.reshape(count_rows, kv_heads, HEAD)
            value_heads = value_block.reshape(count_rows, kv_heads, HEAD).astype(jnp.float32)
            scores = scale * jnp.einsum(
                "gqe,kge->gqk", query_rows, key_heads, preferred_element_type=jnp.float32
            )
            new_max = jnp.maximum(
                run_max, jnp.max(jnp.where(allowed[None], scores, masked_fill), axis=-1)
            )
            weights = jnp.where(allowed[None], jnp.exp(scores - new_max[..., None]), 0.0)
            factor = jnp.exp(run_max - new_max)
            new_sum = run_sum * factor + jnp.sum(weights, axis=-1)
            new_acc = run_acc * factor[..., None] + jnp.einsum(
                "gqk,kge->gqe", weights, value_heads, precision=lax.Precision.HIGHEST
            )
            return (new_max, new_sum, new_acc)

        return lax.cond(jnp.any(allowed), forward_compute, keep_state, running)

    start_forward = (
        jnp.full((kv_heads, query_count), masked_fill, jnp.float32),
        jnp.zeros((kv_heads, query_count), jnp.float32),
        jnp.zeros((kv_heads, query_count, HEAD), jnp.float32),
    )
    run_max, run_sum, run_acc = over_blocks(
        start_forward, side_by_side((keys[0], values[0]), "blk", 0, 1), jnp.int32(0), forward_block
    )
    attn_out = run_acc / run_sum[..., None]
    log_total = run_max + jnp.log(run_sum)
    delta = jnp.sum(grad_rows.astype(jnp.float32) * attn_out, axis=-1)

    def backward_block(running, block_parts, first_row):
        key_block, value_block = block_parts
        count_rows = key_block.shape[0]
        allowed = block_allowed(first_row, count_rows)

        def backward_compute(current):
            query_acc, key_acc, value_acc = current
            key_heads = key_block.reshape(count_rows, kv_heads, HEAD)
            value_heads = value_block.reshape(count_rows, kv_heads, HEAD)
            scores = scale * jnp.einsum(
                "gqe,kge->gqk", query_rows, key_heads, preferred_element_type=jnp.float32
            )
            probs = jnp.where(allowed[None], jnp.exp(scores - log_total[..., None]), 0.0)
            prob_half = probs.astype(jnp.bfloat16)
            prob_grad = jnp.einsum(
                "gqe,kge->gqk", grad_rows, value_heads, preferred_element_type=jnp.float32
            )
            score_grad = (scale * probs * (prob_grad - delta[..., None])).astype(jnp.bfloat16)
            query_acc = query_acc + jnp.einsum(
                "gqk,kge->gqe", score_grad, key_heads, preferred_element_type=jnp.float32
            )
            key_term = jnp.einsum(
                "gqk,gqe->kge", score_grad, query_rows, preferred_element_type=jnp.float32
            ).reshape(count_rows, kv_heads * HEAD)
            value_term = jnp.einsum(
                "gqk,gqe->kge", prob_half, grad_rows, preferred_element_type=jnp.float32
            ).reshape(count_rows, kv_heads * HEAD)
            key_acc = lax.dynamic_update_slice_in_dim(
                key_acc,
                lax.dynamic_slice_in_dim(key_acc, first_row, count_rows, 0) + key_term,
                first_row,
                0,
            )
            value_acc = lax.dynamic_update_slice_in_dim(
                value_acc,
                lax.dynamic_slice_in_dim(value_acc, first_row, count_rows, 0) + value_term,
                first_row,
                0,
            )
            return (query_acc, key_acc, value_acc)

        return lax.cond(jnp.any(allowed), backward_compute, keep_state, running)

    start_backward = (
        jnp.zeros((kv_heads, query_count, HEAD), jnp.float32),
        jnp.zeros((seq_len, kv_heads * HEAD), jnp.float32),
        jnp.zeros((seq_len, kv_heads * HEAD), jnp.float32),
    )
    query_acc, key_acc, value_acc = over_blocks(
        start_backward,
        side_by_side((keys[0], values[0]), "blk", 0, 1),
        jnp.int32(0),
        backward_block,
    )
    key_sum, value_sum = tuple(
        (
            part.astype(jnp.float32)
            for part in in_one_piece(
                (key_acc.astype(jnp.bfloat16), value_acc.astype(jnp.bfloat16)), "blk", 0, 1
            )
        )
    )
    query_grad = (
        query_acc.reshape(kv_heads, group_heads, shard_rows, HEAD)
        .transpose(2, 0, 1, 3)
        .reshape(shard_rows, kv_heads * group_heads * HEAD)
        .astype(jnp.bfloat16)
    )
    key_out = key_sum.astype(jnp.bfloat16)
    value_out = value_sum.astype(jnp.bfloat16)
    half_dim = HEAD // 2
    frequency = jnp.exp(
        -(2.0 * jnp.arange(half_dim, dtype=jnp.float32) / HEAD) * math.log(rope_base)
    )
    angles = own_pos.astype(jnp.float32)[:, None] * frequency[None, :]
    cosine = jnp.concatenate([jnp.cos(angles), jnp.cos(angles)], axis=-1)[:, None, :]
    sine = jnp.concatenate([jnp.sin(angles), jnp.sin(angles)], axis=-1)[:, None, :]
    grad_heads = key_sum.reshape(shard_rows, kv_heads, HEAD)
    rotated = jnp.concatenate([-grad_heads[..., half_dim:], grad_heads[..., :half_dim]], axis=-1)
    key_pre = (
        (grad_heads * cosine - rotated * sine)
        .reshape(shard_rows, kv_heads * HEAD)
        .astype(jnp.bfloat16)
    )
    grad_cols = jnp.concatenate([key_pre, value_out], axis=1)
    input_rows = layer_input[0]
    features = layer_input.shape[2]
    replica_count = lax.axis_size("dp")
    feature_share = features // (replica_count * shard_count)
    grouped_input = input_rows.reshape(shard_rows, replica_count, shard_count * feature_share)
    sequence_input = lax.all_to_all(grouped_input, "blk", split_axis=2, concat_axis=0, tiled=True)
    sequence_weight = jnp.einsum(
        "tif,tc->ifc",
        sequence_input,
        lax.all_gather(grad_cols, "blk", axis=0, tiled=True),
        preferred_element_type=jnp.float32,
    )
    weight_grad = sum_at_owner(sequence_weight.astype(jnp.bfloat16), "dp", 0).reshape(
        feature_share, grad_cols.shape[1]
    )
    return (query_grad[None], key_out[None], value_out[None], weight_grad)


def solution(mesh):
    placed = (
        P("dp", "blk", None),
        P("dp", "blk", None),
        P("dp", "blk", None),
        P("dp", "blk", None),
        P("dp", "blk", None),
        P("dp", None),
    )
    return jax.shard_map(
        body,
        mesh=mesh,
        in_specs=placed,
        out_specs=(
            P("dp", "blk", None),
            P("dp", "blk", None),
            P("dp", "blk", None),
            P(("dp", "blk"), None),
        ),
        check_vma=False,
    )
```

profile of v0, /device:TPU:1, one launch (start us, length us, event | category | flops | bytes accessed | tf_op | source)
XLA Modules:
  0.0 340.4 jit_solution(7980959696925305144)
XLA Ops:
  10.1 1.4 reshape_squeeze.9
  16.5 46.8 %all-gather.3.cloned.1.call-done = bf16[2048,1024]{0,1:T(8,128)(2,1)} async-done(((bf16[128,1024]{0,1:T(8,128)(2,1)}), bf16[2048,1024]{0,1:T(8,128)(2,1)}) %all-gather.3.cloned.1.call-update) | async-done | bytes 4194320 | tf_op jit(solution)/shard_map/all_gather | solution.py:18
  63.3 4.8 %fusion.55 = (bf16[2048,512]{0,1:T(8,128)(2,1)}, bf16[2048,512]{0,1:T(8,128)(2,1)}) fusion(bf16[2048,1024]{0,1:T(8,128)(2,1)} %all-gather.3.cloned.1.call-done), kind=kLoop, calls=%fused_computation.129 | loop fusion | bytes 8388608 | tf_op jit(solution)/shard_map/split | solution.py:19
  68.1 39.9 %while.44 = (s32[]{:T(128)}, f32[4,512]{1,0:T(4,128)S(1)}, f32[4,512]{1,0:T(4,128)S(1)}, f32[4,512,128]{2,1,0:T(8,128)S(1)}, s32[]{:T(128)}, /*index=5*/s32[]{:T...) while((s32[]{:T(128)}, f32[4,512]{1,0:T(4,128)S(1)}, ...), condition=%wide.region_6.7_spmd.clone.clone, body=%wide.region_0.6_spmd.clone.clone.sunk | while | flops 1891420160 | bytes 19541308 | solution.py:78
  70.4 7.7 %conditional.8 = ((f32[4,512]{1,0:T(4,128)S(1)}, f32[4,512]{1,0:T(4,128)S(1)}, f32[4,512,128]{2,1,0:T(8,128)S(1)})) conditional(s32[]{:T(128)} %convert_element_type.118, (f32[4,512]{1,0:T(4,128)S(1)}, f32[4,512]{1,0:T(4,128)S(1)}, f32[4,512,128]{2,1,0:T(8,128)S(1)}) %tuple.160, (pred[512,512]{0,1:T(8,128)(4,1)S(1)}, s32[]{:T(128)}, ...), branch_computations={%region_2.2_spmd, %region_3.5_spmd} | conditional | flops 1890062336 | bytes 19267654 | solution.py:141
  70.4 1.3 constant_dynamic-slice_fusion
  73.6 4.4 %fusion.18 = f32[4,512,128]{2,1,0:T(8,128)S(1)} fusion(bf16[512,4,128]{0,2,1:T(8,128)(2,1)S(1)} %bitcast.111, f32[4,512,512]{2,1,0:T(8,128)S(1)} %get-tuple-element.1214, f32[4,512]{1,0:T(4,128)S(1)} %max.5, pred[512,512]{0,1:T(8,128)(4,1)S(1)} %get-tuple-element.924, f32[4,512,128]{2,1,0:T(8,128)S(1)} %get-tuple-element.929, ...), kind=kOutput, calls=%fused_computation.15 | convolution fusion | flops 1614282752 | bytes 7094272 | tf_op jit(solution)/shard_map/while/body/eval_jaxpr/cond/branch_1_fun/gqk,kge->gqe/dot_general | solution.py:136
  80.3 7.7 %conditional.8 = ((f32[4,512]{1,0:T(4,128)S(1)}, f32[4,512]{1,0:T(4,128)S(1)}, f32[4,512,128]{2,1,0:T(8,128)S(1)})) conditional(s32[]{:T(128)} %convert_element_type.118, (f32[4,512]{1,0:T(4,128)S(1)}, f32[4,512]{1,0:T(4,128)S(1)}, f32[4,512,128]{2,1,0:T(8,128)S(1)}) %tuple.160, (pred[512,512]{0,1:T(8,128)(4,1)S(1)}, s32[]{:T(128)}, ...), branch_computations={%region_2.2_spmd, %region_3.5_spmd} | conditional | flops 1890062336 | bytes 19267654 | solution.py:141
  80.4 1.3 constant_dynamic-slice_fusion
  83.6 4.4 %fusion.18 = f32[4,512,128]{2,1,0:T(8,128)S(1)} fusion(bf16[512,4,128]{0,2,1:T(8,128)(2,1)S(1)} %bitcast.111, f32[4,512,512]{2,1,0:T(8,128)S(1)} %get-tuple-element.1214, f32[4,512]{1,0:T(4,128)S(1)} %max.5, pred[512,512]{0,1:T(8,128)(4,1)S(1)} %get-tuple-element.924, f32[4,512,128]{2,1,0:T(8,128)S(1)} %get-tuple-element.929, ...), kind=kOutput, calls=%fused_computation.15 | convolution fusion | flops 1614282752 | bytes 7094272 | tf_op jit(solution)/shard_map/while/body/eval_jaxpr/cond/branch_1_fun/gqk,kge->gqe/dot_general | solution.py:136
  90.3 7.7 %conditional.8 = ((f32[4,512]{1,0:T(4,128)S(1)}, f32[4,512]{1,0:T(4,128)S(1)}, f32[4,512,128]{2,1,0:T(8,128)S(1)})) conditional(s32[]{:T(128)} %convert_element_type.118, (f32[4,512]{1,0:T(4,128)S(1)}, f32[4,512]{1,0:T(4,128)S(1)}, f32[4,512,128]{2,1,0:T(8,128)S(1)}) %tuple.160, (pred[512,512]{0,1:T(8,128)(4,1)S(1)}, s32[]{:T(128)}, ...), branch_computations={%region_2.2_spmd, %region_3.5_spmd} | conditional | flops 1890062336 | bytes 19267654 | solution.py:141
  90.3 1.3 constant_dynamic-slice_fusion
  93.6 4.4 %fusion.18 = f32[4,512,128]{2,1,0:T(8,128)S(1)} fusion(bf16[512,4,128]{0,2,1:T(8,128)(2,1)S(1)} %bitcast.111, f32[4,512,512]{2,1,0:T(8,128)S(1)} %get-tuple-element.1214, f32[4,512]{1,0:T(4,128)S(1)} %max.5, pred[512,512]{0,1:T(8,128)(4,1)S(1)} %get-tuple-element.924, f32[4,512,128]{2,1,0:T(8,128)S(1)} %get-tuple-element.929, ...), kind=kOutput, calls=%fused_computation.15 | convolution fusion | flops 1614282752 | bytes 7094272 | tf_op jit(solution)/shard_map/while/body/eval_jaxpr/cond/branch_1_fun/gqk,kge->gqe/dot_general | solution.py:136
  100.3 7.7 %conditional.8 = ((f32[4,512]{1,0:T(4,128)S(1)}, f32[4,512]{1,0:T(4,128)S(1)}, f32[4,512,128]{2,1,0:T(8,128)S(1)})) conditional(s32[]{:T(128)} %convert_element_type.118, (f32[4,512]{1,0:T(4,128)S(1)}, f32[4,512]{1,0:T(4,128)S(1)}, f32[4,512,128]{2,1,0:T(8,128)S(1)}) %tuple.160, (pred[512,512]{0,1:T(8,128)(4,1)S(1)}, s32[]{:T(128)}, ...), branch_computations={%region_2.2_spmd, %region_3.5_spmd} | conditional | flops 1890062336 | bytes 19267654 | solution.py:141
  100.3 1.3 constant_dynamic-slice_fusion
  103.6 4.4 %fusion.18 = f32[4,512,128]{2,1,0:T(8,128)S(1)} fusion(bf16[512,4,128]{0,2,1:T(8,128)(2,1)S(1)} %bitcast.111, f32[4,512,512]{2,1,0:T(8,128)S(1)} %get-tuple-element.1214, f32[4,512]{1,0:T(4,128)S(1)} %max.5, pred[512,512]{0,1:T(8,128)(4,1)S(1)} %get-tuple-element.924, f32[4,512,128]{2,1,0:T(8,128)S(1)} %get-tuple-element.929, ...), kind=kOutput, calls=%fused_computation.15 | convolution fusion | flops 1614282752 | bytes 7094272 | tf_op jit(solution)/shard_map/while/body/eval_jaxpr/cond/branch_1_fun/gqk,kge->gqe/dot_general | solution.py:136
  108.4 1.2 multiply_reduce_fusion
  109.7 2.5 broadcast.1267
  112.2 2.5 broadcast.1267.clone
  114.7 53.3 %while.45 = (s32[]{:T(128)}, f32[4,512,128]{2,1,0:T(8,128)S(1)}, f32[2048,512]{0,1:T(8,128)}, f32[2048,512]{0,1:T(8,128)}, s32[]{:T(128)}, /*index=5*/s32[]{:T(1...) while((s32[]{:T(128)}, f32[4,512,128]{2,1,0:T(8,128)S(1)}, ...), condition=%wide.region_12.13_spmd.clone.clone, body=%wide.region_8.12_spmd.clone.clone.sunk | while | flops 1355855872 | bytes 35949944 | solution.py:78
  117.0 11.0 %conditional.9 = ((f32[4,512,128]{2,1,0:T(8,128)S(1)}, f32[2048,512]{0,1:T(8,128)}, f32[2048,512]{0,1:T(8,128)})) conditional(s32[]{:T(128)} %convert_element_type.119, (f32[4,512,128]{2,1,0:T(8,128)S(1)}, f32[2048,512]{0,1:T(8,128)}, f32[2048,512]{0,1:T(8,128)}) %tuple.165, (pred[512,512]{0,1:T(8,128)(4,1)S(1)}, s32[]{:T(128)}, ...), branch_computations={%region_10.10_spmd, %region_11.11_spmd} | conditional | flops 1354498048 | bytes 35676240 | solution.py:196
  120.0 1.7 fusion.23
  121.7 1.2 convolution_add_fusion
  124.7 3.3 constant_dynamic-update-slice_fusion
  130.4 11.0 %conditional.9 = ((f32[4,512,128]{2,1,0:T(8,128)S(1)}, f32[2048,512]{0,1:T(8,128)}, f32[2048,512]{0,1:T(8,128)})) conditional(s32[]{:T(128)} %convert_element_type.119, (f32[4,512,128]{2,1,0:T(8,128)S(1)}, f32[2048,512]{0,1:T(8,128)}, f32[2048,512]{0,1:T(8,128)}) %tuple.165, (pred[512,512]{0,1:T(8,128)(4,1)S(1)}, s32[]{:T(128)}, ...), branch_computations={%region_10.10_spmd, %region_11.11_spmd} | conditional | flops 1354498048 | bytes 35676240 | solution.py:196
  133.3 1.7 fusion.23
  135.0 1.2 convolution_add_fusion
  138.1 3.3 constant_dynamic-update-slice_fusion
  143.7 10.9 %conditional.9 = ((f32[4,512,128]{2,1,0:T(8,128)S(1)}, f32[2048,512]{0,1:T(8,128)}, f32[2048,512]{0,1:T(8,128)})) conditional(s32[]{:T(128)} %convert_element_type.119, (f32[4,512,128]{2,1,0:T(8,128)S(1)}, f32[2048,512]{0,1:T(8,128)}, f32[2048,512]{0,1:T(8,128)}) %tuple.165, (pred[512,512]{0,1:T(8,128)(4,1)S(1)}, s32[]{:T(128)}, ...), branch_computations={%region_10.10_spmd, %region_11.11_spmd} | conditional | flops 1354498048 | bytes 35676240 | solution.py:196
  146.7 1.7 fusion.23
  148.4 1.2 convolution_add_fusion
  151.4 3.2 constant_dynamic-update-slice_fusion
  157.0 10.9 %conditional.9 = ((f32[4,512,128]{2,1,0:T(8,128)S(1)}, f32[2048,512]{0,1:T(8,128)}, f32[2048,512]{0,1:T(8,128)})) conditional(s32[]{:T(128)} %convert_element_type.119, (f32[4,512,128]{2,1,0:T(8,128)S(1)}, f32[2048,512]{0,1:T(8,128)}, f32[2048,512]{0,1:T(8,128)}) %tuple.165, (pred[512,512]{0,1:T(8,128)(4,1)S(1)}, s32[]{:T(128)}, ...), branch_computations={%region_10.10_spmd, %region_11.11_spmd} | conditional | flops 1354498048 | bytes 35676240 | solution.py:196
  160.0 1.7 fusion.23
  161.7 1.2 convolution_add_fusion
  164.7 3.3 constant_dynamic-update-slice_fusion
  168.0 4.6 %copy.91 = bf16[2048,512]{1,0:T(8,128)(2,1)} copy(f32[2048,512]{0,1:T(8,128)} %get-tuple-element.990) | data formatting | bytes 6291456 | tf_op jit(solution)/shard_map/while | solution.py:78
  172.6 4.6 %copy.90 = bf16[2048,512]{1,0:T(8,128)(2,1)} copy(f32[2048,512]{0,1:T(8,128)} %get-tuple-element.989) | data formatting | bytes 6291456 | tf_op jit(solution)/shard_map/while | solution.py:78
  177.2 4.7 %pad_maximum_fusion = bf16[2048,1024]{1,0:T(8,128)(2,1)} fusion(bf16[2048,512]{1,0:T(8,128)(2,1)} %copy.91, bf16[2048,512]{1,0:T(8,128)(2,1)} %copy.90), kind=kLoop, calls=%fused_computation.90 | loop fusion | flops 8388608 | bytes 8388608 | tf_op jit(solution)/shard_map/concatenate | solution.py:24
  182.5 69.4 %reduce-scatter.2.cloned.1.call-done = bf16[128,1024]{1,0:T(8,128)(2,1)} async-done(((bf16[2048,1024]{1,0:T(8,128)(2,1)}), bf16[128,1024]{1,0:T(8,128)(2,1)}) %reduce-scatter.2.cloned.1.call-update) | async-done | bytes 262160 | tf_op jit(solution)/shard_map/reduce_scatter | solution.py:25
  251.9 1.7 slice_convert_fusion
  255.9 1.6 copy.92
  258.2 26.5 %all_to_all.23 = bf16[128,16,256]{0,1,2:T(8,128)(2,1)S(1)} all-to-all(bf16[128,16,256]{0,1,2:T(8,128)(2,1)S(1)} %copy.93), channel_id=1, replica_groups=mesh['dp'=16,'blk'=16] {'blk'}, dimensions={2} | all-to-all | bytes 2097152 | tf_op jit(solution)/shard_map/all_to_all | solution.py:245
  285.4 18.4 %all-gather.5.cloned.1.call-done = bf16[2048,1024]{1,0:T(8,128)(2,1)} async-done(((bf16[128,1024]{1,0:T(8,128)(2,1)}), bf16[2048,1024]{1,0:T(8,128)(2,1)}) %all-gather.5.cloned.1.call-update) | async-done | bytes 4194320 | tf_op jit(solution)/shard_map/all_gather | solution.py:249
  303.8 3.4 %fusion.47 = f32[1024,256]{0,1:S(1)} fusion(bf16[2048,1024]{1,0:T(8,128)(2,1)} %all-gather.5.cloned.1.call-done, bf16[32,8,16,128]{3,2,1,0:T(8,128)(2,1)S(1)} %bitcast.122), kind=kOutput, calls=%fused_computation.91 | convolution fusion | flops 1073741824 | bytes 6291456
  308.1 8.5 %all-to-all-start.1 = ((bf16[16,1,16,1024]{3,2,1,0:T(8,128)(2,1)}), bf16[16,1,16,1024]{3,2,1,0:T(8,128)(2,1)S(1)}, u32[]{:S(2)}, u32[]{:S(2)}) async-start(bf16[16,1,16,1024]{3,2,1,0:T(8,128)(2,1)} %convert_bitcast_fusion), calls=%async_computation.2 | async-start | bytes 1048576 | tf_op jit(solution)/shard_map/all_to_all | solution.py:36
  317.2 1.2 convert_element_type.92
  318.4 14.8 %all-to-all-done.1 = bf16[16,1,16,1024]{3,2,1,0:T(8,128)(2,1)S(1)} async-done(((bf16[16,1,16,1024]{3,2,1,0:T(8,128)(2,1)}), bf16[16,1,16,1024]{3,2,1,0:T(8,128)(2,1)S(1)}, u32[]{:S(2)}, u32[]{:S(2)}) %all-to-all-start.1) | async-done | bytes 524320 | tf_op jit(solution)/shard_map/all_to_all | solution.py:36
  (117 shorter events, 53.5 us)
Async XLA Ops:
  7.2 5.5 %copy-start.1 = (bf16[1,128,2048]{2,1,0:T(8,128)(2,1)S(1)}, bf16[1,128,2048]{2,1,0:T(8,128)(2,1)}, u32[]{:S(2)}) copy-start(bf16[1,128,2048]{2,1,0:T(8,128)(2,1)} %param.17) | copy-start | bytes 1572868
  7.2 56.1 %all-gather.3.cloned.1.call-start = ((), (), s32[]{:S(2)}) async-start(), calls=%async_computation.3 | async-start | bytes 4456448 | tf_op jit(solution)/shard_map/all_gather | solution.py:18
  8.3 6.3 %copy-start.2 = (s32[1,3]{1,0:T(1,128)S(1)}, s32[1,3]{1,0:T(1,128)}, u32[]{:S(2)}) copy-start(s32[1,3]{1,0:T(1,128)} %param.19) | copy-start | bytes 40
  10.1 241.8 %reduce-scatter.2.cloned.1.call-start = ((), (), s32[]{:S(2)}) async-start(), calls=%async_computation.4 | async-start | bytes 4456448 | tf_op jit(solution)/shard_map/reduce_scatter | solution.py:25
  109.7 5.0 %copy-start = (bf16[4,512,128]{1,2,0:T(8,128)(2,1)S(1)}, bf16[4,512,128]{1,2,0:T(8,128)(2,1)}, u32[]{:S(2)}) copy-start(bf16[4,512,128]{1,2,0:T(8,128)(2,1)} %reshape.344) | copy-start | bytes 1572868
  182.0 121.8 %all-gather.5.cloned.1.call-start = ((), (), s32[]{:S(2)}) async-start(), calls=%async_computation.5 | async-start | bytes 4456448 | tf_op jit(solution)/shard_map/all_gather | solution.py:249
  308.1 25.1 %all-to-all-start.1 = ((bf16[16,1,16,1024]{3,2,1,0:T(8,128)(2,1)}), bf16[16,1,16,1024]{3,2,1,0:T(8,128)(2,1)S(1)}, u32[]{:S(2)}, u32[]{:S(2)}) async-start(bf16[16,1,16,1024]{3,2,1,0:T(8,128)(2,1)} %convert_bitcast_fusion), calls=%async_computation.2 | async-start | bytes 1048576 | tf_op jit(solution)/shard_map/all_to_all | solution.py:36
Sparse Core Ops, SparseCore 0:
  10.2 53.0 all-gather.2
  182.1 69.7 reduce-scatter.1
  256.0 47.7 all-gather.4
where the time goes:
time: 342 us; the launch traced here: 340 us
  waiting for transfers between devices  149 us (44%)
  matrix products  47 us (14%)
  local copies, waits for them, and re-layouts  45 us (13%)
  other arithmetic  42.9 us (13%)
  blocking collectives  26.5 us (8%)
  between operations  15.3 us (4%)
  starting transfers between devices  8.67 us (3%)
  loops' own time  5.55 us (2%)
    reduce_scatter x1, waiting for transfers between devices, in_one_piece(): whole = lax.psum_scatter(both, axis, scatter_dimension=dim, tiled=True)  69.4 us
    all_gather x1, waiting for transfers between devices, side_by_side(): whole = lax.all_gather(both, axis, axis=dim, tiled=True)  46.8 us
    all_to_all x1, blocking collectives, body(): lax.all_to_all(grouped_input, 'blk', split_axis=2, concat_axis=0, tiled=T...  26.5 us
    all_gather x1, waiting for transfers between devices, body(): lax.all_gather(grad_cols, 'blk', axis=0, tiled=True)  18.4 us
    dot_general x4, matrix products, forward_compute(): jnp.einsum('gqk,kge->gqe', weights, value_heads, precision=lax.Precision....  17.7 us
    all_to_all x1, waiting for transfers between devices, sum_at_owner(): lax.all_to_all(pieces, axis, split_axis=0, concat_axis=0, tiled=True)  14.8 us
    dynamic_slice x12, local copies, waits for them, and re-layouts, one_turn(): lax.dynamic_slice_in_dim(member, block_start, block_rows, 0)  13.8 us
    dynamic_update_slice x4, other arithmetic, backward_compute(): lax.dynamic_update_slice_in_dim(key_acc, lax.dynamic_slice_in_dim(key_acc...  13 us
  transfers between devices with their start and end apart: 4, of which 4 were waited for; matrix products, arithmetic and copies ran while one was open for 3% of the time, Pallas kernels for 0%

commit v1 on v0

v1 whole, which is shorter than its diff:
```python
import math

import jax
import jax.numpy as jnp
from jax import lax
from jax.experimental import pallas as pl
from jax.experimental.pallas import tpu as pltpu
from jax.sharding import PartitionSpec as P

MESH = pl.DeviceIdType.MESH
F32 = jnp.float32
BF16 = jnp.bfloat16
HEAD = 128
ROPE_BASE = 500000.0
MASKED = -1e30
FAR = 1 << 20
COPIES = 64
LOCALS = 16


def nn(a, b):
    return jnp.dot(a, b, preferred_element_type=F32)


def nt(a, b):
    return lax.dot_general(a, b, (((1,), (1,)), ((), ())), preferred_element_type=F32)


def kernel(
    len_ref, q_in, do_in, k_in, v_in, x_in,
    dq_out, dk_out, dv_out, w_out,
    qbuf, dobuf, kv, xv, xt, xbuf, qs, dos, kt, s_scr, dp_scr, p_t, ds_t, dqacc, dqbuf,
    dkvf, dkvb, ra, rb, rm, rp, gbuf, dkbuf, cosb, sinb, wacc, wb1, r1, wb2, r2, wfin,
    send, recv, loc,
):
    b = lax.axis_index("blk")
    dp = lax.axis_index("dp")
    y, w = b // 4, b % 4
    core = w % 2
    zhi, xx = dp // 4, dp % 4
    yp, y2, ym = (y + 1) % 4, (y + 2) % 4, (y + 3) % 4
    scale = 1.0 / math.sqrt(HEAD)
    prompt_len = len_ref[0]
    reject_start = len_ref[0] + len_ref[1]

    count = [0, 0]
    pending = []

    def remote(src, dst, device):
        i = count[0]
        count[0] += 1
        copy = pltpu.make_async_remote_copy(
            src_ref=src, dst_ref=dst, send_sem=send.at[i], recv_sem=recv.at[i],
            device_id=device, device_id_type=MESH,
        )
        copy.start()
        pending.append(copy)
        return copy

    def local(src, dst):
        i = count[1]
        count[1] += 1
        copy = pltpu.make_async_copy(src, dst, loc.at[i])
        copy.start()
        return copy

    def at_blk(yy, ww):
        return {"blk": 4 * yy + ww}

    def tile(i, size):
        return pl.ds(pl.multiple_of(i * size, size), size)

    barrier = pltpu.get_barrier_semaphore()
    for d in range(1, 4):
        pl.semaphore_signal(barrier, 1, device_id=at_blk(y, (w + d) % 4), device_id_type=MESH)
        pl.semaphore_signal(barrier, 1, device_id=at_blk((y + d) % 4, w), device_id_type=MESH)
        pl.semaphore_signal(
            barrier, 1, device_id={"dp": 4 * zhi + (xx + d) % 4}, device_id_type=MESH
        )
        pl.semaphore_signal(
            barrier, 1, device_id={"dp": 4 * ((zhi + d) % 4) + xx}, device_id_type=MESH
        )
    x_local = local(x_in, xv)
    kv_slots = (tile(4 * y + w, 64), tile(4 * (7 - y) + 3 - w, 64))
    own_kv = []
    for half in range(2):
        for part, ref in ((0, k_in), (1, v_in)):
            own_kv.append(
                local(
                    ref.at[pl.ds(64 * half, 64), tile(w, 128)],
                    kv.at[kv_slots[half], pl.ds(128 * part, 128)],
                )
            )
    own_q = [
        local(q_in.at[:, tile(w, 512)], qbuf.at[w]),
        local(do_in.at[:, tile(w, 512)], dobuf.at[w]),
    ]
    pl.semaphore_wait(barrier, 12)

    kv_first = []
    for d in (2, 1, 3):
        ww = (w + d) % 4
        for half in range(2):
            for part, ref in ((0, k_in), (1, v_in)):
                kv_first.append(
                    remote(
                        ref.at[pl.ds(64 * half, 64), tile(ww, 128)],
                        kv.at[kv_slots[half], pl.ds(128 * part, 128)],
                        at_blk(y, ww),
                    )
                )
    q_first = []
    for d in (2, 1, 3):
        ww = (w + d) % 4
        q_first.append(remote(q_in.at[:, tile(ww, 512)], qbuf.at[w], at_blk(y, ww)))
        q_first.append(remote(do_in.at[:, tile(ww, 512)], dobuf.at[w], at_blk(y, ww)))

    x_local.wait()

    def transpose_x(i, carry):
        block = xv[:, tile(i, 128)].T.reshape(2, 64, 128)
        xt[i // 2, pl.ds((i % 2) * 2, 2)] = block
        return carry

    lax.fori_loop(0, 32, transpose_x, 0)

    for copy in own_kv:
        copy.wait()
    for copy in kv_first:
        copy.wait_recv()
    kv_plus, kv_minus = [], []
    for yy, group in ((yp, kv_plus), (ym, kv_minus)):
        for slot in (tile(y, 256), tile(7 - y, 256)):
            group.append(remote(kv.at[slot], kv.at[slot], at_blk(yy, w)))
    column = tile(w, 128)
    x_first = []
    for d in (2, 1, 3):
        yy = (y + d) % 4
        x_first.append(remote(xt.at[:, yy], xbuf.at[y, :, :, column], at_blk(yy, w)))
    xbuf[y, :, :, column] = xt[:, y]

    lane_row = lax.broadcasted_iota(jnp.int32, (1, HEAD), 1)
    frequency = jnp.exp(
        -(2.0 * (lane_row % 64).astype(F32) / HEAD) * math.log(ROPE_BASE)
    )
    for half, block in ((0, y), (1, 7 - y)):
        position = 256 * block + lax.broadcasted_iota(jnp.int32, (256, HEAD), 0)
        angles = position.astype(F32) * frequency
        cosb[half] = jnp.cos(angles)
        sinb[half] = jnp.where(lane_row < 64, jnp.sin(angles), -jnp.sin(angles))

    for copy in kv_plus:
        copy.wait_recv()
    slot = tile(ym, 256)
    kv_second = [remote(kv.at[slot], kv.at[slot], at_blk(yp, w))]
    for copy in kv_minus:
        copy.wait_recv()
    slot = tile(7 - yp, 256)
    kv_second.append(remote(kv.at[slot], kv.at[slot], at_blk(ym, w)))

    for copy in own_q:
        copy.wait()
    for copy in q_first:
        copy.wait_recv()

    def stack(c, carry):
        half, h = c // 4, c % 4
        for ww in range(4):
            qs[c, pl.ds(64 * ww, 64)] = qbuf[ww, tile(half, 64), tile(h, 128)]
            dos[c, pl.ds(64 * ww, 64)] = dobuf[ww, tile(half, 64), tile(h, 128)]
        return carry

    lax.fori_loop(0, 8, stack, 0)

    for copy in kv_second:
        copy.wait_recv()

    def transpose_k(j, carry):
        kt[j] = kv[tile(j, 256), pl.ds(0, 128)].T
        return carry

    lax.fori_loop(0, 8, transpose_k, 0)

    for copy in x_first:
        copy.wait_recv()
    core_mate = at_blk(y, w + 1 - 2 * core)
    z_mate = at_blk(y, (w + 2) % 4)
    x_second = [
        remote(xbuf.at[:, :, :, column], xbuf.at[:, :, :, column], z_mate),
        remote(xbuf.at[:, :, :, column], xbuf.at[:, :, :, column], core_mate),
    ]

    lane = lax.broadcasted_iota(jnp.int32, (1, 256), 1)
    lane_high = (3 - lane // 64) * 64 + lane % 64
    rows = lax.broadcasted_iota(jnp.int32, (256, 256), 0)

    def chunk(c, carry):
        half, h = c // 4, c % 4
        diagonal = y + half * (7 - 2 * y)
        blocks = diagonal + 1
        query_pos = 256 * diagonal + lane + half * (lane_high - lane)
        rejected = query_pos >= reject_start
        query = qs[c]
        grad = dos[c]
        columns = tile(c, 256)

        def scores(j, top):
            s = nt(kv[tile(j, 256), pl.ds(0, 128)], query)
            key_pos = 256 * j + rows
            chosen = jnp.logical_and(key_pos >= prompt_len, key_pos < reject_start)
            shown = jnp.where(rejected, jnp.where(chosen, FAR, key_pos), key_pos)
            s = jnp.where(shown <= query_pos, s, MASKED)
            s_scr[j] = s
            return jnp.maximum(top, jnp.max(s.reshape(32, 8, 256), axis=0))

        top = lax.fori_loop(0, blocks, scores, jnp.full((8, 256), MASKED, F32))
        top = jnp.max(top, axis=0, keepdims=True)

        def weights(j, sums):
            total, dot_total = sums
            p = jnp.exp((s_scr[j] - top) * scale)
            d = nt(kv[tile(j, 256), pl.ds(128, 128)], grad)
            s_scr[j] = p
            dp_scr[j] = d
            total = total + jnp.sum(p.reshape(32, 8, 256), axis=0)
            dot_total = dot_total + jnp.sum((p * d).reshape(32, 8, 256), axis=0)
            return total, dot_total

        zero = jnp.zeros((8, 256), F32)
        total, dot_total = lax.fori_loop(0, blocks, weights, (zero, zero))
        inverse = 1.0 / jnp.sum(total, axis=0, keepdims=True)
        delta = jnp.sum(dot_total, axis=0, keepdims=True) * inverse
        dqacc[...] = jnp.zeros_like(dqacc)

        def gradients(j, carry):
            p = s_scr[j] * inverse
            ds = ((scale * p) * (dp_scr[j] - delta)).astype(BF16)
            p_t[j, :, columns] = p.astype(BF16)
            ds_t[j, :, columns] = ds
            dqacc[...] += nn(kt[j], ds)
            return carry

        lax.fori_loop(0, blocks, gradients, 0)
        dq = dqacc[...].T.astype(BF16)
        for ww in range(4):
            dqbuf[ww, tile(half, 64), tile(h, 128)] = dq[64 * ww : 64 * ww + 64]
        return carry

    lax.fori_loop(0, 8, chunk, 0)

    own_out, far_out = [local(dqbuf.at[w], dq_out.at[:, tile(w, 512)])], []
    for d in (2, 1, 3):
        ww = (w + d) % 4
        far_out.append(remote(dqbuf.at[ww], dq_out.at[:, tile(w, 512)], at_blk(y, ww)))

    def key_block(j):
        def product(half):
            lanes = pl.ds(1024 * half, 1024)
            dk = nn(ds_t[j, :, lanes], qs[pl.ds(4 * half, 4)].reshape(1024, 128))
            dv = nn(p_t[j, :, lanes], dos[pl.ds(4 * half, 4)].reshape(1024, 128))
            return dk, dv

        @pl.when(j <= 7 - y)
        def _():
            dk, dv = product(1)
            dkvf[j, :, pl.ds(0, 128)] = dk
            dkvf[j, :, pl.ds(128, 128)] = dv

        @pl.when(j > 7 - y)
        def _():
            dkvf[j] = jnp.zeros((256, 256), F32)

        @pl.when(j <= y)
        def _():
            dk, dv = product(0)
            dkvf[j, :, pl.ds(0, 128)] += dk
            dkvf[j, :, pl.ds(128, 128)] += dv

    def key_blocks(yy):
        def one(half, carry):
            key_block(yy + half * (7 - 2 * yy))
            return carry

        lax.fori_loop(0, 2, one, 0)

    key_blocks(y2)
    for j in (y2, 7 - y2):
        dkvb[j] = dkvf[j].astype(BF16)
    far_plus = remote(dkvb.at[y2], ra, at_blk(yp, w))
    far_minus = remote(dkvb.at[7 - y2], rb, at_blk(ym, w))
    key_blocks(yp)
    far_plus.wait_recv()
    dkvb[yp] = (dkvf[yp] + ra[...].astype(F32)).astype(BF16)
    dkvb[7 - yp] = dkvf[7 - yp].astype(BF16)
    near = [
        remote(dkvb.at[yp], rm.at[0], at_blk(yp, w)),
        remote(dkvb.at[7 - yp], rm.at[1], at_blk(yp, w)),
    ]
    key_blocks(ym)
    far_minus.wait_recv()
    dkvb[ym] = dkvf[ym].astype(BF16)
    dkvb[7 - ym] = (dkvf[7 - ym] + rb[...].astype(F32)).astype(BF16)
    near.append(remote(dkvb.at[ym], rp.at[0], at_blk(ym, w)))
    near.append(remote(dkvb.at[7 - ym], rp.at[1], at_blk(ym, w)))
    key_blocks(y)

    x_second[0].wait_recv()
    other = tile((w + 2) % 4, 128)
    x_third = remote(xbuf.at[:, :, :, other], xbuf.at[:, :, :, other], core_mate)

    for copy in near:
        copy.wait_recv()
    for half, j in ((0, y), (1, 7 - y)):
        total = dkvf[j] + rm[half].astype(F32) + rp[half].astype(F32)
        key_sum = total[:, :128]
        value_grad = total[:, 128:].astype(BF16)
        key_grad = key_sum.astype(BF16)
        key_pre = (
            key_sum * cosb[half] + pltpu.roll(key_sum, 64, 1) * sinb[half]
        ).astype(BF16)
        for ww in range(4):
            at = 64 * ww if half == 0 else 64 * (3 - ww)
            dst = pl.ds(128 * ww + 64 * half, 64)
            gbuf[y, dst, pl.ds(0, 128)] = key_pre[at : at + 64]
            gbuf[y, dst, pl.ds(128, 128)] = value_grad[at : at + 64]
            dkbuf[ww, pl.ds(64 * half, 64)] = key_grad[at : at + 64]

    g_near = [
        remote(gbuf.at[y], gbuf.at[y], at_blk(yp, w)),
        remote(gbuf.at[y], gbuf.at[y], at_blk(ym, w)),
    ]
    own_out.append(local(dkbuf.at[w], dk_out.at[:, column]))
    own_out.append(local(gbuf.at[y, tile(w, 128), pl.ds(128, 128)], dv_out.at[:, column]))
    for d in (2, 1, 3):
        ww = (w + d) % 4
        far_out.append(remote(dkbuf.at[ww], dk_out.at[:, column], at_blk(y, ww)))
        far_out.append(
            remote(
                gbuf.at[y, tile(ww, 128), pl.ds(128, 128)], dv_out.at[:, column], at_blk(y, ww)
            )
        )

    x_second[1].wait_recv()
    x_third.wait_recv()

    def weight_rows(yy, x_at):
        left = [xbuf[yy, 4 * k + x_at] for k in range(4)]
        return nn(jnp.concatenate(left, axis=0), gbuf[yy])

    def first_rows(i, carry):
        wacc[i] = weight_rows(y, i)
        return carry

    lax.fori_loop(0, 4, first_rows, 0)
    g_near[0].wait_recv()
    g_far = [remote(gbuf.at[ym, pl.ds(0, 256)], gbuf.at[ym, pl.ds(0, 256)], at_blk(yp, w))]
    g_near[1].wait_recv()
    g_far.append(
        remote(gbuf.at[yp, pl.ds(256, 256)], gbuf.at[yp, pl.ds(256, 256)], at_blk(ym, w))
    )

    def more_rows(i, carry):
        wacc[i] += weight_rows(ym, i)
        wacc[i] += weight_rows(yp, i)
        return carry

    lax.fori_loop(0, 4, more_rows, 0)
    for copy in g_far:
        copy.wait_recv()
    x_sums = []
    for d in (2, 1, 3):
        x_at = (xx + d) % 4
        wb1[x_at] = (wacc[x_at] + weight_rows(y2, x_at)).astype(BF16)
        x_sums.append(remote(wb1.at[x_at], r1.at[d - 1], {"dp": 4 * zhi + x_at}))
    mine = wacc[xx] + weight_rows(y2, xx)
    for copy in x_sums:
        copy.wait_recv()
    for d in range(3):
        mine = mine + r1[d].astype(F32)
    wacc[0] = mine
    wb2[...] = mine.astype(BF16)
    z_sums = []
    for d in (2, 1, 3):
        z_at = (zhi + d) % 4
        z_sums.append(remote(wb2.at[tile(z_at, 64)], r2.at[d - 1], {"dp": 4 * z_at + xx}))
    total = wacc[0, tile(zhi, 64)]
    for copy in z_sums:
        copy.wait_recv()
    for d in range(3):
        total = total + r2[d].astype(F32)
    wfin[...] = total.reshape(4, 16, 256)
    for part in range(2):
        lanes = pl.ds(128 * part, 128)
        dst = w_out.at[:, tile(4 * part + w, 128)]
        own_out.append(local(wfin.at[w, :, lanes], dst))
        for d in (2, 1, 3):
            ww = (w + d) % 4
            far_out.append(remote(wfin.at[ww, :, lanes], dst, at_blk(y, ww)))
    for copy in own_out:
        copy.wait()
    for copy in far_out:
        copy.wait_recv()
    for copy in pending:
        copy.wait_send()


def body(queries, keys, values, out_grad, layer_input, lengths):
    seq = 2048
    anywhere = pl.BlockSpec(memory_space=pltpu.HBM)
    vmem = pltpu.VMEM
    outs = pl.pallas_call(
        kernel,
        out_shape=(
            jax.ShapeDtypeStruct((128, 2048), BF16),
            jax.ShapeDtypeStruct((128, 512), BF16),
            jax.ShapeDtypeStruct((128, 512), BF16),
            jax.ShapeDtypeStruct((16, 1024), F32),
        ),
        in_specs=[pl.BlockSpec(memory_space=pltpu.SMEM)] + [anywhere] * 5,
        out_specs=(anywhere,) * 4,
        scratch_shapes=[
            vmem((4, 128, 512), BF16),
            vmem((4, 128, 512), BF16),
            vmem((2048, 256), BF16),
            vmem((128, 4096), BF16),
            vmem((16, 4, 64, 128), BF16),
            vmem((4, 16, 64, 512), BF16),
            vmem((8, 256, 128), BF16),
            vmem((8, 256, 128), BF16),
            vmem((8, 128, 256), BF16),
            vmem((8, 256, 256), F32),
            vmem((8, 256, 256), F32),
            vmem((8, 256, seq), BF16),
            vmem((8, 256, seq), BF16),
            vmem((128, 256), F32),
            vmem((4, 128, 512), BF16),
            vmem((8, 256, 256), F32),
            vmem((8, 256, 256), BF16),
            vmem((256, 256), BF16),
            vmem((256, 256), BF16),
            vmem((2, 256, 256), BF16),
            vmem((2, 256, 256), BF16),
            vmem((4, 512, 256), BF16),
            vmem((4, 128, 128), BF16),
            vmem((2, 256, 128), F32),
            vmem((2, 256, 128), F32),
            vmem((4, 256, 256), F32),
            vmem((4, 256, 256), BF16),
            vmem((3, 256, 256), BF16),
            vmem((256, 256), BF16),
            vmem((3, 64, 256), BF16),
            vmem((4, 16, 256), F32),
            pltpu.SemaphoreType.DMA((COPIES,)),
            pltpu.SemaphoreType.DMA((COPIES,)),
            pltpu.SemaphoreType.DMA((LOCALS,)),
        ],
        compiler_params=pltpu.CompilerParams(
            collective_id=0, has_side_effects=True, vmem_limit_bytes=60 * 1024 * 1024
        ),
        name="attention_backward",
    )(lengths[0], queries[0], out_grad[0], keys[0], values[0], layer_input[0])
    return (outs[0][None], outs[1][None], outs[2][None], outs[3])


def solution(mesh):
    placed = (P("dp", "blk", None),) * 5 + (P("dp", None),)
    return jax.shard_map(
        body,
        mesh=mesh,
        in_specs=placed,
        out_specs=(P("dp", "blk", None),) * 3 + (P(("dp", "blk"), None),),
        check_vma=False,
    )
```

time: 342 us -> 109 us (0.32)
  waiting for transfers between devices: 149 us -> 0 us
  Pallas kernels: 0 us -> 103 us
  matrix products: 47 us -> 0 us
  other arithmetic: 42.9 us -> 0 us
  local copies, waits for them, and re-layouts: 45 us -> 4.36 us
  blocking collectives: 26.5 us -> 0 us
  between operations: 15.3 us -> 0.65 us
  starting transfers between devices: 8.67 us -> 0 us
  loops' own time: 5.55 us -> 0 us
    pallas_call x0 -> x1, Pallas kernels: none -> 103 us  [body(): pl.pallas_call(kernel, out_shape=(jax.ShapeDtypeStruct((128, 2048), BF16)...]
    reduce_scatter x1 -> x0, waiting for transfers between devices: 69.4 us -> none  [in_one_piece(): whole = lax.psum_scatter(both, axis, scatter_dimension=dim, tiled=True)]
    all_gather x2 -> x0, waiting for transfers between devices: 65.1 us -> none  [the longest x1 46.8 us: side_by_side(): whole = lax.all_gather(both, axis, axis=dim, tiled=True)]
    dot_general x28 -> x0, matrix products: 43.6 us -> none  [the longest x4 17.7 us: forward_compute(): jnp.einsum('gqk,kge->gqe', weights, value_heads, precision=lax.Precision....]
    all_to_all x1 -> x0, blocking collectives: 26.5 us -> none  [body(): lax.all_to_all(grouped_input, 'blk', split_axis=2, concat_axis=0, tiled=T...]
    all_to_all x1 -> x0, waiting for transfers between devices: 14.8 us -> none  [sum_at_owner(): lax.all_to_all(pieces, axis, split_axis=0, concat_axis=0, tiled=True)]
    dynamic_slice x12 -> x0, local copies, waits for them, and re-layouts: 13.8 us -> none  [one_turn(): lax.dynamic_slice_in_dim(member, block_start, block_rows, 0)]
    dynamic_update_slice x4 -> x0, other arithmetic: 13 us -> none  [backward_compute(): lax.dynamic_update_slice_in_dim(key_acc, lax.dynamic_slice_in_dim(key_acc...]
  transfers between devices with their start and end apart: 4 -> 0, of which waited for: 4 -> 0; matrix products, arithmetic and copies ran while one was open for 3% -> 0% of each run, Pallas kernels for 0% -> 0%
where the time goes in v1:
time: 109 us; the launch traced here: 108 us
  Pallas kernels  103 us (94%)
  local copies, waits for them, and re-layouts  4.36 us (4%)
    pallas_call x1, Pallas kernels, body(): pl.pallas_call(kernel, out_shape=(jax.ShapeDtypeStruct((128, 2048), BF16)...  103 us
    unnamed x10, local copies, waits for them, and re-layouts  4.36 us

profile of v1, /device:TPU:1, one launch (start us, length us, event | category | flops | bytes accessed | tf_op | source)
XLA Modules:
  0.0 108.4 jit_solution(1634127317384806833)
XLA Ops:
  0.6 103.4 %attention_backward.1 = (bf16[128,2048]{1,0:T(8,128)(2,1)}, bf16[128,512]{1,0:T(8,128)(2,1)}, bf16[128,512]{1,0:T(8,128)(2,1)}, f32[16,1024]{1,0:T(8,128)}) custom-call(s32[3]{0:T(128)} %bitcast.17, bf16[128,2048]{1,0:T(8,128)(2,1)} %bitcast.10, bf16[128,2048]{1,0:T(8,128)(2,1)} %bitcast.11, bf16[128,512]{1,0:T(8,128)(2,1)} %bitcast.13, ...), custom_call_target="tpu_custom_call" | custom-call | tf_op jit(solution)/shard_map/attention_backward/pallas_call | solution.py:411
  104.0 0.0 copy-start.1
  104.0 1.9 %copy.14 = bf16[1,128,2048]{2,1,0:T(8,128)(2,1)} copy(bf16[1,128,2048]{2,1,0:T(8,128)(2,1)} %bitcast.12) | data formatting | bytes 1048576
  106.0 0.0 copy-done.1
  106.0 0.0 copy-start
  106.0 0.7 copy.15
  106.6 0.3 copy-done
  106.9 0.0 copy-start.2
  106.9 0.7 copy.16
  107.6 0.2 copy-done.2
  107.8 0.6 copy.17
Async XLA Ops:
  104.0 1.9 %copy-start.1 = (bf16[128,512]{1,0:T(8,128)(2,1)S(1)}, bf16[128,512]{1,0:T(8,128)(2,1)}, u32[]{:S(2)}) copy-start(bf16[128,512]{1,0:T(8,128)(2,1)} %get-tuple-element.9) | copy-start | bytes 393220
  106.0 1.0 copy-start
  106.9 0.9 copy-start.2

commit v2 on v1

v2 whole, which is shorter than its diff:
```python
import math

import jax
import jax.numpy as jnp
from jax import lax
from jax.experimental import pallas as pl
from jax.experimental.pallas import tpu as pltpu
from jax.sharding import PartitionSpec as P

MESH = pl.DeviceIdType.MESH
F32 = jnp.float32
BF16 = jnp.bfloat16
HEAD = 128
ROPE_BASE = 500000.0
MASKED = -1e30
FAR = 1 << 20
COPIES = 128
LOCALS = 16


def nn(a, b):
    return jnp.dot(a, b, preferred_element_type=F32)


def nt(a, b):
    return lax.dot_general(a, b, (((1,), (1,)), ((), ())), preferred_element_type=F32)


def kernel(
    len_ref, q_in, do_in, k_in, v_in, x_in,
    dq_out, dk_out, dv_out, w_out,
    qbuf, dobuf, kv, xv, xt, xbuf, qs, dos, qsn, dosn, kt, p_f, dp_s, p_t, ds_t, inv_s, dqacc,
    dqbuf, part_f, part_b, far_a, far_b, near_m, near_p, gbuf, dkbuf, cosb, sinb, wacc, wb1, r1,
    r2, w_stage, send, recv, loc,
):
    b = lax.axis_index("blk")
    dp = lax.axis_index("dp")
    y, w = b // 4, b % 4
    core = w % 2
    zhi, xx = dp // 4, dp % 4
    yp, y2, ym = (y + 1) % 4, (y + 2) % 4, (y + 3) % 4
    scale = 1.0 / math.sqrt(HEAD)
    prompt_len = len_ref[0]
    reject_start = len_ref[0] + len_ref[1]

    count = [0, 0]
    pending = []

    def remote(src, dst, device):
        i = count[0]
        count[0] += 1
        copy = pltpu.make_async_remote_copy(
            src_ref=src, dst_ref=dst, send_sem=send.at[i], recv_sem=recv.at[i],
            device_id=device, device_id_type=MESH,
        )
        copy.start()
        pending.append(copy)
        return copy

    def local(src, dst):
        i = count[1]
        count[1] += 1
        copy = pltpu.make_async_copy(src, dst, loc.at[i])
        copy.start()
        return copy

    def at_blk(yy, ww):
        return {"blk": 4 * yy + ww}

    def at_owner(zz, ww):
        return {"dp": 4 * zz + xx, "blk": 4 * y + ww}

    def tile(i, size):
        return pl.ds(pl.multiple_of(i * size, size), size)

    barrier = pltpu.get_barrier_semaphore()
    for d in range(1, 4):
        for device in (at_blk((y + d) % 4, w), {"dp": 4 * zhi + (xx + d) % 4}):
            pl.semaphore_signal(barrier, 1, device_id=device, device_id_type=MESH)
    for dz in range(4):
        for d in range(4):
            if dz or d:
                pl.semaphore_signal(
                    barrier, 1, device_id=at_owner((zhi + dz) % 4, (w + d) % 4),
                    device_id_type=MESH,
                )
    x_local = local(x_in, xv)
    kv_slots = (tile(4 * y + w, 64), tile(4 * (7 - y) + 3 - w, 64))
    own_kv = []
    for half in range(2):
        for part, ref in ((0, k_in), (1, v_in)):
            own_kv.append(
                local(
                    ref.at[pl.ds(64 * half, 64), tile(w, 128)],
                    kv.at[kv_slots[half], pl.ds(128 * part, 128)],
                )
            )
    own_q = [
        local(q_in.at[:, tile(w, 512)], qbuf.at[w]),
        local(do_in.at[:, tile(w, 512)], dobuf.at[w]),
    ]
    pl.semaphore_wait(barrier, 21)

    kv_first = []
    for d in (2, 1, 3):
        ww = (w + d) % 4
        for half in range(2):
            for part, ref in ((0, k_in), (1, v_in)):
                kv_first.append(
                    remote(
                        ref.at[pl.ds(64 * half, 64), tile(ww, 128)],
                        kv.at[kv_slots[half], pl.ds(128 * part, 128)],
                        at_blk(y, ww),
                    )
                )
    q_first = []
    for d in (2, 1, 3):
        ww = (w + d) % 4
        q_first.append(remote(q_in.at[:, tile(ww, 512)], qbuf.at[w], at_blk(y, ww)))
        q_first.append(remote(do_in.at[:, tile(ww, 512)], dobuf.at[w], at_blk(y, ww)))

    x_local.wait()

    def transpose_x(i, carry):
        block = xv[:, tile(i, 128)].T.reshape(2, 64, 128)
        xt[i // 2, pl.ds((i % 2) * 2, 2)] = block
        return carry

    lax.fori_loop(0, 32, transpose_x, 0)
    column = tile(w, 128)
    other = tile((w + 2) % 4, 128)
    core_mate = at_blk(y, w + 1 - 2 * core)
    z_mate = at_blk(y, (w + 2) % 4)
    xbuf[y, :, :, column] = xt[:, y]

    for copy in own_kv:
        copy.wait()
    for copy in kv_first:
        copy.wait_recv()
    kv_plus, kv_minus = [], []
    for yy, group in ((yp, kv_plus), (ym, kv_minus)):
        for slot in (tile(y, 256), tile(7 - y, 256)):
            group.append(remote(kv.at[slot], kv.at[slot], at_blk(yy, w)))
    x_far = [remote(xt.at[:, y], xbuf.at[y, :, :, column], z_mate)]
    x_mate = [remote(xt.at[:, y], xbuf.at[y, :, :, column], core_mate)]

    lane_row = lax.broadcasted_iota(jnp.int32, (1, HEAD), 1)
    frequency = jnp.exp(
        -(2.0 * (lane_row % 64).astype(F32) / HEAD) * math.log(ROPE_BASE)
    )
    for half, block in ((0, y), (1, 7 - y)):
        position = 256 * block + lax.broadcasted_iota(jnp.int32, (256, HEAD), 0)
        angles = position.astype(F32) * frequency
        cosb[half] = jnp.cos(angles)
        sinb[half] = jnp.where(lane_row < 64, jnp.sin(angles), -jnp.sin(angles))

    for copy in kv_plus:
        copy.wait_recv()
    slot = tile(ym, 256)
    kv_second = [remote(kv.at[slot], kv.at[slot], at_blk(yp, w))]
    for copy in kv_minus:
        copy.wait_recv()
    slot = tile(7 - yp, 256)
    kv_second.append(remote(kv.at[slot], kv.at[slot], at_blk(ym, w)))
    x_first = []
    for d in (1, 3, 2):
        yy = (y + d) % 4
        x_first.append(remote(xt.at[:, yy], xbuf.at[y, :, :, column], at_blk(yy, w)))

    for copy in own_q:
        copy.wait()
    for copy in q_first:
        copy.wait_recv()

    def stack(c, carry):
        half, h = c // 4, c % 4
        for ww in range(4):
            qs[c, pl.ds(64 * ww, 64)] = qbuf[ww, tile(half, 64), tile(h, 128)]
            dos[c, pl.ds(64 * ww, 64)] = dobuf[ww, tile(half, 64), tile(h, 128)]
        return carry

    lax.fori_loop(0, 8, stack, 0)

    for copy in kv_second:
        copy.wait_recv()

    lane = lax.broadcasted_iota(jnp.int32, (1, 256), 1)
    lane_high = (3 - lane // 64) * 64 + lane % 64
    rows = lax.broadcasted_iota(jnp.int32, (256, 256), 0)
    zero = jnp.zeros((8, 256), F32)

    def softmax_half(half, carry):
        diagonal = y + half * (7 - 2 * y)
        blocks = diagonal + 1
        query_pos = 256 * diagonal + lane + half * (lane_high - lane)
        rejected = query_pos >= reject_start

        def scores(j, tops):
            key_pos = 256 * j + rows
            chosen = jnp.logical_and(key_pos >= prompt_len, key_pos < reject_start)
            shown = jnp.where(rejected, jnp.where(chosen, FAR, key_pos), key_pos)
            bias = jnp.where(shown <= query_pos, 0.0, MASKED)
            key = kv[tile(j, 256), pl.ds(0, 128)]
            out = []
            for h in range(4):
                s = nt(key, qs[4 * half + h]) + bias
                p_f[4 * half + j, h] = s
                out.append(jnp.maximum(tops[h], jnp.max(s.reshape(32, 8, 256), axis=0)))
            return tuple(out)

        tops = lax.fori_loop(0, blocks, scores, (jnp.full((8, 256), MASKED, F32),) * 4)
        tops = [jnp.max(t, axis=0, keepdims=True) for t in tops]

        def weights(j, sums):
            out = []
            for h in range(4):
                p = jnp.exp2((p_f[4 * half + j, h] - tops[h]) * (scale * math.log2(math.e)))
                p_f[4 * half + j, h] = p
                p_t[4 * half + j, :, pl.ds(256 * h, 256)] = p.astype(BF16)
                out.append(sums[h] + jnp.sum(p.reshape(32, 8, 256), axis=0))
            return tuple(out)

        sums = lax.fori_loop(0, blocks, weights, (zero,) * 4)
        for h in range(4):
            inverse = 1.0 / jnp.sum(sums[h], axis=0, keepdims=True)
            inv_s[4 * half + h] = jnp.broadcast_to(inverse, (8, 256))
            per_row = jnp.broadcast_to(inverse, (128, 256)).T
            c = 4 * half + h
            dosn[c] = (dos[c].astype(F32) * per_row).astype(BF16)
            qsn[c] = (qs[c].astype(F32) * (per_row * scale)).astype(BF16)
        return carry

    lax.fori_loop(0, 2, softmax_half, 0)

    def sums_for(yy, left, right):
        g = (yy - y + 4) // 5
        low = nn(left[4 + yy], right[pl.ds(4, 4)].reshape(1024, 128))
        more = nn(
            left[g * (11 - yy) + (1 - g) * yy], right[pl.ds(4 * g, 4)].reshape(1024, 128)
        )
        keep = g.astype(F32)
        return low + more * (1.0 - keep), more * keep

    def own_sums(left, right):
        low = nn(left[4 + y], right[pl.ds(4, 4)].reshape(1024, 128))
        low = low + nn(left[y], right[pl.ds(0, 4)].reshape(1024, 128))
        return low, nn(left[11 - y], right[pl.ds(4, 4)].reshape(1024, 128))

    def reduce_first(part, left, right):
        low, high = sums_for(y2, left, right)
        part_b[part, y2, 0] = low.astype(BF16)
        part_b[part, y2, 1] = high.astype(BF16)
        return (
            remote(part_b.at[part, y2, 0], far_a.at[part], at_blk(yp, w)),
            remote(part_b.at[part, y2, 1], far_b.at[part], at_blk(ym, w)),
        )

    def reduce_middle(part, left, right):
        for yy in (yp, ym):
            low, high = sums_for(yy, left, right)
            part_f[part, yy, 0] = low
            part_f[part, yy, 1] = high

    def reduce_second(part, far):
        out = []
        far[0].wait_recv()
        part_b[part, yp, 0] = (part_f[part, yp, 0] + far_a[part].astype(F32)).astype(BF16)
        part_b[part, yp, 1] = part_f[part, yp, 1].astype(BF16)
        out.append(remote(part_b.at[part, yp], near_m.at[part], at_blk(yp, w)))
        far[1].wait_recv()
        part_b[part, ym, 0] = part_f[part, ym, 0].astype(BF16)
        part_b[part, ym, 1] = (part_f[part, ym, 1] + far_b[part].astype(F32)).astype(BF16)
        out.append(remote(part_b.at[part, ym], near_p.at[part], at_blk(ym, w)))
        return out

    def reduce_own(part, left, right):
        low, high = own_sums(left, right)
        part_f[part, y, 0] = low
        part_f[part, y, 1] = high

    far_v = reduce_first(1, p_t, dosn)
    reduce_middle(1, p_t, dosn)

    def transpose_k(j, carry):
        kt[j] = kv[tile(j, 256), pl.ds(0, 128)].T
        return carry

    lax.fori_loop(0, 8, transpose_k, 0)

    def score_grads(half):
        diagonal = y + half * (7 - 2 * y)
        blocks = diagonal + 1

        def products(j, sums):
            value = kv[tile(j, 256), pl.ds(128, 128)]
            out = []
            for h in range(4):
                d = nt(value, dos[4 * half + h])
                dp_s[j, h] = d
                pd = p_f[4 * half + j, h] * d
                out.append(sums[h] + jnp.sum(pd.reshape(32, 8, 256), axis=0))
            return tuple(out)

        sums = lax.fori_loop(0, blocks, products, (zero,) * 4)
        deltas = [
            jnp.sum(sums[h], axis=0, keepdims=True) * inv_s[4 * half + h, pl.ds(0, 1)]
            for h in range(4)
        ]
        dqacc[...] = jnp.zeros_like(dqacc)

        def grads(j, carry):
            key = kt[j]
            for h in range(4):
                ds = (p_f[4 * half + j, h] * (dp_s[j, h] - deltas[h])).astype(BF16)
                ds_t[4 * half + j, :, pl.ds(256 * h, 256)] = ds
                dqacc[h] += nn(key, ds)
            return carry

        lax.fori_loop(0, blocks, grads, 0)
        for h in range(4):
            dq = dqacc[h] * (inv_s[4 * half + h, pl.ds(0, 1)] * scale)
            dq = dq.T.astype(BF16)
            for ww in range(4):
                dqbuf[ww, pl.ds(64 * half, 64), pl.ds(128 * h, 128)] = dq[64 * ww : 64 * ww + 64]

    score_grads(1)
    for k, yy in ((0, ym), (1, yp)):
        x_first[k].wait_recv()
        x_far.append(remote(xbuf.at[yy, :, :, column], xbuf.at[yy, :, :, column], z_mate))
        x_mate.append(remote(xbuf.at[yy, :, :, column], xbuf.at[yy, :, :, column], core_mate))
    near_v = reduce_second(1, far_v)
    score_grads(0)

    far_k = reduce_first(0, ds_t, qsn)
    reduce_middle(0, ds_t, qsn)
    x_first[2].wait_recv()
    x_far.append(remote(xbuf.at[y2, :, :, column], xbuf.at[y2, :, :, column], z_mate))
    x_mate.append(remote(xbuf.at[y2, :, :, column], xbuf.at[y2, :, :, column], core_mate))
    own_out, far_out = [local(dqbuf.at[w], dq_out.at[:, tile(w, 512)])], []
    for d in (2, 1, 3):
        ww = (w + d) % 4
        far_out.append(remote(dqbuf.at[ww], dq_out.at[:, tile(w, 512)], at_blk(y, ww)))
    near_k = reduce_second(0, far_k)
    reduce_own(1, p_t, dosn)
    for copy in near_v:
        copy.wait_recv()

    def gathered(part, half):
        own = part_f[part, y, half]
        return own + near_m[part, half].astype(F32) + near_p[part, half].astype(F32)

    for half in range(2):
        value_grad = gathered(1, half).astype(BF16)
        for ww in range(4):
            at = 64 * ww if half == 0 else 64 * (3 - ww)
            gbuf[1, y, pl.ds(128 * ww + 64 * half, 64)] = value_grad[at : at + 64]

    def gather_near(part):
        return [
            remote(gbuf.at[part, y], gbuf.at[part, y], at_blk(yp, w)),
            remote(gbuf.at[part, y], gbuf.at[part, y], at_blk(ym, w)),
        ]

    def gather_far(part, near):
        low, high = pl.ds(0, 256), pl.ds(256, 256)
        near[0].wait_recv()
        first = remote(gbuf.at[part, ym, low], gbuf.at[part, ym, low], at_blk(yp, w))
        near[1].wait_recv()
        return [first, remote(gbuf.at[part, yp, high], gbuf.at[part, yp, high], at_blk(ym, w))]

    g_near_v = gather_near(1)
    reduce_own(0, ds_t, qsn)
    x_third = []
    for k, yy in ((0, y), (1, ym), (2, yp)):
        x_far[k].wait_recv()
        x_third.append(remote(xbuf.at[yy, :, :, other], xbuf.at[yy, :, :, other], core_mate))
    for copy in near_k:
        copy.wait_recv()
    for half in range(2):
        key_sum = gathered(0, half)
        key_grad = key_sum.astype(BF16)
        key_pre = (
            key_sum * cosb[half] + pltpu.roll(key_sum, 64, 1) * sinb[half]
        ).astype(BF16)
        for ww in range(4):
            at = 64 * ww if half == 0 else 64 * (3 - ww)
            gbuf[0, y, pl.ds(128 * ww + 64 * half, 64)] = key_pre[at : at + 64]
            dkbuf[ww, pl.ds(64 * half, 64)] = key_grad[at : at + 64]
    g_near_k = gather_near(0)
    g_far_v = gather_far(1, g_near_v)
    own_out.append(local(dkbuf.at[w], dk_out.at[:, column]))
    own_out.append(local(gbuf.at[1, y, tile(w, 128)], dv_out.at[:, column]))
    for d in (2, 1, 3):
        ww = (w + d) % 4
        far_out.append(remote(dkbuf.at[ww], dk_out.at[:, column], at_blk(y, ww)))
        far_out.append(
            remote(gbuf.at[1, y, tile(ww, 128)], dv_out.at[:, column], at_blk(y, ww))
        )
    x_far[3].wait_recv()
    x_third.append(remote(xbuf.at[y2, :, :, other], xbuf.at[y2, :, :, other], core_mate))
    for copy in x_mate:
        copy.wait_recv()
    for copy in x_third[:3]:
        copy.wait_recv()

    def weight_rows(part, yy, x_at):
        left = [xbuf[yy, 4 * k + x_at] for k in range(4)]
        return nn(jnp.concatenate(left, axis=0), gbuf[part, yy])

    def near_rows(part):
        def one(i, carry):
            rows_sum = weight_rows(part, y, i) + weight_rows(part, ym, i)
            wacc[part, i] = rows_sum + weight_rows(part, yp, i)
            return carry

        lax.fori_loop(0, 4, one, 0)

    def far_rows(part, far):
        for copy in far:
            copy.wait_recv()
        out = []
        for d in (2, 1, 3):
            x_at = (xx + d) % 4
            wb1[part, x_at] = (wacc[part, x_at] + weight_rows(part, y2, x_at)).astype(BF16)
            out.append(
                remote(wb1.at[part, x_at], r1.at[part, d - 1], {"dp": 4 * zhi + x_at})
            )
        wacc[part, xx] += weight_rows(part, y2, xx)
        return out

    def owner_sums(part, x_sums):
        total = wacc[part, xx]
        for copy in x_sums:
            copy.wait_recv()
        for d in range(3):
            total = total + r1[part, d].astype(F32)
        wb1[part, xx] = total.astype(BF16)
        out = []
        for dz in (2, 1, 3, 0):
            zz = (zhi + dz) % 4
            for d in (2, 1, 3, 0):
                ww = (w + d) % 4
                piece = pl.ds(pl.multiple_of(64 * zz + 16 * ww, 16), 16)
                if dz or d:
                    out.append(
                        remote(wb1.at[part, xx, piece], r2.at[part, zhi, w], at_owner(zz, ww))
                    )
                else:
                    r2[part, zhi, w] = wb1[part, xx, piece]
        return out

    near_rows(1)
    g_far_k = gather_far(0, g_near_k)
    x_third[3].wait_recv()
    x_sums_v = far_rows(1, g_far_v)
    near_rows(0)
    x_sums_k = far_rows(0, g_far_k)
    finals = owner_sums(1, x_sums_v)
    finals = finals + owner_sums(0, x_sums_k)
    for copy in finals:
        copy.wait_recv()
    for part in range(2):
        for ww in range(4):
            total = r2[part, 0, ww].astype(F32)
            for zz in range(1, 4):
                total = total + r2[part, zz, ww].astype(F32)
            w_stage[:, pl.ds(512 * part + 128 * ww, 128)] = total
    own_out.append(local(w_stage, w_out))
    for copy in own_out:
        copy.wait()
    for copy in far_out:
        copy.wait_recv()
    for copy in pending:
        copy.wait_send()


def body(queries, keys, values, out_grad, layer_input, lengths):
    anywhere = pl.BlockSpec(memory_space=pltpu.HBM)
    vmem = pltpu.VMEM
    outs = pl.pallas_call(
        kernel,
        out_shape=(
            jax.ShapeDtypeStruct((128, 2048), BF16),
            jax.ShapeDtypeStruct((128, 512), BF16),
            jax.ShapeDtypeStruct((128, 512), BF16),
            jax.ShapeDtypeStruct((16, 1024), F32),
        ),
        in_specs=[pl.BlockSpec(memory_space=pltpu.SMEM)] + [anywhere] * 5,
        out_specs=(anywhere,) * 4,
        scratch_shapes=[
            vmem((4, 128, 512), BF16),
            vmem((4, 128, 512), BF16),
            vmem((2048, 256), BF16),
            vmem((128, 4096), BF16),
            vmem((16, 4, 64, 128), BF16),
            vmem((4, 16, 64, 512), BF16),
            vmem((8, 256, 128), BF16),
            vmem((8, 256, 128), BF16),
            vmem((8, 256, 128), BF16),
            vmem((8, 256, 128), BF16),
            vmem((8, 128, 256), BF16),
            vmem((12, 4, 256, 256), F32),
            vmem((8, 4, 256, 256), F32),
            vmem((12, 256, 1024), BF16),
            vmem((12, 256, 1024), BF16),
            vmem((8, 8, 256), F32),
            vmem((4, 128, 256), F32),
            vmem((4, 128, 512), BF16),
            vmem((2, 4, 2, 256, 128), F32),
            vmem((2, 4, 2, 256, 128), BF16),
            vmem((2, 256, 128), BF16),
            vmem((2, 256, 128), BF16),
            vmem((2, 2, 256, 128), BF16),
            vmem((2, 2, 256, 128), BF16),
            vmem((2, 4, 512, 128), BF16),
            vmem((4, 128, 128), BF16),
            vmem((2, 256, 128), F32),
            vmem((2, 256, 128), F32),
            vmem((2, 4, 256, 128), F32),
            vmem((2, 4, 256, 128), BF16),
            vmem((2, 3, 256, 128), BF16),
            vmem((2, 4, 4, 16, 128), BF16),
            vmem((16, 1024), F32),
            pltpu.SemaphoreType.DMA((COPIES,)),
            pltpu.SemaphoreType.DMA((COPIES,)),
            pltpu.SemaphoreType.DMA((LOCALS,)),
        ],
        compiler_params=pltpu.CompilerParams(
            collective_id=0, has_side_effects=True, vmem_limit_bytes=60 * 1024 * 1024
        ),
        name="attention_backward",
    )(lengths[0], queries[0], out_grad[0], keys[0], values[0], layer_input[0])
    return (outs[0][None], outs[1][None], outs[2][None], outs[3])


def solution(mesh):
    placed = (P("dp", "blk", None),) * 5 + (P("dp", None),)
    return jax.shard_map(
        body,
        mesh=mesh,
        in_specs=placed,
        out_specs=(P("dp", "blk", None),) * 3 + (P(("dp", "blk"), None),),
        check_vma=False,
    )
```

time: 109 us -> 83.2 us (0.76)
  Pallas kernels: 103 us -> 78 us
    pallas_call x1, Pallas kernels: 103 us -> 78 us  [body(): pl.pallas_call(kernel, out_shape=(jax.ShapeDtypeStruct((128, 2048), BF16)...]
where the time goes in v2:
time: 83.2 us; the launch traced here: 83.1 us
  Pallas kernels  78 us (94%)
  local copies, waits for them, and re-layouts  4.36 us (5%)
    pallas_call x1, Pallas kernels, body(): pl.pallas_call(kernel, out_shape=(jax.ShapeDtypeStruct((128, 2048), BF16)...  78 us
    unnamed x10, local copies, waits for them, and re-layouts  4.36 us

profile of v2, /device:TPU:1, one launch (start us, length us, event | category | flops | bytes accessed | tf_op | source)
XLA Modules:
  0.0 83.1 jit_solution(14886403388605130845)
XLA Ops:
  0.6 78.0 %attention_backward.1 = (bf16[128,2048]{1,0:T(8,128)(2,1)}, bf16[128,512]{1,0:T(8,128)(2,1)}, bf16[128,512]{1,0:T(8,128)(2,1)}, f32[16,1024]{1,0:T(8,128)}) custom-call(s32[3]{0:T(128)} %bitcast.17, bf16[128,2048]{1,0:T(8,128)(2,1)} %bitcast.10, bf16[128,2048]{1,0:T(8,128)(2,1)} %bitcast.11, bf16[128,512]{1,0:T(8,128)(2,1)} %bitcast.13, ...), custom_call_target="tpu_custom_call" | custom-call | tf_op jit(solution)/shard_map/attention_backward/pallas_call | solution.py:480
  78.7 0.0 copy-start.1
  78.7 1.9 %copy.14 = bf16[1,128,2048]{2,1,0:T(8,128)(2,1)} copy(bf16[1,128,2048]{2,1,0:T(8,128)(2,1)} %bitcast.12) | data formatting | bytes 1048576
  80.6 0.0 copy-done.1
  80.6 0.0 copy-start
  80.6 0.7 copy.15
  81.3 0.3 copy-done
  81.6 0.0 copy-start.2
  81.6 0.7 copy.16
  82.2 0.2 copy-done.2
  82.4 0.6 copy.17
Async XLA Ops:
  78.7 1.9 %copy-start.1 = (bf16[128,512]{1,0:T(8,128)(2,1)S(1)}, bf16[128,512]{1,0:T(8,128)(2,1)}, u32[]{:S(2)}) copy-start(bf16[128,512]{1,0:T(8,128)(2,1)} %get-tuple-element.9) | copy-start | bytes 393220
  80.6 1.0 %copy-start = (bf16[128,512]{1,0:T(8,128)(2,1)S(1)}, bf16[128,512]{1,0:T(8,128)(2,1)}, u32[]{:S(2)}) copy-start(bf16[128,512]{1,0:T(8,128)(2,1)} %get-tuple-element.10) | copy-start | bytes 393220
  81.6 0.9 %copy-start.2 = (f32[16,1024]{1,0:T(8,128)S(1)}, f32[16,1024]{1,0:T(8,128)}, u32[]{:S(2)}) copy-start(f32[16,1024]{1,0:T(8,128)} %get-tuple-element.19) | copy-start | bytes 196612

commit v3 on v2

--- a/solution.py
+++ b/solution.py
@@ -30,7 +30,7 @@
     len_ref, q_in, do_in, k_in, v_in, x_in,
     dq_out, dk_out, dv_out, w_out,
     qbuf, dobuf, kv, xv, xt, xbuf, qs, dos, qsn, dosn, kt, p_f, dp_s, p_t, ds_t, inv_s, dqacc,
-    dqbuf, part_f, part_b, far_a, far_b, near_m, near_p, gbuf, dkbuf, cosb, sinb, wacc, wb1, r1,
+    dqbuf, part_f, part_b, near, gbuf, dkbuf, cosb, sinb, wacc, wb1, r1,
     r2, w_stage, send, recv, loc,
 ):
     b = lax.axis_index("blk")
@@ -38,7 +38,8 @@
     y, w = b // 4, b % 4
     core = w % 2
     zhi, xx = dp // 4, dp % 4
-    yp, y2, ym = (y + 1) % 4, (y + 2) % 4, (y + 3) % 4
+    yp, ym = (y + 1) % 4, (y + 3) % 4
+    xp, x2, xm = (xx + 1) % 4, (xx + 2) % 4, (xx + 3) % 4
     scale = 1.0 / math.sqrt(HEAD)
     prompt_len = len_ref[0]
     reject_start = len_ref[0] + len_ref[1]
@@ -66,6 +67,9 @@
 
     def at_blk(yy, ww):
         return {"blk": 4 * yy + ww}
+
+    def at_x(to):
+        return {"dp": 4 * zhi + to}
 
     def at_owner(zz, ww):
         return {"dp": 4 * zz + xx, "blk": 4 * y + ww}
@@ -101,29 +105,46 @@
     ]
     pl.semaphore_wait(barrier, 21)
 
-    kv_first = []
-    for d in (2, 1, 3):
+    def row_slots(ww):
+        return tile(4 * y + ww, 64), tile(4 * (7 - y) + 3 - ww, 64)
+
+    kv_first = {}
+    for d in (1, 3, 2):
         ww = (w + d) % 4
+        kv_first[d] = []
         for half in range(2):
             for part, ref in ((0, k_in), (1, v_in)):
-                kv_first.append(
+                kv_first[d].append(
                     remote(
                         ref.at[pl.ds(64 * half, 64), tile(ww, 128)],
                         kv.at[kv_slots[half], pl.ds(128 * part, 128)],
                         at_blk(y, ww),
                     )
                 )
-    q_first = []
-    for d in (2, 1, 3):
-        ww = (w + d) % 4
-        q_first.append(remote(q_in.at[:, tile(ww, 512)], qbuf.at[w], at_blk(y, ww)))
-        q_first.append(remote(do_in.at[:, tile(ww, 512)], dobuf.at[w], at_blk(y, ww)))
+    q_first, do_first = [], []
+    for ref, buf, group in ((q_in, qbuf, q_first), (do_in, dobuf, do_first)):
+        for d in (1, 3, 2):
+            ww = (w + d) % 4
+            group.append(remote(ref.at[:, tile(ww, 512)], buf.at[w], at_blk(y, ww)))
+
+    kv_plus, kv_minus = ([], []), ([], [])
+
+    def spread(ww):
+        slots = row_slots(ww)
+        for half in range(2):
+            kv_plus[half].append(remote(kv.at[slots[half]], kv.at[slots[half]], at_blk(yp, w)))
+            slot = slots[1 - half]
+            kv_minus[1 - half].append(remote(kv.at[slot], kv.at[slot], at_blk(ym, w)))
+
+    for copy in own_kv:
+        copy.wait()
+    spread(w)
 
     x_local.wait()
 
     def transpose_x(i, carry):
-        block = xv[:, tile(i, 128)].T.reshape(2, 64, 128)
-        xt[i // 2, pl.ds((i % 2) * 2, 2)] = block
+        to = i % 8 // 2
+        xt[to, i // 8, pl.ds((i % 2) * 2, 2)] = xv[:, tile(i, 128)].T.reshape(2, 64, 128)
         return carry
 
     lax.fori_loop(0, 32, transpose_x, 0)
@@ -131,19 +152,18 @@
     other = tile((w + 2) % 4, 128)
     core_mate = at_blk(y, w + 1 - 2 * core)
     z_mate = at_blk(y, (w + 2) % 4)
-    xbuf[y, :, :, column] = xt[:, y]
-
-    for copy in own_kv:
-        copy.wait()
-    for copy in kv_first:
-        copy.wait_recv()
-    kv_plus, kv_minus = [], []
-    for yy, group in ((yp, kv_plus), (ym, kv_minus)):
-        for slot in (tile(y, 256), tile(7 - y, 256)):
-            group.append(remote(kv.at[slot], kv.at[slot], at_blk(yy, w)))
-    x_far = [remote(xt.at[:, y], xbuf.at[y, :, :, column], z_mate)]
-    x_mate = [remote(xt.at[:, y], xbuf.at[y, :, :, column], core_mate)]
-
+    x_first = []
+    for d in (1, 3, 2):
+        to = (xx + d) % 4
+        x_first.append(remote(xt.at[to], xbuf.at[xx, :, :, :, column], at_x(to)))
+    x_far = [remote(xt.at[xx], xbuf.at[xx, :, :, :, column], z_mate)]
+    x_mate = [remote(xt.at[xx], xbuf.at[xx, :, :, :, column], core_mate)]
+
+    for d in (1, 3, 2):
+        for copy in kv_first[d]:
+            copy.wait_recv()
+        spread((w + 4 - d) % 4)
+    xbuf[xx, :, :, :, column] = xt[xx]
     lane_row = lax.broadcasted_iota(jnp.int32, (1, HEAD), 1)
     frequency = jnp.exp(
         -(2.0 * (lane_row % 64).astype(F32) / HEAD) * math.log(ROPE_BASE)
@@ -154,33 +174,40 @@
         cosb[half] = jnp.cos(angles)
         sinb[half] = jnp.where(lane_row < 64, jnp.sin(angles), -jnp.sin(angles))
 
-    for copy in kv_plus:
+    for copy in kv_plus[0]:
         copy.wait_recv()
     slot = tile(ym, 256)
     kv_second = [remote(kv.at[slot], kv.at[slot], at_blk(yp, w))]
-    for copy in kv_minus:
+    for copy in kv_minus[1]:
         copy.wait_recv()
     slot = tile(7 - yp, 256)
     kv_second.append(remote(kv.at[slot], kv.at[slot], at_blk(ym, w)))
-    x_first = []
-    for d in (1, 3, 2):
-        yy = (y + d) % 4
-        x_first.append(remote(xt.at[:, yy], xbuf.at[y, :, :, column], at_blk(yy, w)))
-
-    for copy in own_q:
-        copy.wait()
+    for copy in kv_plus[1] + kv_minus[0]:
+        copy.wait_recv()
+
+    own_q[0].wait()
     for copy in q_first:
         copy.wait_recv()
 
-    def stack(c, carry):
-        half, h = c // 4, c % 4
-        for ww in range(4):
-            qs[c, pl.ds(64 * ww, 64)] = qbuf[ww, tile(half, 64), tile(h, 128)]
-            dos[c, pl.ds(64 * ww, 64)] = dobuf[ww, tile(half, 64), tile(h, 128)]
-        return carry
-
-    lax.fori_loop(0, 8, stack, 0)
-
+    def stack(buf, stacked):
+        def one(c, carry):
+            half, h = c // 4, c % 4
+            for ww in range(4):
+                stacked[c, pl.ds(64 * ww, 64)] = buf[ww, tile(half, 64), tile(h, 128)]
+            return carry
+
+        lax.fori_loop(0, 8, one, 0)
+
+    stack(qbuf, qs)
+
+    def forward_x(k, src):
+        x_first[k].wait_recv()
+        ref = xbuf.at[src, :, :, :, column]
+        x_far.append(remote(ref, ref, z_mate))
+        x_mate.append(remote(ref, ref, core_mate))
+
+    forward_x(0, xm)
+    forward_x(1, xp)
     for copy in kv_second:
         copy.wait_recv()
 
@@ -224,14 +251,23 @@
         for h in range(4):
             inverse = 1.0 / jnp.sum(sums[h], axis=0, keepdims=True)
             inv_s[4 * half + h] = jnp.broadcast_to(inverse, (8, 256))
-            per_row = jnp.broadcast_to(inverse, (128, 256)).T
-            c = 4 * half + h
-            dosn[c] = (dos[c].astype(F32) * per_row).astype(BF16)
-            qsn[c] = (qs[c].astype(F32) * (per_row * scale)).astype(BF16)
         return carry
 
     lax.fori_loop(0, 2, softmax_half, 0)
 
+    forward_x(2, x2)
+    own_q[1].wait()
+    for copy in do_first:
+        copy.wait_recv()
+    stack(dobuf, dos)
+
+    def scale_rows(c, carry):
+        per_row = jnp.broadcast_to(inv_s[c, pl.ds(0, 1)], (128, 256)).T
+        dosn[c] = (dos[c].astype(F32) * per_row).astype(BF16)
+        qsn[c] = (qs[c].astype(F32) * (per_row * scale)).astype(BF16)
+        return carry
+
+    lax.fori_loop(0, 8, scale_rows, 0)
     def sums_for(yy, left, right):
         g = (yy - y + 4) // 5
         low = nn(left[4 + yy], right[pl.ds(4, 4)].reshape(1024, 128))
@@ -246,40 +282,22 @@
         low = low + nn(left[y], right[pl.ds(0, 4)].reshape(1024, 128))
         return low, nn(left[11 - y], right[pl.ds(4, 4)].reshape(1024, 128))
 
-    def reduce_first(part, left, right):
-        low, high = sums_for(y2, left, right)
-        part_b[part, y2, 0] = low.astype(BF16)
-        part_b[part, y2, 1] = high.astype(BF16)
-        return (
-            remote(part_b.at[part, y2, 0], far_a.at[part], at_blk(yp, w)),
-            remote(part_b.at[part, y2, 1], far_b.at[part], at_blk(ym, w)),
-        )
-
-    def reduce_middle(part, left, right):
-        for yy in (yp, ym):
+    def reduce_send(part, left, right):
+        out = []
+        for d in (2, 1, 3):
+            yy = (y + d) % 4
             low, high = sums_for(yy, left, right)
-            part_f[part, yy, 0] = low
-            part_f[part, yy, 1] = high
-
-    def reduce_second(part, far):
-        out = []
-        far[0].wait_recv()
-        part_b[part, yp, 0] = (part_f[part, yp, 0] + far_a[part].astype(F32)).astype(BF16)
-        part_b[part, yp, 1] = part_f[part, yp, 1].astype(BF16)
-        out.append(remote(part_b.at[part, yp], near_m.at[part], at_blk(yp, w)))
-        far[1].wait_recv()
-        part_b[part, ym, 0] = part_f[part, ym, 0].astype(BF16)
-        part_b[part, ym, 1] = (part_f[part, ym, 1] + far_b[part].astype(F32)).astype(BF16)
-        out.append(remote(part_b.at[part, ym], near_p.at[part], at_blk(ym, w)))
+            part_b[part, yy, 0] = low.astype(BF16)
+            part_b[part, yy, 1] = high.astype(BF16)
+            out.append(remote(part_b.at[part, yy], near.at[part, d - 1], at_blk(yy, w)))
         return out
 
     def reduce_own(part, left, right):
         low, high = own_sums(left, right)
-        part_f[part, y, 0] = low
-        part_f[part, y, 1] = high
-
-    far_v = reduce_first(1, p_t, dosn)
-    reduce_middle(1, p_t, dosn)
+        part_f[part, 0] = low
+        part_f[part, 1] = high
+
+    near_v = reduce_send(1, p_t, dosn)
 
     def transpose_k(j, carry):
         kt[j] = kv[tile(j, 256), pl.ds(0, 128)].T
@@ -324,56 +342,43 @@
                 dqbuf[ww, pl.ds(64 * half, 64), pl.ds(128 * h, 128)] = dq[64 * ww : 64 * ww + 64]
 
     score_grads(1)
-    for k, yy in ((0, ym), (1, yp)):
-        x_first[k].wait_recv()
-        x_far.append(remote(xbuf.at[yy, :, :, column], xbuf.at[yy, :, :, column], z_mate))
-        x_mate.append(remote(xbuf.at[yy, :, :, column], xbuf.at[yy, :, :, column], core_mate))
-    near_v = reduce_second(1, far_v)
     score_grads(0)
 
-    far_k = reduce_first(0, ds_t, qsn)
-    reduce_middle(0, ds_t, qsn)
-    x_first[2].wait_recv()
-    x_far.append(remote(xbuf.at[y2, :, :, column], xbuf.at[y2, :, :, column], z_mate))
-    x_mate.append(remote(xbuf.at[y2, :, :, column], xbuf.at[y2, :, :, column], core_mate))
+    near_k = reduce_send(0, ds_t, qsn)
     own_out, far_out = [local(dqbuf.at[w], dq_out.at[:, tile(w, 512)])], []
     for d in (2, 1, 3):
         ww = (w + d) % 4
         far_out.append(remote(dqbuf.at[ww], dq_out.at[:, tile(w, 512)], at_blk(y, ww)))
-    near_k = reduce_second(0, far_k)
     reduce_own(1, p_t, dosn)
     for copy in near_v:
         copy.wait_recv()
 
     def gathered(part, half):
-        own = part_f[part, y, half]
-        return own + near_m[part, half].astype(F32) + near_p[part, half].astype(F32)
+        total = part_f[part, half]
+        for d in range(3):
+            total = total + near[part, d, half].astype(F32)
+        return total
 
     for half in range(2):
         value_grad = gathered(1, half).astype(BF16)
         for ww in range(4):
             at = 64 * ww if half == 0 else 64 * (3 - ww)
-            gbuf[1, y, pl.ds(128 * ww + 64 * half, 64)] = value_grad[at : at + 64]
-
-    def gather_near(part):
-        return [
-            remote(gbuf.at[part, y], gbuf.at[part, y], at_blk(yp, w)),
-            remote(gbuf.at[part, y], gbuf.at[part, y], at_blk(ym, w)),
-        ]
-
-    def gather_far(part, near):
-        low, high = pl.ds(0, 256), pl.ds(256, 256)
-        near[0].wait_recv()
-        first = remote(gbuf.at[part, ym, low], gbuf.at[part, ym, low], at_blk(yp, w))
-        near[1].wait_recv()
-        return [first, remote(gbuf.at[part, yp, high], gbuf.at[part, yp, high], at_blk(ym, w))]
-
-    g_near_v = gather_near(1)
+            gbuf[1, xx, pl.ds(128 * ww + 64 * half, 64)] = value_grad[at : at + 64]
+
+    def gather(part):
+        ref = gbuf.at[part, xx]
+        return [remote(ref, ref, at_x((xx + d) % 4)) for d in (2, 1, 3)]
+
+    g_v = gather(1)
     reduce_own(0, ds_t, qsn)
     x_third = []
-    for k, yy in ((0, y), (1, ym), (2, yp)):
+
+    def third_x(k, src):
         x_far[k].wait_recv()
-        x_third.append(remote(xbuf.at[yy, :, :, other], xbuf.at[yy, :, :, other], core_mate))
+        ref = xbuf.at[src, :, :, :, other]
+        x_third.append(remote(ref, ref, core_mate))
+
+    third_x(0, xx)
     for copy in near_k:
         copy.wait_recv()
     for half in range(2):
@@ -384,57 +389,57 @@
         ).astype(BF16)
         for ww in range(4):
             at = 64 * ww if half == 0 else 64 * (3 - ww)
-            gbuf[0, y, pl.ds(128 * ww + 64 * half, 64)] = key_pre[at : at + 64]
+            gbuf[0, xx, pl.ds(128 * ww + 64 * half, 64)] = key_pre[at : at + 64]
             dkbuf[ww, pl.ds(64 * half, 64)] = key_grad[at : at + 64]
-    g_near_k = gather_near(0)
-    g_far_v = gather_far(1, g_near_v)
+    g_k = gather(0)
+    third_x(1, xm)
+    third_x(2, xp)
     own_out.append(local(dkbuf.at[w], dk_out.at[:, column]))
-    own_out.append(local(gbuf.at[1, y, tile(w, 128)], dv_out.at[:, column]))
+    own_out.append(local(gbuf.at[1, xx, tile(w, 128)], dv_out.at[:, column]))
+    third_x(3, x2)
     for d in (2, 1, 3):
         ww = (w + d) % 4
         far_out.append(remote(dkbuf.at[ww], dk_out.at[:, column], at_blk(y, ww)))
         far_out.append(
-            remote(gbuf.at[1, y, tile(ww, 128)], dv_out.at[:, column], at_blk(y, ww))
+            remote(gbuf.at[1, xx, tile(ww, 128)], dv_out.at[:, column], at_blk(y, ww))
         )
-    x_far[3].wait_recv()
-    x_third.append(remote(xbuf.at[y2, :, :, other], xbuf.at[y2, :, :, other], core_mate))
-    for copy in x_mate:
-        copy.wait_recv()
-    for copy in x_third[:3]:
-        copy.wait_recv()
-
-    def weight_rows(part, yy, x_at):
-        left = [xbuf[yy, 4 * k + x_at] for k in range(4)]
-        return nn(jnp.concatenate(left, axis=0), gbuf[part, yy])
+    for copy in x_mate + x_third:
+        copy.wait_recv()
+
+    def weight_rows(part, src, to):
+        left = [xbuf[src, k, to] for k in range(4)]
+        return nn(jnp.concatenate(left, axis=0), gbuf[part, src])
+
+    def own_rows(part):
+        def one(i, carry):
+            wacc[part, i] = weight_rows(part, xx, i)
+            return carry
+
+        lax.fori_loop(0, 4, one, 0)
 
     def near_rows(part):
         def one(i, carry):
-            rows_sum = weight_rows(part, y, i) + weight_rows(part, ym, i)
-            wacc[part, i] = rows_sum + weight_rows(part, yp, i)
+            wacc[part, i] += weight_rows(part, xm, i) + weight_rows(part, xp, i)
             return carry
 
         lax.fori_loop(0, 4, one, 0)
 
-    def far_rows(part, far):
-        for copy in far:
-            copy.wait_recv()
+    def far_rows(part):
         out = []
         for d in (2, 1, 3):
-            x_at = (xx + d) % 4
-            wb1[part, x_at] = (wacc[part, x_at] + weight_rows(part, y2, x_at)).astype(BF16)
-            out.append(
-                remote(wb1.at[part, x_at], r1.at[part, d - 1], {"dp": 4 * zhi + x_at})
-            )
-        wacc[part, xx] += weight_rows(part, y2, xx)
+            to = (y + d) % 4
+            wb1[part, to] = (wacc[part, to] + weight_rows(part, x2, to)).astype(BF16)
+            out.append(remote(wb1.at[part, to], r1.at[part, d - 1], at_blk(to, w)))
+        wacc[part, y] += weight_rows(part, x2, y)
         return out
 
-    def owner_sums(part, x_sums):
-        total = wacc[part, xx]
-        for copy in x_sums:
+    def owner_sums(part, y_sums):
+        total = wacc[part, y]
+        for copy in y_sums:
             copy.wait_recv()
         for d in range(3):
             total = total + r1[part, d].astype(F32)
-        wb1[part, xx] = total.astype(BF16)
+        wb1[part, y] = total.astype(BF16)
         out = []
         for dz in (2, 1, 3, 0):
             zz = (zhi + dz) % 4
@@ -443,20 +448,25 @@
                 piece = pl.ds(pl.multiple_of(64 * zz + 16 * ww, 16), 16)
                 if dz or d:
                     out.append(
-                        remote(wb1.at[part, xx, piece], r2.at[part, zhi, w], at_owner(zz, ww))
+                        remote(wb1.at[part, y, piece], r2.at[part, zhi, w], at_owner(zz, ww))
                     )
                 else:
-                    r2[part, zhi, w] = wb1[part, xx, piece]
+                    r2[part, zhi, w] = wb1[part, y, piece]
         return out
 
+    own_rows(1)
+    own_rows(0)
+    for copy in g_v:
+        copy.wait_recv()
     near_rows(1)
-    g_far_k = gather_far(0, g_near_k)
-    x_third[3].wait_recv()
-    x_sums_v = far_rows(1, g_far_v)
+    y_sums_v = far_rows(1)
+    for copy in g_k[1:]:
+        copy.wait_recv()
     near_rows(0)
-    x_sums_k = far_rows(0, g_far_k)
-    finals = owner_sums(1, x_sums_v)
-    finals = finals + owner_sums(0, x_sums_k)
+    g_k[0].wait_recv()
+    y_sums_k = far_rows(0)
+    finals = owner_sums(1, y_sums_v)
+    finals = finals + owner_sums(0, y_sums_k)
     for copy in finals:
         copy.wait_recv()
     for part in range(2):
@@ -492,8 +502,8 @@
             vmem((4, 128, 512), BF16),
             vmem((2048, 256), BF16),
             vmem((128, 4096), BF16),
-            vmem((16, 4, 64, 128), BF16),
-            vmem((4, 16, 64, 512), BF16),
+            vmem((4, 4, 4, 64, 128), BF16),
+            vmem((4, 4, 4, 64, 512), BF16),
             vmem((8, 256, 128), BF16),
             vmem((8, 256, 128), BF16),
             vmem((8, 256, 128), BF16),
@@ -506,12 +516,9 @@
             vmem((8, 8, 256), F32),
             vmem((4, 128, 256), F32),
             vmem((4, 128, 512), BF16),
-            vmem((2, 4, 2, 256, 128), F32),
+            vmem((2, 2, 256, 128), F32),
             vmem((2, 4, 2, 256, 128), BF16),
-            vmem((2, 256, 128), BF16),
-            vmem((2, 256, 128), BF16),
-            vmem((2, 2, 256, 128), BF16),
-            vmem((2, 2, 256, 128), BF16),
+            vmem((2, 3, 2, 256, 128), BF16),
             vmem((2, 4, 512, 128), BF16),
             vmem((4, 128, 128), BF16),
             vmem((2, 256, 128), F32),

time: 83.2 us -> 74.7 us (0.90)
  Pallas kernels: 78 us -> 69.5 us
    pallas_call x1, Pallas kernels: 78 us -> 69.5 us  [body(): pl.pallas_call(kernel, out_shape=(jax.ShapeDtypeStruct((128, 2048), BF16)...]
where the time goes in v3:
time: 74.7 us; the launch traced here: 74.5 us
  Pallas kernels  69.5 us (93%)
  local copies, waits for them, and re-layouts  4.36 us (6%)
    pallas_call x1, Pallas kernels, body(): pl.pallas_call(kernel, out_shape=(jax.ShapeDtypeStruct((128, 2048), BF16)...  69.5 us
    unnamed x10, local copies, waits for them, and re-layouts  4.36 us

profile of v3, /device:TPU:1, one launch (start us, length us, event | category | flops | bytes accessed | tf_op | source)
XLA Modules:
  0.0 74.5 jit_solution(3942094407523221947)
XLA Ops:
  0.6 69.5 %attention_backward.1 = (bf16[128,2048]{1,0:T(8,128)(2,1)}, bf16[128,512]{1,0:T(8,128)(2,1)}, bf16[128,512]{1,0:T(8,128)(2,1)}, f32[16,1024]{1,0:T(8,128)}) custom-call(s32[3]{0:T(128)} %bitcast.17, bf16[128,2048]{1,0:T(8,128)(2,1)} %bitcast.10, bf16[128,2048]{1,0:T(8,128)(2,1)} %bitcast.11, bf16[128,512]{1,0:T(8,128)(2,1)} %bitcast.13, ...), custom_call_target="tpu_custom_call" | custom-call | tf_op jit(solution)/shard_map/attention_backward/pallas_call | solution.py:490
  70.1 0.0 copy-start.1
  70.1 1.9 %copy.14 = bf16[1,128,2048]{2,1,0:T(8,128)(2,1)} copy(bf16[1,128,2048]{2,1,0:T(8,128)(2,1)} %bitcast.12) | data formatting | bytes 1048576
  72.0 0.0 copy-done.1
  72.0 0.0 copy-start
  72.0 0.7 copy.15
  72.7 0.3 copy-done
  73.0 0.0 copy-start.2
  73.0 0.7 copy.16
  73.7 0.2 copy-done.2
  73.9 0.6 copy.17
Async XLA Ops:
  70.1 1.9 %copy-start.1 = (bf16[128,512]{1,0:T(8,128)(2,1)S(1)}, bf16[128,512]{1,0:T(8,128)(2,1)}, u32[]{:S(2)}) copy-start(bf16[128,512]{1,0:T(8,128)(2,1)} %get-tuple-element.9) | copy-start | bytes 393220
  72.0 1.0 %copy-start = (bf16[128,512]{1,0:T(8,128)(2,1)S(1)}, bf16[128,512]{1,0:T(8,128)(2,1)}, u32[]{:S(2)}) copy-start(bf16[128,512]{1,0:T(8,128)(2,1)} %get-tuple-element.10) | copy-start | bytes 393220
  73.0 0.9 %copy-start.2 = (f32[16,1024]{1,0:T(8,128)S(1)}, f32[16,1024]{1,0:T(8,128)}, u32[]{:S(2)}) copy-start(f32[16,1024]{1,0:T(8,128)} %get-tuple-element.19) | copy-start | bytes 196612

commit v4 on v3

--- a/solution.py
+++ b/solution.py
@@ -29,8 +29,8 @@
 def kernel(
     len_ref, q_in, do_in, k_in, v_in, x_in,
     dq_out, dk_out, dv_out, w_out,
-    qbuf, dobuf, kv, xv, xt, xbuf, qs, dos, qsn, dosn, kt, p_f, dp_s, p_t, ds_t, inv_s, dqacc,
-    dqbuf, part_f, part_b, near, gbuf, dkbuf, cosb, sinb, wacc, wb1, r1,
+    qbuf, dobuf, kv, xv, xt, xbuf, qs, dos, qsn, dosn, kt, p_f, dp_s, p_t, ds_t, top_s, inv_s, del_s, dqacc,
+    dqbuf, part_f, part_b, near, gbuf, dkbuf, cosb, sinb, wb1, r1,
     r2, w_stage, send, recv, loc,
 ):
     b = lax.axis_index("blk")
@@ -144,7 +144,7 @@
 
     def transpose_x(i, carry):
         to = i % 8 // 2
-        xt[to, i // 8, pl.ds((i % 2) * 2, 2)] = xv[:, tile(i, 128)].T.reshape(2, 64, 128)
+        xt[to, pl.ds((i % 2) * 2, 2), i // 8] = xv[:, tile(i, 128)].T.reshape(2, 64, 128)
         return carry
 
     lax.fori_loop(0, 32, transpose_x, 0)
@@ -155,15 +155,15 @@
     x_first = []
     for d in (1, 3, 2):
         to = (xx + d) % 4
-        x_first.append(remote(xt.at[to], xbuf.at[xx, :, :, :, column], at_x(to)))
-    x_far = [remote(xt.at[xx], xbuf.at[xx, :, :, :, column], z_mate)]
-    x_mate = [remote(xt.at[xx], xbuf.at[xx, :, :, :, column], core_mate)]
+        x_first.append(remote(xt.at[to], xbuf.at[:, 4 - d, :, :, column], at_x(to)))
+    x_far = [remote(xt.at[xx], xbuf.at[:, 0, :, :, column], z_mate)]
+    x_mate = [remote(xt.at[xx], xbuf.at[:, 0, :, :, column], core_mate)]
 
     for d in (1, 3, 2):
         for copy in kv_first[d]:
             copy.wait_recv()
         spread((w + 4 - d) % 4)
-    xbuf[xx, :, :, :, column] = xt[xx]
+    xbuf[:, 0, :, :, column] = xt[xx]
     lane_row = lax.broadcasted_iota(jnp.int32, (1, HEAD), 1)
     frequency = jnp.exp(
         -(2.0 * (lane_row % 64).astype(F32) / HEAD) * math.log(ROPE_BASE)
@@ -174,14 +174,15 @@
         cosb[half] = jnp.cos(angles)
         sinb[half] = jnp.where(lane_row < 64, jnp.sin(angles), -jnp.sin(angles))
 
-    for copy in kv_plus[0]:
-        copy.wait_recv()
-    slot = tile(ym, 256)
-    kv_second = [remote(kv.at[slot], kv.at[slot], at_blk(yp, w))]
-    for copy in kv_minus[1]:
-        copy.wait_recv()
-    slot = tile(7 - yp, 256)
-    kv_second.append(remote(kv.at[slot], kv.at[slot], at_blk(ym, w)))
+    kv_second = []
+    for k, d in enumerate((0, 1, 3, 2)):
+        ww = (w + 4 - d) % 4
+        kv_plus[0][k].wait_recv()
+        slot = tile(4 * ym + ww, 64)
+        kv_second.append(remote(kv.at[slot], kv.at[slot], at_blk(yp, w)))
+        kv_minus[1][k].wait_recv()
+        slot = tile(4 * (7 - yp) + 3 - ww, 64)
+        kv_second.append(remote(kv.at[slot], kv.at[slot], at_blk(ym, w)))
     for copy in kv_plus[1] + kv_minus[0]:
         copy.wait_recv()
 
@@ -196,18 +197,10 @@
                 stacked[c, pl.ds(64 * ww, 64)] = buf[ww, tile(half, 64), tile(h, 128)]
             return carry
 
-        lax.fori_loop(0, 8, one, 0)
+        lax.fori_loop(0, 8, one, 0, unroll=True)
 
     stack(qbuf, qs)
 
-    def forward_x(k, src):
-        x_first[k].wait_recv()
-        ref = xbuf.at[src, :, :, :, column]
-        x_far.append(remote(ref, ref, z_mate))
-        x_mate.append(remote(ref, ref, core_mate))
-
-    forward_x(0, xm)
-    forward_x(1, xp)
     for copy in kv_second:
         copy.wait_recv()
 
@@ -236,30 +229,54 @@
             return tuple(out)
 
         tops = lax.fori_loop(0, blocks, scores, (jnp.full((8, 256), MASKED, F32),) * 4)
-        tops = [jnp.max(t, axis=0, keepdims=True) for t in tops]
-
-        def weights(j, sums):
-            out = []
-            for h in range(4):
-                p = jnp.exp2((p_f[4 * half + j, h] - tops[h]) * (scale * math.log2(math.e)))
-                p_f[4 * half + j, h] = p
-                p_t[4 * half + j, :, pl.ds(256 * h, 256)] = p.astype(BF16)
-                out.append(sums[h] + jnp.sum(p.reshape(32, 8, 256), axis=0))
-            return tuple(out)
-
-        sums = lax.fori_loop(0, blocks, weights, (zero,) * 4)
         for h in range(4):
-            inverse = 1.0 / jnp.sum(sums[h], axis=0, keepdims=True)
-            inv_s[4 * half + h] = jnp.broadcast_to(inverse, (8, 256))
+            top_s[4 * half + h] = jnp.broadcast_to(
+                jnp.max(tops[h], axis=0, keepdims=True), (8, 256)
+            )
         return carry
 
     lax.fori_loop(0, 2, softmax_half, 0)
 
-    forward_x(2, x2)
+    order = (2, 1, 3, 0)
+    for copy in x_first:
+        copy.wait_recv()
+    for d in order:
+        ref = xbuf.at[(y + d) % 4, pl.ds(1, 3), :, :, column]
+        x_far.append(remote(ref, ref, z_mate))
+        x_mate.append(remote(ref, ref, core_mate))
+
     own_q[1].wait()
     for copy in do_first:
         copy.wait_recv()
     stack(dobuf, dos)
+
+    def weights_half(half, carry):
+        blocks = y + half * (7 - 2 * y) + 1
+        tops = [top_s[4 * half + h, pl.ds(0, 1)] for h in range(4)]
+
+        def weights(j, sums):
+            value = kv[tile(j, 256), pl.ds(128, 128)]
+            slot = 4 * half + j
+            totals, dots = [], []
+            for h in range(4):
+                p = jnp.exp2((p_f[slot, h] - tops[h]) * (scale * math.log2(math.e)))
+                p_f[slot, h] = p
+                p_t[slot, :, pl.ds(256 * h, 256)] = p.astype(BF16)
+                totals.append(sums[0][h] + jnp.sum(p.reshape(32, 8, 256), axis=0))
+                d = nt(value, dos[4 * half + h])
+                dp_s[slot, h] = d
+                dots.append(sums[1][h] + jnp.sum((p * d).reshape(32, 8, 256), axis=0))
+            return tuple(totals), tuple(dots)
+
+        totals, dots = lax.fori_loop(0, blocks, weights, ((zero,) * 4, (zero,) * 4))
+        for h in range(4):
+            inverse = 1.0 / jnp.sum(totals[h], axis=0, keepdims=True)
+            delta = jnp.sum(dots[h], axis=0, keepdims=True) * inverse
+            inv_s[4 * half + h] = jnp.broadcast_to(inverse, (8, 256))
+            del_s[4 * half + h] = jnp.broadcast_to(delta, (8, 256))
+        return carry
+
+    lax.fori_loop(0, 2, weights_half, 0)
 
     def scale_rows(c, carry):
         per_row = jnp.broadcast_to(inv_s[c, pl.ds(0, 1)], (128, 256)).T
@@ -267,7 +284,7 @@
         qsn[c] = (qs[c].astype(F32) * (per_row * scale)).astype(BF16)
         return carry
 
-    lax.fori_loop(0, 8, scale_rows, 0)
+    lax.fori_loop(0, 8, scale_rows, 0, unroll=True)
     def sums_for(yy, left, right):
         g = (yy - y + 4) // 5
         low = nn(left[4 + yy], right[pl.ds(4, 4)].reshape(1024, 128))
@@ -299,56 +316,22 @@
 
     near_v = reduce_send(1, p_t, dosn)
 
-    def transpose_k(j, carry):
-        kt[j] = kv[tile(j, 256), pl.ds(0, 128)].T
-        return carry
-
-    lax.fori_loop(0, 8, transpose_k, 0)
-
-    def score_grads(half):
-        diagonal = y + half * (7 - 2 * y)
-        blocks = diagonal + 1
-
-        def products(j, sums):
-            value = kv[tile(j, 256), pl.ds(128, 128)]
-            out = []
+    def grads_half(half, carry):
+        blocks = y + half * (7 - 2 * y) + 1
+        deltas = [del_s[4 * half + h, pl.ds(0, 1)] for h in range(4)]
+
+        def grads(j, carry):
+            slot = 4 * half + j
             for h in range(4):
-                d = nt(value, dos[4 * half + h])
-                dp_s[j, h] = d
-                pd = p_f[4 * half + j, h] * d
-                out.append(sums[h] + jnp.sum(pd.reshape(32, 8, 256), axis=0))
-            return tuple(out)
-
-        sums = lax.fori_loop(0, blocks, products, (zero,) * 4)
-        deltas = [
-            jnp.sum(sums[h], axis=0, keepdims=True) * inv_s[4 * half + h, pl.ds(0, 1)]
-            for h in range(4)
-        ]
-        dqacc[...] = jnp.zeros_like(dqacc)
-
-        def grads(j, carry):
-            key = kt[j]
-            for h in range(4):
-                ds = (p_f[4 * half + j, h] * (dp_s[j, h] - deltas[h])).astype(BF16)
-                ds_t[4 * half + j, :, pl.ds(256 * h, 256)] = ds
-                dqacc[h] += nn(key, ds)
+                ds = p_f[slot, h] * (dp_s[slot, h] - deltas[h])
+                ds_t[slot, :, pl.ds(256 * h, 256)] = ds.astype(BF16)
             return carry
 
-        lax.fori_loop(0, blocks, grads, 0)
-        for h in range(4):
-            dq = dqacc[h] * (inv_s[4 * half + h, pl.ds(0, 1)] * scale)
-            dq = dq.T.astype(BF16)
-            for ww in range(4):
-                dqbuf[ww, pl.ds(64 * half, 64), pl.ds(128 * h, 128)] = dq[64 * ww : 64 * ww + 64]
-
-    score_grads(1)
-    score_grads(0)
+        return lax.fori_loop(0, blocks, grads, carry)
+
+    lax.fori_loop(0, 2, grads_half, 0)
 
     near_k = reduce_send(0, ds_t, qsn)
-    own_out, far_out = [local(dqbuf.at[w], dq_out.at[:, tile(w, 512)])], []
-    for d in (2, 1, 3):
-        ww = (w + d) % 4
-        far_out.append(remote(dqbuf.at[ww], dq_out.at[:, tile(w, 512)], at_blk(y, ww)))
     reduce_own(1, p_t, dosn)
     for copy in near_v:
         copy.wait_recv()
@@ -363,22 +346,57 @@
         value_grad = gathered(1, half).astype(BF16)
         for ww in range(4):
             at = 64 * ww if half == 0 else 64 * (3 - ww)
-            gbuf[1, xx, pl.ds(128 * ww + 64 * half, 64)] = value_grad[at : at + 64]
+            rows_at = pl.ds(128 * ww + 64 * half, 64)
+            gbuf[0, rows_at, pl.ds(128, 128)] = value_grad[at : at + 64]
 
     def gather(part):
-        ref = gbuf.at[part, xx]
-        return [remote(ref, ref, at_x((xx + d) % 4)) for d in (2, 1, 3)]
+        lanes = pl.ds(128 * part, 128)
+        return [
+            remote(gbuf.at[0, :, lanes], gbuf.at[4 - d, :, lanes], at_x((xx + d) % 4))
+            for d in (2, 1, 3)
+        ]
 
     g_v = gather(1)
     reduce_own(0, ds_t, qsn)
+    def transpose_k(j, carry):
+        kt[j] = kv[tile(j, 256), pl.ds(0, 128)].T
+        return carry
+
+    lax.fori_loop(0, 8, transpose_k, 0, unroll=2)
+
+    def query_half(half, carry):
+        blocks = y + half * (7 - 2 * y) + 1
+        dqacc[...] = jnp.zeros_like(dqacc)
+
+        def one(j, carry):
+            for h in range(4):
+                dqacc[h] += nn(kt[j], ds_t[4 * half + j, :, pl.ds(256 * h, 256)])
+            return carry
+
+        lax.fori_loop(0, blocks, one, 0)
+        for h in range(4):
+            dq = dqacc[h] * (inv_s[4 * half + h, pl.ds(0, 1)] * scale)
+            dq = dq.T.astype(BF16)
+            for ww in range(4):
+                dqbuf[ww, tile(half, 64), pl.ds(128 * h, 128)] = dq[64 * ww : 64 * ww + 64]
+        return carry
+
+    lax.fori_loop(0, 2, query_half, 0)
+    own_out, far_out = [local(dqbuf.at[w], dq_out.at[:, tile(w, 512)])], []
+    for d in (2, 1, 3):
+        ww = (w + d) % 4
+        far_out.append(remote(dqbuf.at[ww], dq_out.at[:, tile(w, 512)], at_blk(y, ww)))
     x_third = []
 
-    def third_x(k, src):
+    def third_x(k):
         x_far[k].wait_recv()
-        ref = xbuf.at[src, :, :, :, other]
+        if k == 0:
+            ref = xbuf.at[:, 0, :, :, other]
+        else:
+            ref = xbuf.at[(y + order[k - 1]) % 4, pl.ds(1, 3), :, :, other]
         x_third.append(remote(ref, ref, core_mate))
 
-    third_x(0, xx)
+    third_x(0)
     for copy in near_k:
         copy.wait_recv()
     for half in range(2):
@@ -389,92 +407,68 @@
         ).astype(BF16)
         for ww in range(4):
             at = 64 * ww if half == 0 else 64 * (3 - ww)
-            gbuf[0, xx, pl.ds(128 * ww + 64 * half, 64)] = key_pre[at : at + 64]
+            gbuf[0, pl.ds(128 * ww + 64 * half, 64), pl.ds(0, 128)] = key_pre[at : at + 64]
             dkbuf[ww, pl.ds(64 * half, 64)] = key_grad[at : at + 64]
     g_k = gather(0)
-    third_x(1, xm)
-    third_x(2, xp)
+    third_x(1)
+    values_out = pl.ds(128, 128)
     own_out.append(local(dkbuf.at[w], dk_out.at[:, column]))
-    own_out.append(local(gbuf.at[1, xx, tile(w, 128)], dv_out.at[:, column]))
-    third_x(3, x2)
+    own_out.append(local(gbuf.at[0, tile(w, 128), values_out], dv_out.at[:, column]))
     for d in (2, 1, 3):
         ww = (w + d) % 4
         far_out.append(remote(dkbuf.at[ww], dk_out.at[:, column], at_blk(y, ww)))
         far_out.append(
-            remote(gbuf.at[1, xx, tile(ww, 128)], dv_out.at[:, column], at_blk(y, ww))
+            remote(gbuf.at[0, tile(ww, 128), values_out], dv_out.at[:, column], at_blk(y, ww))
         )
-    for copy in x_mate + x_third:
-        copy.wait_recv()
-
-    def weight_rows(part, src, to):
-        left = [xbuf[src, k, to] for k in range(4)]
-        return nn(jnp.concatenate(left, axis=0), gbuf[part, src])
-
-    def own_rows(part):
-        def one(i, carry):
-            wacc[part, i] = weight_rows(part, xx, i)
-            return carry
-
-        lax.fori_loop(0, 4, one, 0)
-
-    def near_rows(part):
-        def one(i, carry):
-            wacc[part, i] += weight_rows(part, xm, i) + weight_rows(part, xp, i)
-            return carry
-
-        lax.fori_loop(0, 4, one, 0)
-
-    def far_rows(part):
-        out = []
-        for d in (2, 1, 3):
-            to = (y + d) % 4
-            wb1[part, to] = (wacc[part, to] + weight_rows(part, x2, to)).astype(BF16)
-            out.append(remote(wb1.at[part, to], r1.at[part, d - 1], at_blk(to, w)))
-        wacc[part, y] += weight_rows(part, x2, y)
-        return out
-
-    def owner_sums(part, y_sums):
-        total = wacc[part, y]
-        for copy in y_sums:
-            copy.wait_recv()
-        for d in range(3):
-            total = total + r1[part, d].astype(F32)
-        wb1[part, y] = total.astype(BF16)
-        out = []
-        for dz in (2, 1, 3, 0):
-            zz = (zhi + dz) % 4
-            for d in (2, 1, 3, 0):
-                ww = (w + d) % 4
-                piece = pl.ds(pl.multiple_of(64 * zz + 16 * ww, 16), 16)
-                if dz or d:
-                    out.append(
-                        remote(wb1.at[part, y, piece], r2.at[part, zhi, w], at_owner(zz, ww))
-                    )
-                else:
-                    r2[part, zhi, w] = wb1[part, y, piece]
-        return out
-
-    own_rows(1)
-    own_rows(0)
-    for copy in g_v:
-        copy.wait_recv()
-    near_rows(1)
-    y_sums_v = far_rows(1)
-    for copy in g_k[1:]:
-        copy.wait_recv()
-    near_rows(0)
-    g_k[0].wait_recv()
-    y_sums_k = far_rows(0)
-    finals = owner_sums(1, y_sums_v)
-    finals = finals + owner_sums(0, y_sums_k)
+
+    third_x(2)
+    for copy in g_v + g_k:
+        copy.wait_recv()
+
+    def weight_tile(to):
+        total = nn(xbuf[to, 0].reshape(256, 512), gbuf[0])
+        for rel in range(1, 4):
+            total = total + nn(xbuf[to, rel].reshape(256, 512), gbuf[rel])
+        return total
+
+    y_sums = []
+    x_mate[0].wait_recv()
+    x_third[0].wait_recv()
+    for k, d in enumerate(order[:3]):
+        to = (y + d) % 4
+        x_mate[k + 1].wait_recv()
+        x_third[k + 1].wait_recv()
+        wb1[to] = weight_tile(to).astype(BF16)
+        y_sums.append(remote(wb1.at[to], r1.at[d - 1], at_blk(to, w)))
+        if k:
+            third_x(k + 2)
+    x_mate[4].wait_recv()
+    x_third[4].wait_recv()
+    total = weight_tile(y)
+    for copy in y_sums:
+        copy.wait_recv()
+    for d in range(3):
+        total = total + r1[d].astype(F32)
+    wb1[y] = total.astype(BF16)
+    finals = []
+    for dz in (2, 1, 3, 0):
+        zz = (zhi + dz) % 4
+        for d in (2, 1, 3, 0):
+            ww = (w + d) % 4
+            piece = pl.ds(pl.multiple_of(64 * zz + 16 * ww, 16), 16)
+            if dz or d:
+                finals.append(remote(wb1.at[y, piece], r2.at[zhi, w], at_owner(zz, ww)))
+            else:
+                r2[zhi, w] = wb1[y, piece]
     for copy in finals:
         copy.wait_recv()
-    for part in range(2):
-        for ww in range(4):
-            total = r2[part, 0, ww].astype(F32)
-            for zz in range(1, 4):
-                total = total + r2[part, zz, ww].astype(F32)
-            w_stage[:, pl.ds(512 * part + 128 * ww, 128)] = total
+    for ww in range(4):
+        total = r2[0, ww].astype(F32)
+        for zz in range(1, 4):
+            total = total + r2[zz, ww].astype(F32)
+        for part in range(2):
+            lanes = pl.ds(512 * part + 128 * ww, 128)
+            w_stage[:, lanes] = total[:, 128 * part : 128 * part + 128]
     own_out.append(local(w_stage, w_out))
     for copy in own_out:
         copy.wait()
@@ -510,30 +504,31 @@
             vmem((8, 256, 128), BF16),
             vmem((8, 128, 256), BF16),
             vmem((12, 4, 256, 256), F32),
-            vmem((8, 4, 256, 256), F32),
+            vmem((12, 4, 256, 256), F32),
             vmem((12, 256, 1024), BF16),
             vmem((12, 256, 1024), BF16),
+            vmem((8, 8, 256), F32),
+            vmem((8, 8, 256), F32),
             vmem((8, 8, 256), F32),
             vmem((4, 128, 256), F32),
             vmem((4, 128, 512), BF16),
             vmem((2, 2, 256, 128), F32),
             vmem((2, 4, 2, 256, 128), BF16),
             vmem((2, 3, 2, 256, 128), BF16),
-            vmem((2, 4, 512, 128), BF16),
+            vmem((4, 512, 256), BF16),
             vmem((4, 128, 128), BF16),
             vmem((2, 256, 128), F32),
             vmem((2, 256, 128), F32),
-            vmem((2, 4, 256, 128), F32),
-            vmem((2, 4, 256, 128), BF16),
-            vmem((2, 3, 256, 128), BF16),
-            vmem((2, 4, 4, 16, 128), BF16),
+            vmem((4, 256, 256), BF16),
+            vmem((3, 256, 256), BF16),
+            vmem((4, 4, 16, 256), BF16),
             vmem((16, 1024), F32),
             pltpu.SemaphoreType.DMA((COPIES,)),
             pltpu.SemaphoreType.DMA((COPIES,)),
             pltpu.SemaphoreType.DMA((LOCALS,)),
         ],
         compiler_params=pltpu.CompilerParams(
-            collective_id=0, has_side_effects=True, vmem_limit_bytes=60 * 1024 * 1024
+            collective_id=0, has_side_effects=True, vmem_limit_bytes=62 * 1024 * 1024
         ),
         name="attention_backward",
     )(lengths[0], queries[0], out_grad[0], keys[0], values[0], layer_input[0])

time: 74.7 us -> 75.6 us (1.012)
  Pallas kernels: 69.5 us -> 70.4 us
    pallas_call x1, Pallas kernels: 69.5 us -> 70.4 us  [body(): pl.pallas_call(kernel, out_shape=(jax.ShapeDtypeStruct((128, 2048), BF16)...]
where the time goes in v4:
time: 75.6 us; the launch traced here: 75.4 us
  Pallas kernels  70.4 us (93%)
  local copies, waits for them, and re-layouts  4.36 us (6%)
    pallas_call x1, Pallas kernels, body(): pl.pallas_call(kernel, out_shape=(jax.ShapeDtypeStruct((128, 2048), BF16)...  70.4 us
    unnamed x10, local copies, waits for them, and re-layouts  4.36 us

profile of v4, /device:TPU:1, one launch (start us, length us, event | category | flops | bytes accessed | tf_op | source)
XLA Modules:
  0.0 75.4 jit_solution(17046085646198008405)
XLA Ops:
  0.6 70.4 %attention_backward.1 = (bf16[128,2048]{1,0:T(8,128)(2,1)}, bf16[128,512]{1,0:T(8,128)(2,1)}, bf16[128,512]{1,0:T(8,128)(2,1)}, f32[16,1024]{1,0:T(8,128)}) custom-call(s32[3]{0:T(128)} %bitcast.17, bf16[128,2048]{1,0:T(8,128)(2,1)} %bitcast.10, bf16[128,2048]{1,0:T(8,128)(2,1)} %bitcast.11, bf16[128,512]{1,0:T(8,128)(2,1)} %bitcast.13, ...), custom_call_target="tpu_custom_call" | custom-call | tf_op jit(solution)/shard_map/attention_backward/pallas_call | solution.py:484
  71.1 0.0 copy-start.1
  71.1 1.9 %copy.14 = bf16[1,128,2048]{2,1,0:T(8,128)(2,1)} copy(bf16[1,128,2048]{2,1,0:T(8,128)(2,1)} %bitcast.12) | data formatting | bytes 1048576
  73.0 0.0 copy-done.1
  73.0 0.0 copy-start
  73.0 0.7 copy.15
  73.6 0.3 copy-done
  73.9 0.0 copy-start.2
  73.9 0.7 copy.16
  74.6 0.2 copy-done.2
  74.8 0.6 copy.17
Async XLA Ops:
  71.1 1.9 %copy-start.1 = (bf16[128,512]{1,0:T(8,128)(2,1)S(1)}, bf16[128,512]{1,0:T(8,128)(2,1)}, u32[]{:S(2)}) copy-start(bf16[128,512]{1,0:T(8,128)(2,1)} %get-tuple-element.9) | copy-start | bytes 393220
  73.0 1.0 %copy-start = (bf16[128,512]{1,0:T(8,128)(2,1)S(1)}, bf16[128,512]{1,0:T(8,128)(2,1)}, u32[]{:S(2)}) copy-start(bf16[128,512]{1,0:T(8,128)(2,1)} %get-tuple-element.10) | copy-start | bytes 393220
  73.9 0.9 %copy-start.2 = (f32[16,1024]{1,0:T(8,128)S(1)}, f32[16,1024]{1,0:T(8,128)}, u32[]{:S(2)}) copy-start(f32[16,1024]{1,0:T(8,128)} %get-tuple-element.19) | copy-start | bytes 196612

commit v5 on v4

--- a/solution.py
+++ b/solution.py
@@ -14,7 +14,7 @@
 ROPE_BASE = 500000.0
 MASKED = -1e30
 FAR = 1 << 20
-COPIES = 128
+COPIES = 144
 LOCALS = 16
 
 
@@ -30,7 +30,7 @@
     len_ref, q_in, do_in, k_in, v_in, x_in,
     dq_out, dk_out, dv_out, w_out,
     qbuf, dobuf, kv, xv, xt, xbuf, qs, dos, qsn, dosn, kt, p_f, dp_s, p_t, ds_t, top_s, inv_s, del_s, dqacc,
-    dqbuf, part_f, part_b, near, gbuf, dkbuf, cosb, sinb, wb1, r1,
+    dqbuf, part_f, part_b, far_a, far_b, near_m, near_p, gbuf, dkbuf, cosb, sinb, wacc, wb1, r1,
     r2, w_stage, send, recv, loc,
 ):
     b = lax.axis_index("blk")
@@ -38,8 +38,8 @@
     y, w = b // 4, b % 4
     core = w % 2
     zhi, xx = dp // 4, dp % 4
-    yp, ym = (y + 1) % 4, (y + 3) % 4
-    xp, x2, xm = (xx + 1) % 4, (xx + 2) % 4, (xx + 3) % 4
+    yp, y2, ym = (y + 1) % 4, (y + 2) % 4, (y + 3) % 4
+    xp, xm = (xx + 1) % 4, (xx + 3) % 4
     scale = 1.0 / math.sqrt(HEAD)
     prompt_len = len_ref[0]
     reject_start = len_ref[0] + len_ref[1]
@@ -299,22 +299,40 @@
         low = low + nn(left[y], right[pl.ds(0, 4)].reshape(1024, 128))
         return low, nn(left[11 - y], right[pl.ds(4, 4)].reshape(1024, 128))
 
-    def reduce_send(part, left, right):
+    def reduce_first(part, left, right):
+        low, high = sums_for(y2, left, right)
+        part_b[part, y2, 0] = low.astype(BF16)
+        part_b[part, y2, 1] = high.astype(BF16)
+        return (
+            remote(part_b.at[part, y2, 0], far_a.at[part], at_blk(yp, w)),
+            remote(part_b.at[part, y2, 1], far_b.at[part], at_blk(ym, w)),
+        )
+
+    def reduce_middle(part, left, right):
+        for yy in (yp, ym):
+            low, high = sums_for(yy, left, right)
+            part_f[part, yy, 0] = low
+            part_f[part, yy, 1] = high
+
+    def reduce_second(part, far):
         out = []
-        for d in (2, 1, 3):
-            yy = (y + d) % 4
-            low, high = sums_for(yy, left, right)
-            part_b[part, yy, 0] = low.astype(BF16)
-            part_b[part, yy, 1] = high.astype(BF16)
-            out.append(remote(part_b.at[part, yy], near.at[part, d - 1], at_blk(yy, w)))
+        far[0].wait_recv()
+        part_b[part, yp, 0] = (part_f[part, yp, 0] + far_a[part].astype(F32)).astype(BF16)
+        part_b[part, yp, 1] = part_f[part, yp, 1].astype(BF16)
+        out.append(remote(part_b.at[part, yp], near_m.at[part], at_blk(yp, w)))
+        far[1].wait_recv()
+        part_b[part, ym, 0] = part_f[part, ym, 0].astype(BF16)
+        part_b[part, ym, 1] = (part_f[part, ym, 1] + far_b[part].astype(F32)).astype(BF16)
+        out.append(remote(part_b.at[part, ym], near_p.at[part], at_blk(ym, w)))
         return out
 
     def reduce_own(part, left, right):
         low, high = own_sums(left, right)
-        part_f[part, 0] = low
-        part_f[part, 1] = high
-
-    near_v = reduce_send(1, p_t, dosn)
+        part_f[part, y, 0] = low
+        part_f[part, y, 1] = high
+
+    far_v = reduce_first(1, p_t, dosn)
+    reduce_middle(1, p_t, dosn)
 
     def grads_half(half, carry):
         blocks = y + half * (7 - 2 * y) + 1
@@ -331,33 +349,12 @@
 
     lax.fori_loop(0, 2, grads_half, 0)
 
-    near_k = reduce_send(0, ds_t, qsn)
+    far_k = reduce_first(0, ds_t, qsn)
+    reduce_middle(0, ds_t, qsn)
+    near_v = reduce_second(1, far_v)
     reduce_own(1, p_t, dosn)
-    for copy in near_v:
-        copy.wait_recv()
-
-    def gathered(part, half):
-        total = part_f[part, half]
-        for d in range(3):
-            total = total + near[part, d, half].astype(F32)
-        return total
-
-    for half in range(2):
-        value_grad = gathered(1, half).astype(BF16)
-        for ww in range(4):
-            at = 64 * ww if half == 0 else 64 * (3 - ww)
-            rows_at = pl.ds(128 * ww + 64 * half, 64)
-            gbuf[0, rows_at, pl.ds(128, 128)] = value_grad[at : at + 64]
-
-    def gather(part):
-        lanes = pl.ds(128 * part, 128)
-        return [
-            remote(gbuf.at[0, :, lanes], gbuf.at[4 - d, :, lanes], at_x((xx + d) % 4))
-            for d in (2, 1, 3)
-        ]
-
-    g_v = gather(1)
     reduce_own(0, ds_t, qsn)
+    near_k = reduce_second(0, far_k)
     def transpose_k(j, carry):
         kt[j] = kv[tile(j, 256), pl.ds(0, 128)].T
         return carry
@@ -386,6 +383,36 @@
     for d in (2, 1, 3):
         ww = (w + d) % 4
         far_out.append(remote(dqbuf.at[ww], dq_out.at[:, tile(w, 512)], at_blk(y, ww)))
+    for copy in near_v:
+        copy.wait_recv()
+
+    def gathered(part, half):
+        own = part_f[part, y, half]
+        return own + near_m[part, half].astype(F32) + near_p[part, half].astype(F32)
+
+    for half in range(2):
+        value_grad = gathered(1, half).astype(BF16)
+        for ww in range(4):
+            at = 64 * ww if half == 0 else 64 * (3 - ww)
+            rows_at = pl.ds(128 * ww + 64 * half, 64)
+            gbuf[0, rows_at, pl.ds(128, 128)] = value_grad[at : at + 64]
+
+    def gather_near(part):
+        lanes = pl.ds(128 * part, 128)
+        return [
+            remote(gbuf.at[0, :, lanes], gbuf.at[3, :, lanes], at_x(xp)),
+            remote(gbuf.at[0, :, lanes], gbuf.at[1, :, lanes], at_x(xm)),
+        ]
+
+    def gather_far(part, near):
+        lanes = pl.ds(128 * part, 128)
+        low, high = pl.ds(0, 256), pl.ds(256, 256)
+        near[0].wait_recv()
+        first = remote(gbuf.at[3, low, lanes], gbuf.at[2, low, lanes], at_x(xp))
+        near[1].wait_recv()
+        return [first, remote(gbuf.at[1, high, lanes], gbuf.at[2, high, lanes], at_x(xm))]
+
+    g_v = gather_near(1)
     x_third = []
 
     def third_x(k):
@@ -409,7 +436,7 @@
             at = 64 * ww if half == 0 else 64 * (3 - ww)
             gbuf[0, pl.ds(128 * ww + 64 * half, 64), pl.ds(0, 128)] = key_pre[at : at + 64]
             dkbuf[ww, pl.ds(64 * half, 64)] = key_grad[at : at + 64]
-    g_k = gather(0)
+    g_k = gather_near(0)
     third_x(1)
     values_out = pl.ds(128, 128)
     own_out.append(local(dkbuf.at[w], dk_out.at[:, column]))
@@ -421,54 +448,83 @@
             remote(gbuf.at[0, tile(ww, 128), values_out], dv_out.at[:, column], at_blk(y, ww))
         )
 
+    far_g_v = gather_far(1, g_v)
     third_x(2)
-    for copy in g_v + g_k:
-        copy.wait_recv()
-
-    def weight_tile(to):
-        total = nn(xbuf[to, 0].reshape(256, 512), gbuf[0])
-        for rel in range(1, 4):
-            total = total + nn(xbuf[to, rel].reshape(256, 512), gbuf[rel])
+
+    def weights_of(part, to, rels):
+        lanes = pl.ds(128 * part, 128)
+        total = nn(xbuf[to, rels[0]].reshape(256, 512), gbuf[rels[0], :, lanes])
+        for rel in rels[1:]:
+            total = total + nn(xbuf[to, rel].reshape(256, 512), gbuf[rel, :, lanes])
         return total
 
-    y_sums = []
-    x_mate[0].wait_recv()
-    x_third[0].wait_recv()
-    for k, d in enumerate(order[:3]):
+    def near_tile(part, d):
         to = (y + d) % 4
-        x_mate[k + 1].wait_recv()
-        x_third[k + 1].wait_recv()
-        wb1[to] = weight_tile(to).astype(BF16)
-        y_sums.append(remote(wb1.at[to], r1.at[d - 1], at_blk(to, w)))
-        if k:
-            third_x(k + 2)
+        wacc[part, to] = weights_of(part, to, (0, 1, 3))
+
+    def far_tiles(part):
+        out = []
+        for d in order[:3]:
+            to = (y + d) % 4
+            wb1[part, to] = (wacc[part, to] + weights_of(part, to, (2,))).astype(BF16)
+            out.append(remote(wb1.at[part, to], r1.at[part, d - 1], at_blk(to, w)))
+        return out
+
+    def owner_sums(part, own, y_sums):
+        total = own
+        for copy in y_sums:
+            copy.wait_recv()
+        for d in range(3):
+            total = total + r1[part, d].astype(F32)
+        wb1[part, y] = total.astype(BF16)
+        out = []
+        for dz in (2, 1, 3, 0):
+            zz = (zhi + dz) % 4
+            for d in (2, 1, 3, 0):
+                ww = (w + d) % 4
+                piece = pl.ds(pl.multiple_of(64 * zz + 16 * ww, 16), 16)
+                if dz or d:
+                    out.append(
+                        remote(wb1.at[part, y, piece], r2.at[part, zhi, w], at_owner(zz, ww))
+                    )
+                else:
+                    r2[part, zhi, w] = wb1[part, y, piece]
+        return out
+
+    for k in range(3):
+        x_mate[k].wait_recv()
+        x_third[k].wait_recv()
+    near_tile(1, 2)
+    near_tile(1, 1)
+    third_x(3)
+    far_g_k = gather_far(0, g_k)
+    near_tile(0, 2)
+    near_tile(0, 1)
+    x_mate[3].wait_recv()
+    x_third[3].wait_recv()
+    near_tile(1, 3)
+    for copy in far_g_v:
+        copy.wait_recv()
+    y_sums_v = far_tiles(1)
+    near_tile(0, 3)
+    for copy in far_g_k:
+        copy.wait_recv()
+    y_sums_k = far_tiles(0)
+    third_x(4)
     x_mate[4].wait_recv()
     x_third[4].wait_recv()
-    total = weight_tile(y)
-    for copy in y_sums:
-        copy.wait_recv()
-    for d in range(3):
-        total = total + r1[d].astype(F32)
-    wb1[y] = total.astype(BF16)
-    finals = []
-    for dz in (2, 1, 3, 0):
-        zz = (zhi + dz) % 4
-        for d in (2, 1, 3, 0):
-            ww = (w + d) % 4
-            piece = pl.ds(pl.multiple_of(64 * zz + 16 * ww, 16), 16)
-            if dz or d:
-                finals.append(remote(wb1.at[y, piece], r2.at[zhi, w], at_owner(zz, ww)))
-            else:
-                r2[zhi, w] = wb1[y, piece]
+    own_v = weights_of(1, y, (0, 1, 2, 3))
+    wacc[0, y] = weights_of(0, y, (0, 1, 2, 3))
+    finals = owner_sums(1, own_v, y_sums_v)
+    finals = finals + owner_sums(0, wacc[0, y], y_sums_k)
     for copy in finals:
         copy.wait_recv()
-    for ww in range(4):
-        total = r2[0, ww].astype(F32)
-        for zz in range(1, 4):
-            total = total + r2[zz, ww].astype(F32)
-        for part in range(2):
-            lanes = pl.ds(512 * part + 128 * ww, 128)
-            w_stage[:, lanes] = total[:, 128 * part : 128 * part + 128]
+    for part in range(2):
+        for ww in range(4):
+            total = r2[part, 0, ww].astype(F32)
+            for zz in range(1, 4):
+                total = total + r2[part, zz, ww].astype(F32)
+            w_stage[:, pl.ds(512 * part + 128 * ww, 128)] = total
     own_out.append(local(w_stage, w_out))
     for copy in own_out:
         copy.wait()
@@ -512,16 +568,20 @@
             vmem((8, 8, 256), F32),
             vmem((4, 128, 256), F32),
             vmem((4, 128, 512), BF16),
-            vmem((2, 2, 256, 128), F32),
+            vmem((2, 4, 2, 256, 128), F32),
             vmem((2, 4, 2, 256, 128), BF16),
-            vmem((2, 3, 2, 256, 128), BF16),
+            vmem((2, 256, 128), BF16),
+            vmem((2, 256, 128), BF16),
+            vmem((2, 2, 256, 128), BF16),
+            vmem((2, 2, 256, 128), BF16),
             vmem((4, 512, 256), BF16),
             vmem((4, 128, 128), BF16),
             vmem((2, 256, 128), F32),
             vmem((2, 256, 128), F32),
-            vmem((4, 256, 256), BF16),
-            vmem((3, 256, 256), BF16),
-            vmem((4, 4, 16, 256), BF16),
+            vmem((2, 4, 256, 128), F32),
+            vmem((2, 4, 256, 128), BF16),
+            vmem((2, 3, 256, 128), BF16),
+            vmem((2, 4, 4, 16, 128), BF16),
             vmem((16, 1024), F32),
             pltpu.SemaphoreType.DMA((COPIES,)),
             pltpu.SemaphoreType.DMA((COPIES,)),

time: 75.6 us -> 71.8 us (0.950)
  Pallas kernels: 70.4 us -> 66.6 us
    pallas_call x1, Pallas kernels: 70.4 us -> 66.6 us  [body(): pl.pallas_call(kernel, out_shape=(jax.ShapeDtypeStruct((128, 2048), BF16)...]
where the time goes in v5:
time: 71.8 us; the launch traced here: 71.6 us
  Pallas kernels  66.6 us (93%)
  local copies, waits for them, and re-layouts  4.36 us (6%)
    pallas_call x1, Pallas kernels, body(): pl.pallas_call(kernel, out_shape=(jax.ShapeDtypeStruct((128, 2048), BF16)...  66.6 us
    unnamed x10, local copies, waits for them, and re-layouts  4.36 us

profile of v5, /device:TPU:1, one launch (start us, length us, event | category | flops | bytes accessed | tf_op | source)
XLA Modules:
  0.0 71.6 jit_solution(10528767838958141336)
XLA Ops:
  0.6 66.6 %attention_backward.1 = (bf16[128,2048]{1,0:T(8,128)(2,1)}, bf16[128,512]{1,0:T(8,128)(2,1)}, bf16[128,512]{1,0:T(8,128)(2,1)}, f32[16,1024]{1,0:T(8,128)}) custom-call(s32[3]{0:T(128)} %bitcast.17, bf16[128,2048]{1,0:T(8,128)(2,1)} %bitcast.10, bf16[128,2048]{1,0:T(8,128)(2,1)} %bitcast.11, bf16[128,512]{1,0:T(8,128)(2,1)} %bitcast.13, ...), custom_call_target="tpu_custom_call" | custom-call | tf_op jit(solution)/shard_map/attention_backward/pallas_call | solution.py:540
  67.2 0.0 copy-start.1
  67.2 1.9 %copy.14 = bf16[1,128,2048]{2,1,0:T(8,128)(2,1)} copy(bf16[1,128,2048]{2,1,0:T(8,128)(2,1)} %bitcast.12) | data formatting | bytes 1048576
  69.2 0.0 copy-done.1
  69.2 0.0 copy-start
  69.2 0.7 copy.15
  69.8 0.3 copy-done
  70.1 0.0 copy-start.2
  70.1 0.7 copy.16
  70.8 0.2 copy-done.2
  71.0 0.6 copy.17
Async XLA Ops:
  67.2 1.9 %copy-start.1 = (bf16[128,512]{1,0:T(8,128)(2,1)S(1)}, bf16[128,512]{1,0:T(8,128)(2,1)}, u32[]{:S(2)}) copy-start(bf16[128,512]{1,0:T(8,128)(2,1)} %get-tuple-element.9) | copy-start | bytes 393220
  69.2 1.0 %copy-start = (bf16[128,512]{1,0:T(8,128)(2,1)S(1)}, bf16[128,512]{1,0:T(8,128)(2,1)}, u32[]{:S(2)}) copy-start(bf16[128,512]{1,0:T(8,128)(2,1)} %get-tuple-element.10) | copy-start | bytes 393220
  70.1 0.9 %copy-start.2 = (f32[16,1024]{1,0:T(8,128)S(1)}, f32[16,1024]{1,0:T(8,128)}, u32[]{:S(2)}) copy-start(f32[16,1024]{1,0:T(8,128)} %get-tuple-element.19) | copy-start | bytes 196612

commit v6 on v5

--- a/solution.py
+++ b/solution.py
@@ -14,8 +14,9 @@
 ROPE_BASE = 500000.0
 MASKED = -1e30
 FAR = 1 << 20
-COPIES = 144
-LOCALS = 16
+SENDS = 11
+ARRIVALS = 51
+LOCALS = 17
 
 
 def nn(a, b):
@@ -29,7 +30,7 @@
 def kernel(
     len_ref, q_in, do_in, k_in, v_in, x_in,
     dq_out, dk_out, dv_out, w_out,
-    qbuf, dobuf, kv, xv, xt, xbuf, qs, dos, qsn, dosn, kt, p_f, dp_s, p_t, ds_t, top_s, inv_s, del_s, dqacc,
+    kvin, qbuf, dobuf, kv, xv, xt, xbuf, qs, dos, qsn, dosn, kt, p_f, dp_s, p_t, ds_t, top_s, inv_s, del_s, dqacc,
     dqbuf, part_f, part_b, far_a, far_b, near_m, near_p, gbuf, dkbuf, cosb, sinb, wacc, wb1, r1,
     r2, w_stage, send, recv, loc,
 ):
@@ -44,19 +45,49 @@
     prompt_len = len_ref[0]
     reject_start = len_ref[0] + len_ref[1]
 
-    count = [0, 0]
-    pending = []
-
-    def remote(src, dst, device):
-        i = count[0]
-        count[0] += 1
-        copy = pltpu.make_async_remote_copy(
-            src_ref=src, dst_ref=dst, send_sem=send.at[i], recv_sem=recv.at[i],
+    count = [0, 0, 0]
+
+    def covering(size):
+        if size % 8192:
+            return kv.at[pl.ds(0, size // 256), pl.ds(0, 128)]
+        if size <= 1 << 20:
+            return kv.at[pl.ds(0, size // 512)]
+        return ds_t.at[pl.ds(0, size >> 19)]
+
+    def bytes_of(ref):
+        return math.prod(ref.shape) * ref.dtype.itemsize
+
+    def wait_bytes(sem, size):
+        ref = covering(size)
+        pltpu.make_async_copy(ref, ref, sem).wait()
+
+    class Sends:
+        def __init__(self):
+            self.at = count[2]
+            self.size = 0
+            count[2] += 1
+
+        def wait(self):
+            wait_bytes(send.at[self.at], self.size)
+
+    class Arrivals:
+        def __init__(self):
+            self.at = count[0]
+            self.size = 0
+            count[0] += 1
+
+        def wait_recv(self):
+            wait_bytes(recv.at[self.at], self.size)
+
+    def remote(src, dst, device, sends, arrivals=None):
+        arrivals = arrivals or Arrivals()
+        pltpu.make_async_remote_copy(
+            src_ref=src, dst_ref=dst, send_sem=send.at[sends.at], recv_sem=recv.at[arrivals.at],
             device_id=device, device_id_type=MESH,
-        )
-        copy.start()
-        pending.append(copy)
-        return copy
+        ).start()
+        sends.size += bytes_of(src)
+        arrivals.size += bytes_of(src)
+        return arrivals
 
     def local(src, dst):
         i = count[1]
@@ -88,6 +119,12 @@
                     barrier, 1, device_id=at_owner((zhi + dz) % 4, (w + d) % 4),
                     device_id_type=MESH,
                 )
+    staged = [local(ref, kvin.at[part]) for part, ref in ((0, k_in), (1, v_in))]
+    for ref, stage in ((q_in, p_t), (do_in, ds_t)):
+        for side in range(2):
+            staged.append(
+                local(ref.at[:, pl.ds(1024 * side, 1024)], stage.at[0, pl.ds(128 * side, 128)])
+            )
     x_local = local(x_in, xv)
     kv_slots = (tile(4 * y + w, 64), tile(4 * (7 - y) + 3 - w, 64))
     own_kv = []
@@ -108,33 +145,41 @@
     def row_slots(ww):
         return tile(4 * y + ww, 64), tile(4 * (7 - y) + 3 - ww, 64)
 
+    for copy in staged[:2]:
+        copy.wait()
     kv_first = {}
+    sends_kv = Sends()
     for d in (1, 3, 2):
         ww = (w + d) % 4
-        kv_first[d] = []
+        kv_first[d] = Arrivals()
         for half in range(2):
-            for part, ref in ((0, k_in), (1, v_in)):
-                kv_first[d].append(
-                    remote(
-                        ref.at[pl.ds(64 * half, 64), tile(ww, 128)],
-                        kv.at[kv_slots[half], pl.ds(128 * part, 128)],
-                        at_blk(y, ww),
-                    )
+            for part in range(2):
+                remote(
+                    kvin.at[part, pl.ds(64 * half, 64), tile(ww, 128)],
+                    kv.at[kv_slots[half], pl.ds(128 * part, 128)],
+                    at_blk(y, ww), sends_kv, kv_first[d],
                 )
-    q_first, do_first = [], []
-    for ref, buf, group in ((q_in, qbuf, q_first), (do_in, dobuf, do_first)):
+    for copy in staged[2:]:
+        copy.wait()
+    sends_q, sends_do, q_first, do_first = Sends(), Sends(), Arrivals(), Arrivals()
+    for stage, buf, sends, group in (
+        (p_t, qbuf, sends_q, q_first), (ds_t, dobuf, sends_do, do_first),
+    ):
         for d in (1, 3, 2):
             ww = (w + d) % 4
-            group.append(remote(ref.at[:, tile(ww, 512)], buf.at[w], at_blk(y, ww)))
-
-    kv_plus, kv_minus = ([], []), ([], [])
+            src = stage.at[0, tile(ww // 2, 128), tile(ww % 2, 512)]
+            remote(src, buf.at[w], at_blk(y, ww), sends, group)
+
+    sends_spread, kv_rest = Sends(), Arrivals()
+    kv_plus, kv_minus = [], []
 
     def spread(ww):
         slots = row_slots(ww)
-        for half in range(2):
-            kv_plus[half].append(remote(kv.at[slots[half]], kv.at[slots[half]], at_blk(yp, w)))
-            slot = slots[1 - half]
-            kv_minus[1 - half].append(remote(kv.at[slot], kv.at[slot], at_blk(ym, w)))
+        low, high = kv.at[slots[0]], kv.at[slots[1]]
+        kv_plus.append(remote(low, low, at_blk(yp, w), sends_spread))
+        kv_minus.append(remote(high, high, at_blk(ym, w), sends_spread))
+        remote(high, high, at_blk(yp, w), sends_spread, kv_rest)
+        remote(low, low, at_blk(ym, w), sends_spread, kv_rest)
 
     for copy in own_kv:
         copy.wait()
@@ -152,16 +197,15 @@
     other = tile((w + 2) % 4, 128)
     core_mate = at_blk(y, w + 1 - 2 * core)
     z_mate = at_blk(y, (w + 2) % 4)
-    x_first = []
+    sends_x, sends_first, x_first = Sends(), Sends(), Arrivals()
     for d in (1, 3, 2):
         to = (xx + d) % 4
-        x_first.append(remote(xt.at[to], xbuf.at[:, 4 - d, :, :, column], at_x(to)))
-    x_far = [remote(xt.at[xx], xbuf.at[:, 0, :, :, column], z_mate)]
-    x_mate = [remote(xt.at[xx], xbuf.at[:, 0, :, :, column], core_mate)]
+        remote(xt.at[to], xbuf.at[:, 4 - d, :, :, column], at_x(to), sends_first, x_first)
+    x_far = [remote(xt.at[xx], xbuf.at[:, 0, :, :, column], z_mate, sends_x)]
+    x_mate = [remote(xt.at[xx], xbuf.at[:, 0, :, :, column], core_mate, sends_x)]
 
     for d in (1, 3, 2):
-        for copy in kv_first[d]:
-            copy.wait_recv()
+        kv_first[d].wait_recv()
         spread((w + 4 - d) % 4)
     xbuf[:, 0, :, :, column] = xt[xx]
     lane_row = lax.broadcasted_iota(jnp.int32, (1, HEAD), 1)
@@ -174,21 +218,19 @@
         cosb[half] = jnp.cos(angles)
         sinb[half] = jnp.where(lane_row < 64, jnp.sin(angles), -jnp.sin(angles))
 
-    kv_second = []
+    kv_second = Arrivals()
     for k, d in enumerate((0, 1, 3, 2)):
         ww = (w + 4 - d) % 4
-        kv_plus[0][k].wait_recv()
-        slot = tile(4 * ym + ww, 64)
-        kv_second.append(remote(kv.at[slot], kv.at[slot], at_blk(yp, w)))
-        kv_minus[1][k].wait_recv()
-        slot = tile(4 * (7 - yp) + 3 - ww, 64)
-        kv_second.append(remote(kv.at[slot], kv.at[slot], at_blk(ym, w)))
-    for copy in kv_plus[1] + kv_minus[0]:
-        copy.wait_recv()
+        kv_plus[k].wait_recv()
+        ref = kv.at[tile(4 * ym + ww, 64)]
+        remote(ref, ref, at_blk(yp, w), sends_spread, kv_second)
+        kv_minus[k].wait_recv()
+        ref = kv.at[tile(4 * (7 - yp) + 3 - ww, 64)]
+        remote(ref, ref, at_blk(ym, w), sends_spread, kv_second)
+    kv_rest.wait_recv()
 
     own_q[0].wait()
-    for copy in q_first:
-        copy.wait_recv()
+    q_first.wait_recv()
 
     def stack(buf, stacked):
         def one(c, carry):
@@ -201,8 +243,7 @@
 
     stack(qbuf, qs)
 
-    for copy in kv_second:
-        copy.wait_recv()
+    kv_second.wait_recv()
 
     lane = lax.broadcasted_iota(jnp.int32, (1, 256), 1)
     lane_high = (3 - lane // 64) * 64 + lane % 64
@@ -237,17 +278,8 @@
 
     lax.fori_loop(0, 2, softmax_half, 0)
 
-    order = (2, 1, 3, 0)
-    for copy in x_first:
-        copy.wait_recv()
-    for d in order:
-        ref = xbuf.at[(y + d) % 4, pl.ds(1, 3), :, :, column]
-        x_far.append(remote(ref, ref, z_mate))
-        x_mate.append(remote(ref, ref, core_mate))
-
     own_q[1].wait()
-    for copy in do_first:
-        copy.wait_recv()
+    do_first.wait_recv()
     stack(dobuf, dos)
 
     def weights_half(half, carry):
@@ -276,7 +308,15 @@
             del_s[4 * half + h] = jnp.broadcast_to(delta, (8, 256))
         return carry
 
-    lax.fori_loop(0, 2, weights_half, 0)
+    sends_q.wait()
+    weights_half(0, 0)
+    order = (2, 1, 3, 0)
+    x_first.wait_recv()
+    for d in order:
+        ref = xbuf.at[(y + d) % 4, pl.ds(1, 3), :, :, column]
+        x_far.append(remote(ref, ref, z_mate, sends_x))
+        x_mate.append(remote(ref, ref, core_mate, sends_x))
+    weights_half(1, 0)
 
     def scale_rows(c, carry):
         per_row = jnp.broadcast_to(inv_s[c, pl.ds(0, 1)], (128, 256)).T
@@ -304,8 +344,8 @@
         part_b[part, y2, 0] = low.astype(BF16)
         part_b[part, y2, 1] = high.astype(BF16)
         return (
-            remote(part_b.at[part, y2, 0], far_a.at[part], at_blk(yp, w)),
-            remote(part_b.at[part, y2, 1], far_b.at[part], at_blk(ym, w)),
+            remote(part_b.at[part, y2, 0], far_a.at[part], at_blk(yp, w), sends_sum),
+            remote(part_b.at[part, y2, 1], far_b.at[part], at_blk(ym, w), sends_sum),
         )
 
     def reduce_middle(part, left, right):
@@ -319,11 +359,11 @@
         far[0].wait_recv()
         part_b[part, yp, 0] = (part_f[part, yp, 0] + far_a[part].astype(F32)).astype(BF16)
         part_b[part, yp, 1] = part_f[part, yp, 1].astype(BF16)
-        out.append(remote(part_b.at[part, yp], near_m.at[part], at_blk(yp, w)))
+        out.append(remote(part_b.at[part, yp], near_m.at[part], at_blk(yp, w), sends_sum))
         far[1].wait_recv()
         part_b[part, ym, 0] = part_f[part, ym, 0].astype(BF16)
         part_b[part, ym, 1] = (part_f[part, ym, 1] + far_b[part].astype(F32)).astype(BF16)
-        out.append(remote(part_b.at[part, ym], near_p.at[part], at_blk(ym, w)))
+        out.append(remote(part_b.at[part, ym], near_p.at[part], at_blk(ym, w), sends_sum))
         return out
 
     def reduce_own(part, left, right):
@@ -331,9 +371,11 @@
         part_f[part, y, 0] = low
         part_f[part, y, 1] = high
 
+    sends_sum = Sends()
     far_v = reduce_first(1, p_t, dosn)
     reduce_middle(1, p_t, dosn)
 
+    sends_do.wait()
     def grads_half(half, carry):
         blocks = y + half * (7 - 2 * y) + 1
         deltas = [del_s[4 * half + h, pl.ds(0, 1)] for h in range(4)]
@@ -379,10 +421,6 @@
         return carry
 
     lax.fori_loop(0, 2, query_half, 0)
-    own_out, far_out = [local(dqbuf.at[w], dq_out.at[:, tile(w, 512)])], []
-    for d in (2, 1, 3):
-        ww = (w + d) % 4
-        far_out.append(remote(dqbuf.at[ww], dq_out.at[:, tile(w, 512)], at_blk(y, ww)))
     for copy in near_v:
         copy.wait_recv()
 
@@ -400,18 +438,21 @@
     def gather_near(part):
         lanes = pl.ds(128 * part, 128)
         return [
-            remote(gbuf.at[0, :, lanes], gbuf.at[3, :, lanes], at_x(xp)),
-            remote(gbuf.at[0, :, lanes], gbuf.at[1, :, lanes], at_x(xm)),
+            remote(gbuf.at[0, :, lanes], gbuf.at[3, :, lanes], at_x(xp), sends_g),
+            remote(gbuf.at[0, :, lanes], gbuf.at[1, :, lanes], at_x(xm), sends_g),
         ]
 
     def gather_far(part, near):
         lanes = pl.ds(128 * part, 128)
         low, high = pl.ds(0, 256), pl.ds(256, 256)
         near[0].wait_recv()
-        first = remote(gbuf.at[3, low, lanes], gbuf.at[2, low, lanes], at_x(xp))
+        src, dst = gbuf.at[3, low, lanes], gbuf.at[2, low, lanes]
+        first = remote(src, dst, at_x(xp), sends_g)
         near[1].wait_recv()
-        return [first, remote(gbuf.at[1, high, lanes], gbuf.at[2, high, lanes], at_x(xm))]
-
+        src, dst = gbuf.at[1, high, lanes], gbuf.at[2, high, lanes]
+        return [first, remote(src, dst, at_x(xm), sends_g)]
+
+    sends_g = Sends()
     g_v = gather_near(1)
     x_third = []
 
@@ -421,7 +462,7 @@
             ref = xbuf.at[:, 0, :, :, other]
         else:
             ref = xbuf.at[(y + order[k - 1]) % 4, pl.ds(1, 3), :, :, other]
-        x_third.append(remote(ref, ref, core_mate))
+        x_third.append(remote(ref, ref, core_mate, sends_x))
 
     third_x(0)
     for copy in near_k:
@@ -438,16 +479,6 @@
             dkbuf[ww, pl.ds(64 * half, 64)] = key_grad[at : at + 64]
     g_k = gather_near(0)
     third_x(1)
-    values_out = pl.ds(128, 128)
-    own_out.append(local(dkbuf.at[w], dk_out.at[:, column]))
-    own_out.append(local(gbuf.at[0, tile(w, 128), values_out], dv_out.at[:, column]))
-    for d in (2, 1, 3):
-        ww = (w + d) % 4
-        far_out.append(remote(dkbuf.at[ww], dk_out.at[:, column], at_blk(y, ww)))
-        far_out.append(
-            remote(gbuf.at[0, tile(ww, 128), values_out], dv_out.at[:, column], at_blk(y, ww))
-        )
-
     far_g_v = gather_far(1, g_v)
     third_x(2)
 
@@ -463,40 +494,52 @@
         wacc[part, to] = weights_of(part, to, (0, 1, 3))
 
     def far_tiles(part):
-        out = []
+        out = Arrivals()
         for d in order[:3]:
             to = (y + d) % 4
             wb1[part, to] = (wacc[part, to] + weights_of(part, to, (2,))).astype(BF16)
-            out.append(remote(wb1.at[part, to], r1.at[part, d - 1], at_blk(to, w)))
+            remote(wb1.at[part, to], r1.at[part, d - 1], at_blk(to, w), sends_w, out)
         return out
 
     def owner_sums(part, own, y_sums):
         total = own
-        for copy in y_sums:
-            copy.wait_recv()
+        y_sums.wait_recv()
         for d in range(3):
             total = total + r1[part, d].astype(F32)
         wb1[part, y] = total.astype(BF16)
-        out = []
         for dz in (2, 1, 3, 0):
             zz = (zhi + dz) % 4
             for d in (2, 1, 3, 0):
                 ww = (w + d) % 4
                 piece = pl.ds(pl.multiple_of(64 * zz + 16 * ww, 16), 16)
                 if dz or d:
-                    out.append(
-                        remote(wb1.at[part, y, piece], r2.at[part, zhi, w], at_owner(zz, ww))
+                    remote(
+                        wb1.at[part, y, piece], r2.at[part, zhi, w], at_owner(zz, ww),
+                        sends_last, finals,
                     )
                 else:
                     r2[part, zhi, w] = wb1[part, y, piece]
-        return out
-
+
+    sends_w, sends_last, finals = Sends(), Sends(), Arrivals()
     for k in range(3):
         x_mate[k].wait_recv()
         x_third[k].wait_recv()
     near_tile(1, 2)
     near_tile(1, 1)
     third_x(3)
+    sends_out, far_out = Sends(), Arrivals()
+    values_out = pl.ds(128, 128)
+    own_out = [
+        local(dqbuf.at[w], dq_out.at[:, tile(w, 512)]),
+        local(dkbuf.at[w], dk_out.at[:, column]),
+        local(gbuf.at[0, tile(w, 128), values_out], dv_out.at[:, column]),
+    ]
+    for d in (2, 1, 3):
+        ww = (w + d) % 4
+        values = gbuf.at[0, tile(ww, 128), values_out]
+        remote(dqbuf.at[ww], dq_out.at[:, tile(w, 512)], at_blk(y, ww), sends_out, far_out)
+        remote(dkbuf.at[ww], dk_out.at[:, column], at_blk(y, ww), sends_out, far_out)
+        remote(values, dv_out.at[:, column], at_blk(y, ww), sends_out, far_out)
     far_g_k = gather_far(0, g_k)
     near_tile(0, 2)
     near_tile(0, 1)
@@ -507,18 +550,17 @@
         copy.wait_recv()
     y_sums_v = far_tiles(1)
     near_tile(0, 3)
+    third_x(4)
     for copy in far_g_k:
         copy.wait_recv()
     y_sums_k = far_tiles(0)
-    third_x(4)
     x_mate[4].wait_recv()
     x_third[4].wait_recv()
     own_v = weights_of(1, y, (0, 1, 2, 3))
     wacc[0, y] = weights_of(0, y, (0, 1, 2, 3))
-    finals = owner_sums(1, own_v, y_sums_v)
-    finals = finals + owner_sums(0, wacc[0, y], y_sums_k)
-    for copy in finals:
-        copy.wait_recv()
+    owner_sums(1, own_v, y_sums_v)
+    owner_sums(0, wacc[0, y], y_sums_k)
+    finals.wait_recv()
     for part in range(2):
         for ww in range(4):
             total = r2[part, 0, ww].astype(F32)
@@ -528,10 +570,13 @@
     own_out.append(local(w_stage, w_out))
     for copy in own_out:
         copy.wait()
-    for copy in far_out:
-        copy.wait_recv()
-    for copy in pending:
-        copy.wait_send()
+    far_out.wait_recv()
+    assert count == [ARRIVALS, LOCALS, SENDS], count
+    for sends in (
+        sends_kv, sends_spread, sends_first, sends_x, sends_sum, sends_g, sends_out, sends_w,
+        sends_last,
+    ):
+        sends.wait()
 
 
 def body(queries, keys, values, out_grad, layer_input, lengths):
@@ -548,6 +593,7 @@
         in_specs=[pl.BlockSpec(memory_space=pltpu.SMEM)] + [anywhere] * 5,
         out_specs=(anywhere,) * 4,
         scratch_shapes=[
+            vmem((2, 128, 512), BF16),
             vmem((4, 128, 512), BF16),
             vmem((4, 128, 512), BF16),
             vmem((2048, 256), BF16),
@@ -583,8 +629,8 @@
             vmem((2, 3, 256, 128), BF16),
             vmem((2, 4, 4, 16, 128), BF16),
             vmem((16, 1024), F32),
-            pltpu.SemaphoreType.DMA((COPIES,)),
-            pltpu.SemaphoreType.DMA((COPIES,)),
+            pltpu.SemaphoreType.DMA((SENDS,)),
+            pltpu.SemaphoreType.DMA((ARRIVALS,)),
             pltpu.SemaphoreType.DMA((LOCALS,)),
         ],
         compiler_params=pltpu.CompilerParams(

time: 71.8 us -> 69.4 us (0.967)
  Pallas kernels: 66.6 us -> 64.2 us
    pallas_call x1, Pallas kernels: 66.6 us -> 64.2 us  [body(): pl.pallas_call(kernel, out_shape=(jax.ShapeDtypeStruct((128, 2048), BF16)...]
where the time goes in v6:
time: 69.4 us; the launch traced here: 69.2 us
  Pallas kernels  64.2 us (93%)
  local copies, waits for them, and re-layouts  4.36 us (6%)
    pallas_call x1, Pallas kernels, body(): pl.pallas_call(kernel, out_shape=(jax.ShapeDtypeStruct((128, 2048), BF16)...  64.2 us
    unnamed x10, local copies, waits for them, and re-layouts  4.36 us

profile of v6, /device:TPU:1, one launch (start us, length us, event | category | flops | bytes accessed | tf_op | source)
XLA Modules:
  0.0 69.2 jit_solution(15610433498728093814)
XLA Ops:
  0.6 64.2 %attention_backward.1 = (bf16[128,2048]{1,0:T(8,128)(2,1)}, bf16[128,512]{1,0:T(8,128)(2,1)}, bf16[128,512]{1,0:T(8,128)(2,1)}, f32[16,1024]{1,0:T(8,128)}) custom-call(s32[3]{0:T(128)} %bitcast.17, bf16[128,2048]{1,0:T(8,128)(2,1)} %bitcast.10, bf16[128,2048]{1,0:T(8,128)(2,1)} %bitcast.11, bf16[128,512]{1,0:T(8,128)(2,1)} %bitcast.13, ...), custom_call_target="tpu_custom_call" | custom-call | tf_op jit(solution)/shard_map/attention_backward/pallas_call | solution.py:585
  64.8 0.0 copy-start.1
  64.8 1.9 %copy.14 = bf16[1,128,2048]{2,1,0:T(8,128)(2,1)} copy(bf16[1,128,2048]{2,1,0:T(8,128)(2,1)} %bitcast.12) | data formatting | bytes 1048576
  66.8 0.0 copy-done.1
  66.8 0.0 copy-start
  66.8 0.7 copy.15
  67.4 0.3 copy-done
  67.7 0.0 copy-start.2
  67.7 0.7 copy.16
  68.4 0.2 copy-done.2
  68.6 0.6 copy.17
Async XLA Ops:
  64.8 1.9 %copy-start.1 = (bf16[128,512]{1,0:T(8,128)(2,1)S(1)}, bf16[128,512]{1,0:T(8,128)(2,1)}, u32[]{:S(2)}) copy-start(bf16[128,512]{1,0:T(8,128)(2,1)} %get-tuple-element.9) | copy-start | bytes 393220
  66.8 1.0 %copy-start = (bf16[128,512]{1,0:T(8,128)(2,1)S(1)}, bf16[128,512]{1,0:T(8,128)(2,1)}, u32[]{:S(2)}) copy-start(bf16[128,512]{1,0:T(8,128)(2,1)} %get-tuple-element.10) | copy-start | bytes 393220
  67.7 0.9 %copy-start.2 = (f32[16,1024]{1,0:T(8,128)S(1)}, f32[16,1024]{1,0:T(8,128)}, u32[]{:S(2)}) copy-start(f32[16,1024]{1,0:T(8,128)} %get-tuple-element.19) | copy-start | bytes 196612

commit v7 on v6

--- a/solution.py
+++ b/solution.py
@@ -15,7 +15,7 @@
 MASKED = -1e30
 FAR = 1 << 20
 SENDS = 11
-ARRIVALS = 51
+ARRIVALS = 52
 LOCALS = 17
 
 
@@ -161,14 +161,18 @@
                 )
     for copy in staged[2:]:
         copy.wait()
-    sends_q, sends_do, q_first, do_first = Sends(), Sends(), Arrivals(), Arrivals()
-    for stage, buf, sends, group in (
-        (p_t, qbuf, sends_q, q_first), (ds_t, dobuf, sends_do, do_first),
-    ):
+    sends_q, sends_do, q_first = Sends(), Sends(), Arrivals()
+    for d in (1, 3, 2):
+        ww = (w + d) % 4
+        src = p_t.at[0, tile(ww // 2, 128), tile(ww % 2, 512)]
+        remote(src, qbuf.at[w], at_blk(y, ww), sends_q, q_first)
+    do_first = {1: Arrivals(), 0: Arrivals()}
+    for half in (1, 0):
         for d in (1, 3, 2):
             ww = (w + d) % 4
-            src = stage.at[0, tile(ww // 2, 128), tile(ww % 2, 512)]
-            remote(src, buf.at[w], at_blk(y, ww), sends, group)
+            src = ds_t.at[0, tile(2 * (ww // 2) + half, 64), tile(ww % 2, 512)]
+            dst = dobuf.at[w, pl.ds(64 * half, 64)]
+            remote(src, dst, at_blk(y, ww), sends_do, do_first[half])
 
     sends_spread, kv_rest = Sends(), Arrivals()
     kv_plus, kv_minus = [], []
@@ -194,20 +198,20 @@
 
     lax.fori_loop(0, 32, transpose_x, 0)
     column = tile(w, 128)
-    other = tile((w + 2) % 4, 128)
+    w_other = (w + 2) % 4
     core_mate = at_blk(y, w + 1 - 2 * core)
     z_mate = at_blk(y, (w + 2) % 4)
     sends_x, sends_first, x_first = Sends(), Sends(), Arrivals()
     for d in (1, 3, 2):
         to = (xx + d) % 4
-        remote(xt.at[to], xbuf.at[:, 4 - d, :, :, column], at_x(to), sends_first, x_first)
-    x_far = [remote(xt.at[xx], xbuf.at[:, 0, :, :, column], z_mate, sends_x)]
-    x_mate = [remote(xt.at[xx], xbuf.at[:, 0, :, :, column], core_mate, sends_x)]
+        remote(xt.at[to], xbuf.at[:, 4 - d, w], at_x(to), sends_first, x_first)
+    x_far = [remote(xt.at[xx], xbuf.at[:, 0, w], z_mate, sends_x)]
+    x_mate = [remote(xt.at[xx], xbuf.at[:, 0, w], core_mate, sends_x)]
 
     for d in (1, 3, 2):
         kv_first[d].wait_recv()
         spread((w + 4 - d) % 4)
-    xbuf[:, 0, :, :, column] = xt[xx]
+    xbuf[:, 0, w] = xt[xx]
     lane_row = lax.broadcasted_iota(jnp.int32, (1, HEAD), 1)
     frequency = jnp.exp(
         -(2.0 * (lane_row % 64).astype(F32) / HEAD) * math.log(ROPE_BASE)
@@ -232,59 +236,72 @@
     own_q[0].wait()
     q_first.wait_recv()
 
-    def stack(buf, stacked):
-        def one(c, carry):
-            half, h = c // 4, c % 4
-            for ww in range(4):
-                stacked[c, pl.ds(64 * ww, 64)] = buf[ww, tile(half, 64), tile(h, 128)]
-            return carry
-
-        lax.fori_loop(0, 8, one, 0, unroll=True)
-
-    stack(qbuf, qs)
-
-    kv_second.wait_recv()
+    def stack(buf, stacked, halves):
+        for half in halves:
+            for h in range(4):
+                for ww in range(4):
+                    piece = buf[ww, pl.ds(64 * half, 64), pl.ds(128 * h, 128)]
+                    stacked[4 * half + h, pl.ds(64 * ww, 64)] = piece
+
+    stack(qbuf, qs, (0, 1))
 
     lane = lax.broadcasted_iota(jnp.int32, (1, 256), 1)
     lane_high = (3 - lane // 64) * 64 + lane % 64
     rows = lax.broadcasted_iota(jnp.int32, (256, 256), 0)
     zero = jnp.zeros((8, 256), F32)
 
-    def softmax_half(half, carry):
+    def score_block(half, j):
         diagonal = y + half * (7 - 2 * y)
-        blocks = diagonal + 1
         query_pos = 256 * diagonal + lane + half * (lane_high - lane)
         rejected = query_pos >= reject_start
-
-        def scores(j, tops):
-            key_pos = 256 * j + rows
-            chosen = jnp.logical_and(key_pos >= prompt_len, key_pos < reject_start)
-            shown = jnp.where(rejected, jnp.where(chosen, FAR, key_pos), key_pos)
-            bias = jnp.where(shown <= query_pos, 0.0, MASKED)
-            key = kv[tile(j, 256), pl.ds(0, 128)]
-            out = []
-            for h in range(4):
-                s = nt(key, qs[4 * half + h]) + bias
-                p_f[4 * half + j, h] = s
-                out.append(jnp.maximum(tops[h], jnp.max(s.reshape(32, 8, 256), axis=0)))
-            return tuple(out)
-
+        key_pos = 256 * j + rows
+        chosen = jnp.logical_and(key_pos >= prompt_len, key_pos < reject_start)
+        shown = jnp.where(rejected, jnp.where(chosen, FAR, key_pos), key_pos)
+        bias = jnp.where(shown <= query_pos, 0.0, MASKED)
+        key = kv[tile(j, 256), pl.ds(0, 128)]
+        out = []
+        for h in range(4):
+            s = nt(key, qs[4 * half + h]) + bias
+            p_f[4 * half + j, h] = s
+            out.append(jnp.max(s.reshape(32, 8, 256), axis=0))
+        return out
+
+    last_high = (5 - y) // 4
+
+    def scores_half(half, carry):
+        def scores(t, tops):
+            j = t + (t - y2 + 8) // 8
+            j = j + (j - (7 - y2) + 8) // 8
+            new = score_block(half, j)
+            return tuple(jnp.maximum(tops[h], new[h]) for h in range(4))
+
+        blocks = half * (7 - y - last_high) + (1 - half) * (y + last_high)
         tops = lax.fori_loop(0, blocks, scores, (jnp.full((8, 256), MASKED, F32),) * 4)
         for h in range(4):
-            top_s[4 * half + h] = jnp.broadcast_to(
-                jnp.max(tops[h], axis=0, keepdims=True), (8, 256)
-            )
+            top_s[4 * half + h] = tops[h]
         return carry
 
-    lax.fori_loop(0, 2, softmax_half, 0)
+    lax.fori_loop(0, 2, scores_half, 0)
+    kv_second.wait_recv()
+
+    def last_block(i, carry):
+        half = i * last_high + (1 - i)
+        j = half * i * (7 - y2) + (1 - half * i) * y2
+        new = score_block(half, j)
+        for h in range(4):
+            top_s[4 * half + h] = jnp.maximum(top_s[4 * half + h], new[h])
+        return carry
+
+    lax.fori_loop(0, 2, last_block, 0)
 
     own_q[1].wait()
-    do_first.wait_recv()
-    stack(dobuf, dos)
+    sends_q.wait()
+    do_first[1].wait_recv()
+    stack(dobuf, dos, (1,))
 
     def weights_half(half, carry):
         blocks = y + half * (7 - 2 * y) + 1
-        tops = [top_s[4 * half + h, pl.ds(0, 1)] for h in range(4)]
+        tops = [jnp.max(top_s[4 * half + h], axis=0, keepdims=True) for h in range(4)]
 
         def weights(j, sums):
             value = kv[tile(j, 256), pl.ds(128, 128)]
@@ -308,15 +325,16 @@
             del_s[4 * half + h] = jnp.broadcast_to(delta, (8, 256))
         return carry
 
-    sends_q.wait()
-    weights_half(0, 0)
+    weights_half(1, 0)
     order = (2, 1, 3, 0)
     x_first.wait_recv()
     for d in order:
-        ref = xbuf.at[(y + d) % 4, pl.ds(1, 3), :, :, column]
+        ref = xbuf.at[(y + d) % 4, pl.ds(1, 3), w]
         x_far.append(remote(ref, ref, z_mate, sends_x))
         x_mate.append(remote(ref, ref, core_mate, sends_x))
-    weights_half(1, 0)
+    do_first[0].wait_recv()
+    stack(dobuf, dos, (0,))
+    weights_half(0, 0)
 
     def scale_rows(c, carry):
         per_row = jnp.broadcast_to(inv_s[c, pl.ds(0, 1)], (128, 256)).T
@@ -459,9 +477,9 @@
     def third_x(k):
         x_far[k].wait_recv()
         if k == 0:
-            ref = xbuf.at[:, 0, :, :, other]
+            ref = xbuf.at[:, 0, w_other]
         else:
-            ref = xbuf.at[(y + order[k - 1]) % 4, pl.ds(1, 3), :, :, other]
+            ref = xbuf.at[(y + order[k - 1]) % 4, pl.ds(1, 3), w_other]
         x_third.append(remote(ref, ref, core_mate, sends_x))
 
     third_x(0)
@@ -484,9 +502,11 @@
 
     def weights_of(part, to, rels):
         lanes = pl.ds(128 * part, 128)
-        total = nn(xbuf[to, rels[0]].reshape(256, 512), gbuf[rels[0], :, lanes])
-        for rel in rels[1:]:
-            total = total + nn(xbuf[to, rel].reshape(256, 512), gbuf[rel, :, lanes])
+        total = None
+        for rel in rels:
+            left = [xbuf[to, rel, ww].reshape(256, 128) for ww in range(4)]
+            term = nn(jnp.concatenate(left, axis=1), gbuf[rel, :, lanes])
+            total = term if total is None else total + term
         return total
 
     def near_tile(part, d):
@@ -579,17 +599,36 @@
         sends.wait()
 
 
+def place(*refs):
+    sources, targets, stages, sem_in, sem_out = refs[:4], refs[4:8], refs[8:12], *refs[12:]
+    parts = []
+    for source, target, stage in zip(sources, targets, stages, strict=True):
+        for side in range(4 if source.shape[1] == 2048 else 1):
+            at = pl.ds(side * 32, 32) if source.shape[1] == 2048 else slice(None)
+            i = len(parts)
+            arrive = pltpu.make_async_copy(source.at[at], stage.at[at], sem_in.at[i])
+            arrive.start()
+            leave = pltpu.make_async_copy(stage.at[at], target.at[at], sem_out.at[i])
+            parts.append((arrive, leave))
+    for arrive, leave in parts:
+        arrive.wait()
+        leave.start()
+    for _, leave in parts:
+        leave.wait()
+
+
 def body(queries, keys, values, out_grad, layer_input, lengths):
     anywhere = pl.BlockSpec(memory_space=pltpu.HBM)
     vmem = pltpu.VMEM
+    shapes = (
+        jax.ShapeDtypeStruct((128, 2048), BF16),
+        jax.ShapeDtypeStruct((128, 512), BF16),
+        jax.ShapeDtypeStruct((128, 512), BF16),
+        jax.ShapeDtypeStruct((16, 1024), F32),
+    )
     outs = pl.pallas_call(
         kernel,
-        out_shape=(
-            jax.ShapeDtypeStruct((128, 2048), BF16),
-            jax.ShapeDtypeStruct((128, 512), BF16),
-            jax.ShapeDtypeStruct((128, 512), BF16),
-            jax.ShapeDtypeStruct((16, 1024), F32),
-        ),
+        out_shape=shapes,
         in_specs=[pl.BlockSpec(memory_space=pltpu.SMEM)] + [anywhere] * 5,
         out_specs=(anywhere,) * 4,
         scratch_shapes=[
@@ -599,7 +638,7 @@
             vmem((2048, 256), BF16),
             vmem((128, 4096), BF16),
             vmem((4, 4, 4, 64, 128), BF16),
-            vmem((4, 4, 4, 64, 512), BF16),
+            vmem((4, 4, 4, 4, 64, 128), BF16),
             vmem((8, 256, 128), BF16),
             vmem((8, 256, 128), BF16),
             vmem((8, 256, 128), BF16),
@@ -638,6 +677,15 @@
         ),
         name="attention_backward",
     )(lengths[0], queries[0], out_grad[0], keys[0], values[0], layer_input[0])
+    outs = pl.pallas_call(
+        place,
+        out_shape=shapes,
+        in_specs=[anywhere] * 4,
+        out_specs=(anywhere,) * 4,
+        scratch_shapes=[vmem(shape.shape, shape.dtype) for shape in shapes]
+        + [pltpu.SemaphoreType.DMA((7,)), pltpu.SemaphoreType.DMA((7,))],
+        name="place_outputs",
+    )(*outs)
     return (outs[0][None], outs[1][None], outs[2][None], outs[3])
 
 

time: 69.4 us -> 65.1 us (0.938)
  local copies, waits for them, and re-layouts: 4.36 us -> 0 us
    unnamed x10 -> x0, local copies, waits for them, and re-layouts: 4.36 us -> none
    pallas_call x1 -> x2, Pallas kernels: 64.2 us -> 64.3 us  [the longest x1 62.3 us: body(): pl.pallas_call(kernel, out_shape=shapes, in_specs=[pl.BlockSpec(memory_sp...]
where the time goes in v7:
time: 65.1 us; the launch traced here: 64.9 us
  Pallas kernels  64.3 us (99%)
    pallas_call x1, Pallas kernels, body(): pl.pallas_call(kernel, out_shape=shapes, in_specs=[pl.BlockSpec(memory_sp...  62.3 us
    pallas_call x1, Pallas kernels, body(): pl.pallas_call(place, out_shape=shapes, in_specs=[anywhere] * 4, out_spec...  2 us

profile of v7, /device:TPU:1, one launch (start us, length us, event | category | flops | bytes accessed | tf_op | source)
XLA Modules:
  0.0 64.9 jit_solution(13009714130977583231)
XLA Ops:
  0.6 62.3 %attention_backward.1 = (bf16[128,2048]{1,0:T(8,128)(2,1)}, bf16[128,512]{1,0:T(8,128)(2,1)}, bf16[128,512]{1,0:T(8,128)(2,1)}, f32[16,1024]{1,0:T(8,128)}) custom-call(s32[3]{0:T(128)} %bitcast.14, bf16[128,2048]{1,0:T(8,128)(2,1)} %bitcast.10, bf16[128,2048]{1,0:T(8,128)(2,1)} %bitcast.11, bf16[128,512]{1,0:T(8,128)(2,1)} %bitcast.12, ...), custom_call_target="tpu_custom_call" | custom-call | tf_op jit(solution)/shard_map/attention_backward/pallas_call | solution.py:629
  62.9 2.0 %place_outputs.1 = (bf16[128,2048]{1,0:T(8,128)(2,1)}, bf16[128,512]{1,0:T(8,128)(2,1)}, bf16[128,512]{1,0:T(8,128)(2,1)}, f32[16,1024]{1,0:T(8,128)}) custom-call(bf16[128,2048]{1,0:T(8,128)(2,1)} %get-tuple-element.12.refs_0_, bf16[128,512]{1,0:T(8,128)(2,1)} %get-tuple-element.13.refs_1_, bf16[128,512]{1,0:T(8,128)(2,1)} %get-tuple-element.14.refs_2_, ...), custom_call_target="tpu_custom_call" | custom-call | tf_op jit(solution)/shard_map/place_outputs/pallas_call | solution.py:680

commit v8 on v7

--- a/solution.py
+++ b/solution.py
@@ -439,6 +439,12 @@
         return carry
 
     lax.fori_loop(0, 2, query_half, 0)
+    sends_out, far_out = Sends(), Arrivals()
+    own_out = [local(dqbuf.at[w], dq_out.at[:, tile(w, 512)])]
+    for d in (2, 1, 3):
+        ww = (w + d) % 4
+        dst = dq_out.at[:, tile(w, 512)]
+        remote(dqbuf.at[ww], dst, at_blk(y, ww), sends_out, far_out)
     for copy in near_v:
         copy.wait_recv()
 
@@ -453,22 +459,25 @@
             rows_at = pl.ds(128 * ww + 64 * half, 64)
             gbuf[0, rows_at, pl.ds(128, 128)] = value_grad[at : at + 64]
 
+    low_rows, high_rows = pl.ds(0, 256), pl.ds(256, 256)
+
     def gather_near(part):
         lanes = pl.ds(128 * part, 128)
-        return [
-            remote(gbuf.at[0, :, lanes], gbuf.at[3, :, lanes], at_x(xp), sends_g),
-            remote(gbuf.at[0, :, lanes], gbuf.at[1, :, lanes], at_x(xm), sends_g),
-        ]
+        low, high = gbuf.at[0, low_rows, lanes], gbuf.at[0, high_rows, lanes]
+        plus = remote(low, gbuf.at[3, low_rows, lanes], at_x(xp), sends_g)
+        minus = remote(high, gbuf.at[1, high_rows, lanes], at_x(xm), sends_g)
+        rest = remote(high, gbuf.at[3, high_rows, lanes], at_x(xp), sends_g)
+        remote(low, gbuf.at[1, low_rows, lanes], at_x(xm), sends_g, rest)
+        return plus, minus, rest
 
     def gather_far(part, near):
         lanes = pl.ds(128 * part, 128)
-        low, high = pl.ds(0, 256), pl.ds(256, 256)
         near[0].wait_recv()
-        src, dst = gbuf.at[3, low, lanes], gbuf.at[2, low, lanes]
-        first = remote(src, dst, at_x(xp), sends_g)
+        src, dst = gbuf.at[3, low_rows, lanes], gbuf.at[2, low_rows, lanes]
+        far = remote(src, dst, at_x(xp), sends_g)
         near[1].wait_recv()
-        src, dst = gbuf.at[1, high, lanes], gbuf.at[2, high, lanes]
-        return [first, remote(src, dst, at_x(xm), sends_g)]
+        src, dst = gbuf.at[1, high_rows, lanes], gbuf.at[2, high_rows, lanes]
+        return remote(src, dst, at_x(xm), sends_g, far)
 
     sends_g = Sends()
     g_v = gather_near(1)
@@ -483,6 +492,7 @@
         x_third.append(remote(ref, ref, core_mate, sends_x))
 
     third_x(0)
+    third_x(1)
     for copy in near_k:
         copy.wait_recv()
     for half in range(2):
@@ -496,7 +506,14 @@
             gbuf[0, pl.ds(128 * ww + 64 * half, 64), pl.ds(0, 128)] = key_pre[at : at + 64]
             dkbuf[ww, pl.ds(64 * half, 64)] = key_grad[at : at + 64]
     g_k = gather_near(0)
-    third_x(1)
+    values_out = pl.ds(128, 128)
+    own_out.append(local(dkbuf.at[w], dk_out.at[:, column]))
+    own_out.append(local(gbuf.at[0, tile(w, 128), values_out], dv_out.at[:, column]))
+    for d in (2, 1, 3):
+        ww = (w + d) % 4
+        values = gbuf.at[0, tile(ww, 128), values_out]
+        remote(dkbuf.at[ww], dk_out.at[:, column], at_blk(y, ww), sends_out, far_out)
+        remote(values, dv_out.at[:, column], at_blk(y, ww), sends_out, far_out)
     far_g_v = gather_far(1, g_v)
     third_x(2)
 
@@ -513,13 +530,11 @@
         to = (y + d) % 4
         wacc[part, to] = weights_of(part, to, (0, 1, 3))
 
-    def far_tiles(part):
-        out = Arrivals()
-        for d in order[:3]:
-            to = (y + d) % 4
-            wb1[part, to] = (wacc[part, to] + weights_of(part, to, (2,))).astype(BF16)
-            remote(wb1.at[part, to], r1.at[part, d - 1], at_blk(to, w), sends_w, out)
-        return out
+    def far_tile(part, d, arrivals=None):
+        to = (y + d) % 4
+        wb1[part, to] = (wacc[part, to] + weights_of(part, to, (2,))).astype(BF16)
+        dst = r1.at[part, d - 1]
+        return remote(wb1.at[part, to], dst, at_blk(to, w), sends_w, arrivals)
 
     def owner_sums(part, own, y_sums):
         total = own
@@ -541,39 +556,33 @@
                     r2[part, zhi, w] = wb1[part, y, piece]
 
     sends_w, sends_last, finals = Sends(), Sends(), Arrivals()
-    for k in range(3):
+    def wait_x(k):
         x_mate[k].wait_recv()
         x_third[k].wait_recv()
+
+    wait_x(0)
+    wait_x(1)
+    g_v[2].wait_recv()
     near_tile(1, 2)
+    far_g_k = gather_far(0, g_k)
+    g_k[2].wait_recv()
+    near_tile(0, 2)
+    third_x(3)
+    wait_x(2)
     near_tile(1, 1)
-    third_x(3)
-    sends_out, far_out = Sends(), Arrivals()
-    values_out = pl.ds(128, 128)
-    own_out = [
-        local(dqbuf.at[w], dq_out.at[:, tile(w, 512)]),
-        local(dkbuf.at[w], dk_out.at[:, column]),
-        local(gbuf.at[0, tile(w, 128), values_out], dv_out.at[:, column]),
-    ]
-    for d in (2, 1, 3):
-        ww = (w + d) % 4
-        values = gbuf.at[0, tile(ww, 128), values_out]
-        remote(dqbuf.at[ww], dq_out.at[:, tile(w, 512)], at_blk(y, ww), sends_out, far_out)
-        remote(dkbuf.at[ww], dk_out.at[:, column], at_blk(y, ww), sends_out, far_out)
-        remote(values, dv_out.at[:, column], at_blk(y, ww), sends_out, far_out)
-    far_g_k = gather_far(0, g_k)
-    near_tile(0, 2)
     near_tile(0, 1)
-    x_mate[3].wait_recv()
-    x_third[3].wait_recv()
+    far_g_v.wait_recv()
+    y_sums_v = far_tile(1, 2)
+    far_tile(1, 1, y_sums_v)
+    wait_x(3)
     near_tile(1, 3)
-    for copy in far_g_v:
-        copy.wait_recv()
-    y_sums_v = far_tiles(1)
+    far_tile(1, 3, y_sums_v)
     near_tile(0, 3)
     third_x(4)
-    for copy in far_g_k:
-        copy.wait_recv()
-    y_sums_k = far_tiles(0)
+    far_g_k.wait_recv()
+    y_sums_k = far_tile(0, 2)
+    far_tile(0, 1, y_sums_k)
+    far_tile(0, 3, y_sums_k)
     x_mate[4].wait_recv()
     x_third[4].wait_recv()
     own_v = weights_of(1, y, (0, 1, 2, 3))

time: 65.1 us -> 64.8 us (level)
  no operation moved by 1% of the time
where the time goes in v8:
time: 64.8 us; the launch traced here: 64.7 us
  Pallas kernels  64 us (99%)
    pallas_call x1, Pallas kernels, body(): pl.pallas_call(kernel, out_shape=shapes, in_specs=[pl.BlockSpec(memory_sp...  62 us
    pallas_call x1, Pallas kernels, body(): pl.pallas_call(place, out_shape=shapes, in_specs=[anywhere] * 4, out_spec...  2 us

profile of v8, /device:TPU:1, one launch (start us, length us, event | category | flops | bytes accessed | tf_op | source)
XLA Modules:
  0.0 64.7 jit_solution(12748712848800020015)
XLA Ops:
  0.6 62.0 %attention_backward.1 = (bf16[128,2048]{1,0:T(8,128)(2,1)}, bf16[128,512]{1,0:T(8,128)(2,1)}, bf16[128,512]{1,0:T(8,128)(2,1)}, f32[16,1024]{1,0:T(8,128)}) custom-call(s32[3]{0:T(128)} %bitcast.14, bf16[128,2048]{1,0:T(8,128)(2,1)} %bitcast.10, bf16[128,2048]{1,0:T(8,128)(2,1)} %bitcast.11, bf16[128,512]{1,0:T(8,128)(2,1)} %bitcast.12, ...), custom_call_target="tpu_custom_call" | custom-call | tf_op jit(solution)/shard_map/attention_backward/pallas_call | solution.py:638
  62.7 2.0 %place_outputs.1 = (bf16[128,2048]{1,0:T(8,128)(2,1)}, bf16[128,512]{1,0:T(8,128)(2,1)}, bf16[128,512]{1,0:T(8,128)(2,1)}, f32[16,1024]{1,0:T(8,128)}) custom-call(bf16[128,2048]{1,0:T(8,128)(2,1)} %get-tuple-element.12.refs_0_, bf16[128,512]{1,0:T(8,128)(2,1)} %get-tuple-element.13.refs_1_, bf16[128,512]{1,0:T(8,128)(2,1)} %get-tuple-element.14.refs_2_, ...), custom_call_target="tpu_custom_call" | custom-call | tf_op jit(solution)/shard_map/place_outputs/pallas_call | solution.py:689

commit v9 on v8

--- a/solution.py
+++ b/solution.py
@@ -16,7 +16,7 @@
 FAR = 1 << 20
 SENDS = 11
 ARRIVALS = 52
-LOCALS = 17
+LOCALS = 18
 
 
 def nn(a, b):
@@ -29,10 +29,10 @@
 
 def kernel(
     len_ref, q_in, do_in, k_in, v_in, x_in,
-    dq_out, dk_out, dv_out, w_out,
+    dq_out, dk_out, dv_out, r2,
     kvin, qbuf, dobuf, kv, xv, xt, xbuf, qs, dos, qsn, dosn, kt, p_f, dp_s, p_t, ds_t, top_s, inv_s, del_s, dqacc,
     dqbuf, part_f, part_b, far_a, far_b, near_m, near_p, gbuf, dkbuf, cosb, sinb, wacc, wb1, r1,
-    r2, w_stage, send, recv, loc,
+    send, recv, loc,
 ):
     b = lax.axis_index("blk")
     dp = lax.axis_index("dp")
@@ -553,7 +553,7 @@
                         sends_last, finals,
                     )
                 else:
-                    r2[part, zhi, w] = wb1[part, y, piece]
+                    own_out.append(local(wb1.at[part, y, piece], r2.at[part, zhi, w]))
 
     sends_w, sends_last, finals = Sends(), Sends(), Arrivals()
     def wait_x(k):
@@ -590,13 +590,6 @@
     owner_sums(1, own_v, y_sums_v)
     owner_sums(0, wacc[0, y], y_sums_k)
     finals.wait_recv()
-    for part in range(2):
-        for ww in range(4):
-            total = r2[part, 0, ww].astype(F32)
-            for zz in range(1, 4):
-                total = total + r2[part, zz, ww].astype(F32)
-            w_stage[:, pl.ds(512 * part + 128 * ww, 128)] = total
-    own_out.append(local(w_stage, w_out))
     for copy in own_out:
         copy.wait()
     far_out.wait_recv()
@@ -609,9 +602,12 @@
 
 
 def place(*refs):
-    sources, targets, stages, sem_in, sem_out = refs[:4], refs[4:8], refs[8:12], *refs[12:]
+    sources, targets, stages = refs[:4], refs[4:8], refs[8:12]
+    w_stage, sem_in, sem_out = refs[12:]
+    pieces = pltpu.make_async_copy(sources[3], stages[3], sem_in.at[6])
+    pieces.start()
     parts = []
-    for source, target, stage in zip(sources, targets, stages, strict=True):
+    for source, target, stage in zip(sources[:3], targets[:3], stages[:3], strict=True):
         for side in range(4 if source.shape[1] == 2048 else 1):
             at = pl.ds(side * 32, 32) if source.shape[1] == 2048 else slice(None)
             i = len(parts)
@@ -619,11 +615,21 @@
             arrive.start()
             leave = pltpu.make_async_copy(stage.at[at], target.at[at], sem_out.at[i])
             parts.append((arrive, leave))
+    pieces.wait()
+    for part in range(2):
+        for ww in range(4):
+            total = stages[3][part, 0, ww].astype(F32)
+            for zz in range(1, 4):
+                total = total + stages[3][part, zz, ww].astype(F32)
+            w_stage[:, pl.ds(512 * part + 128 * ww, 128)] = total
+    last = pltpu.make_async_copy(w_stage, targets[3], sem_out.at[6])
+    last.start()
     for arrive, leave in parts:
         arrive.wait()
         leave.start()
     for _, leave in parts:
         leave.wait()
+    last.wait()
 
 
 def body(queries, keys, values, out_grad, layer_input, lengths):
@@ -633,8 +639,9 @@
         jax.ShapeDtypeStruct((128, 2048), BF16),
         jax.ShapeDtypeStruct((128, 512), BF16),
         jax.ShapeDtypeStruct((128, 512), BF16),
-        jax.ShapeDtypeStruct((16, 1024), F32),
+        jax.ShapeDtypeStruct((2, 4, 4, 16, 128), BF16),
     )
+    weight = jax.ShapeDtypeStruct((16, 1024), F32)
     outs = pl.pallas_call(
         kernel,
         out_shape=shapes,
@@ -675,8 +682,6 @@
             vmem((2, 4, 256, 128), F32),
             vmem((2, 4, 256, 128), BF16),
             vmem((2, 3, 256, 128), BF16),
-            vmem((2, 4, 4, 16, 128), BF16),
-            vmem((16, 1024), F32),
             pltpu.SemaphoreType.DMA((SENDS,)),
             pltpu.SemaphoreType.DMA((ARRIVALS,)),
             pltpu.SemaphoreType.DMA((LOCALS,)),
@@ -688,11 +693,11 @@
     )(lengths[0], queries[0], out_grad[0], keys[0], values[0], layer_input[0])
     outs = pl.pallas_call(
         place,
-        out_shape=shapes,
+        out_shape=(*shapes[:3], weight),
         in_specs=[anywhere] * 4,
         out_specs=(anywhere,) * 4,
         scratch_shapes=[vmem(shape.shape, shape.dtype) for shape in shapes]
-        + [pltpu.SemaphoreType.DMA((7,)), pltpu.SemaphoreType.DMA((7,))],
+        + [vmem((16, 1024), F32), pltpu.SemaphoreType.DMA((7,)), pltpu.SemaphoreType.DMA((7,))],
         name="place_outputs",
     )(*outs)
     return (outs[0][None], outs[1][None], outs[2][None], outs[3])

time: 64.8 us -> 64.3 us (level)
  no operation moved by 1% of the time
where the time goes in v9:
time: 64.3 us; the launch traced here: 64.2 us
  Pallas kernels  63.6 us (99%)
    pallas_call x1, Pallas kernels, body(): pl.pallas_call(kernel, out_shape=shapes, in_specs=[pl.BlockSpec(memory_sp...  61.5 us
    pallas_call x1, Pallas kernels, body(): pl.pallas_call(place, out_shape=(*shapes[:3], weight), in_specs=[anywhere...  2.03 us

profile of v9, /device:TPU:1, one launch (start us, length us, event | category | flops | bytes accessed | tf_op | source)
XLA Modules:
  0.0 64.2 jit_solution(15284078147061385276)
XLA Ops:
  0.6 61.5 %attention_backward.1 = (bf16[128,2048]{1,0:T(8,128)(2,1)}, bf16[128,512]{1,0:T(8,128)(2,1)}, bf16[128,512]{1,0:T(8,128)(2,1)}, bf16[2,4,4,16,128]{4,3,2,1,0:T(8,128)(2,1)}) custom-call(s32[3]{0:T(128)} %bitcast.14, bf16[128,2048]{1,0:T(8,128)(2,1)} %bitcast.10, bf16[128,2048]{1,0:T(8,128)(2,1)} %bitcast.11, bf16[128,512]{1,0:T(8,128)(2,1)} %bitcast.12, ...), custom_call_target="tpu_custom_call" | custom-call | tf_op jit(solution)/shard_map/attention_backward/pallas_call | solution.py:645
  62.2 2.0 %place_outputs.1 = (bf16[128,2048]{1,0:T(8,128)(2,1)}, bf16[128,512]{1,0:T(8,128)(2,1)}, bf16[128,512]{1,0:T(8,128)(2,1)}, f32[16,1024]{1,0:T(8,128)}) custom-call(bf16[128,2048]{1,0:T(8,128)(2,1)} %get-tuple-element.12.refs_0_, bf16[128,512]{1,0:T(8,128)(2,1)} %get-tuple-element.13.refs_1_, bf16[128,512]{1,0:T(8,128)(2,1)} %get-tuple-element.14.refs_2_, ...), custom_call_target="tpu_custom_call" | custom-call | tf_op jit(solution)/shard_map/place_outputs/pallas_call | solution.py:694

commit v10 on v9

--- a/solution.py
+++ b/solution.py
@@ -326,16 +326,16 @@
         return carry
 
     weights_half(1, 0)
+    do_first[0].wait_recv()
+    stack(dobuf, dos, (0,))
+    weights_half(0, 0)
+
     order = (2, 1, 3, 0)
     x_first.wait_recv()
     for d in order:
         ref = xbuf.at[(y + d) % 4, pl.ds(1, 3), w]
         x_far.append(remote(ref, ref, z_mate, sends_x))
         x_mate.append(remote(ref, ref, core_mate, sends_x))
-    do_first[0].wait_recv()
-    stack(dobuf, dos, (0,))
-    weights_half(0, 0)
-
     def scale_rows(c, carry):
         per_row = jnp.broadcast_to(inv_s[c, pl.ds(0, 1)], (128, 256)).T
         dosn[c] = (dos[c].astype(F32) * per_row).astype(BF16)

time: 64.3 us -> 64.3 us (level)
  no operation moved by 1% of the time
where the time goes in v10:
time: 64.3 us; the launch traced here: 64.1 us
  Pallas kernels  63.5 us (99%)
    pallas_call x1, Pallas kernels, body(): pl.pallas_call(kernel, out_shape=shapes, in_specs=[pl.BlockSpec(memory_sp...  61.4 us
    pallas_call x1, Pallas kernels, body(): pl.pallas_call(place, out_shape=(*shapes[:3], weight), in_specs=[anywhere...  2.03 us

profile of v10, /device:TPU:1, one launch (start us, length us, event | category | flops | bytes accessed | tf_op | source)
XLA Modules:
  0.0 64.1 jit_solution(7291875280867048934)
XLA Ops:
  0.6 61.4 %attention_backward.1 = (bf16[128,2048]{1,0:T(8,128)(2,1)}, bf16[128,512]{1,0:T(8,128)(2,1)}, bf16[128,512]{1,0:T(8,128)(2,1)}, bf16[2,4,4,16,128]{4,3,2,1,0:T(8,128)(2,1)}) custom-call(s32[3]{0:T(128)} %bitcast.14, bf16[128,2048]{1,0:T(8,128)(2,1)} %bitcast.10, bf16[128,2048]{1,0:T(8,128)(2,1)} %bitcast.11, bf16[128,512]{1,0:T(8,128)(2,1)} %bitcast.12, ...), custom_call_target="tpu_custom_call" | custom-call | tf_op jit(solution)/shard_map/attention_backward/pallas_call | solution.py:645
  62.1 2.0 %place_outputs.1 = (bf16[128,2048]{1,0:T(8,128)(2,1)}, bf16[128,512]{1,0:T(8,128)(2,1)}, bf16[128,512]{1,0:T(8,128)(2,1)}, f32[16,1024]{1,0:T(8,128)}) custom-call(bf16[128,2048]{1,0:T(8,128)(2,1)} %get-tuple-element.12.refs_0_, bf16[128,512]{1,0:T(8,128)(2,1)} %get-tuple-element.13.refs_1_, bf16[128,512]{1,0:T(8,128)(2,1)} %get-tuple-element.14.refs_2_, ...), custom_call_target="tpu_custom_call" | custom-call | tf_op jit(solution)/shard_map/place_outputs/pallas_call | solution.py:694
